TPU v7x, 8 devices: a whole 2x2x1 slice. The times are simulated.
8 devices in a mesh: grp: 1 (over z), pp: 2 (over y), dp: 4 (over x, core).
Axes of the slice: x: 2, y: 2, z: 1, core: 2. Of those that a mesh axis runs over, the one named last changes fastest.
Arguments:
- dy: bfloat16 [2, 2048, 1280], P(('grp', 'pp'), 'dp')
- xs: bfloat16 [2, 2, 2, 2048, 1280], P(('grp', 'pp'), None, None, 'dp')
- hs: bfloat16 [2, 2, 2, 2048, 5120], P(('grp', 'pp'), None, None, 'dp')
- w1: bfloat16 [2, 2, 1280, 5120], P(('grp', 'pp'))
- w2: bfloat16 [2, 2, 5120, 1280], P(('grp', 'pp'))
- acc1: float32 [2, 4, 2, 1280, 5120], P(('grp', 'pp'), 'dp')
- acc2: float32 [2, 4, 2, 5120, 1280], P(('grp', 'pp'), 'dp')
Outputs:
- output 1: float32 [2, 2, 1280, 5120], P(('grp', 'pp'), None, 'dp')
- output 2: float32 [2, 2, 5120, 1280], P(('grp', 'pp'), None, 'dp')
- output 3: bfloat16 [2, 2048, 1280], P(('grp', 'pp'), 'dp')
All inputs are finite; a program needn't handle non-finite values.
Results may differ from a plain program's by a relative error of at most 0.00518973.
Values are sent between devices in bfloat16 or wider.
A program may use at most 1 GiB of HBM per device.

v0:
```python
import jax
import jax.numpy as jnp
from jax import lax
from jax.sharding import PartitionSpec as P


def gelu_fn(v):
    return jax.nn.gelu(v, approximate=True)


def layer_back(g, x, h, wa, wb):
    act, act_vjp = jax.vjp(gelu_fn, h.astype(jnp.float32))
    u = jnp.einsum('td,fd->tf', g, wb, preferred_element_type=jnp.float32)
    dh = act_vjp(u)[0].astype(jnp.bfloat16)
    gx = (g.astype(jnp.float32) + jnp.einsum('tf,df->td', dh, wa, preferred_element_type=jnp.float32)).astype(jnp.bfloat16)
    dwa = jnp.einsum('td,tf->df', x, dh, preferred_element_type=jnp.float32)
    dwb = jnp.einsum('tf,td->fd', act.astype(jnp.bfloat16), g, preferred_element_type=jnp.float32)
    return gx, dwa, dwb


def stage_back(g, xj, hj, wa, wb, ga, gb):
    for k in reversed(range(wa.shape[0])):
        g, dwa, dwb = layer_back(g, xj[k], hj[k], wa[k], wb[k])
        ga = ga.at[k].add(dwa)
        gb = gb.at[k].add(dwb)
    return g, ga, gb


def reduce_avg(acc, ndp):
    nk, rows, cols = acc.shape
    pieces = acc.astype(jnp.bfloat16).reshape(nk, ndp, rows // ndp, cols)
    recv = lax.all_to_all(pieces, 'dp', 1, 1, tiled=True)
    return jnp.sum(recv, axis=1, dtype=jnp.float32) / ndp


def solution(mesh):
    npp = mesh.shape['pp']
    ndp = mesh.shape['dp']

    def body(dy, xs, hs, w1, w2, acc1, acc2):
        s = lax.axis_index('pp')
        g = dy[0]
        ga = acc1[0, 0]
        gb = acc2[0, 0]
        wa = w1[0]
        wb = w2[0]
        r1 = jnp.zeros((ga.shape[0], ga.shape[1] // ndp, ga.shape[2]), jnp.float32)
        r2 = jnp.zeros((gb.shape[0], gb.shape[1] // ndp, gb.shape[2]), jnp.float32)
        outs0 = []
        for t in range(npp):
            j = npp - 1 - s - t
            jc = jnp.maximum(j, 0)
            xj = lax.dynamic_index_in_dim(xs[0], jc, 0, keepdims=False)
            hj = lax.dynamic_index_in_dim(hs[0], jc, 0, keepdims=False)
            g, ga, gb = lax.cond(j >= 0, lambda c: stage_back(c[0], xj, hj, wa, wb, c[1], c[2]), lambda c: c, (g, ga, gb))
            r1, r2 = lax.cond(j == 0, lambda c: (reduce_avg(c[0], ndp), reduce_avg(c[1], ndp)), lambda c: (c[2], c[3]), (ga, gb, r1, r2))
            outs0.append(g)
            if t < npp - 1:
                g = lax.ppermute(g, 'pp', [(r, r - 1) for r in range(1, npp - t)])
        dx_local = jnp.where(s == 0, outs0[npp - 1], jnp.zeros_like(g))
        for jj in range(1, npp):
            dx_local = dx_local + lax.ppermute(outs0[npp - 1 - jj], 'pp', [(0, jj)])
        return r1[None], r2[None], dx_local[None]

    spec_row = P(('grp', 'pp'), 'dp', None)
    spec_saved = P(('grp', 'pp'), None, None, 'dp', None)
    spec_w = P(('grp', 'pp'), None, None, None)
    spec_acc = P(('grp', 'pp'), 'dp', None, None, None)
    spec_g = P(('grp', 'pp'), None, 'dp', None)
    return jax.shard_map(body, mesh=mesh, in_specs=(spec_row, spec_saved, spec_saved, spec_w, spec_w, spec_acc, spec_acc), out_specs=(spec_g, spec_g, spec_row), check_vma=False)
```

profile of v0, /device:TPU:0, one launch (start us, length us, event | category | flops | bytes accessed | tf_op | source)
XLA Modules:
  0.0 1044.8 jit_solution(4032871527216475182)
XLA Ops:
  0.6 35.1 %copy.45 = f32[1,1,2,1280,5120]{4,3,2,1,0:T(8,128)} copy(f32[1,1,2,1280,5120]{4,3,2,1,0:T(8,128)} %param.36) | data formatting | bytes 104857600
  35.8 0.0 copy-start.2
  35.8 34.7 %copy.46 = f32[1,1,2,5120,1280]{4,3,2,1,0:T(8,128)} copy(f32[1,1,2,5120,1280]{4,3,2,1,0:T(8,128)} %param.37) | data formatting | bytes 104857600
  70.5 0.0 copy-done.2
  70.5 1.1 copy.44
  71.5 136.6 %conditional.4 = ((bf16[512,1280]{1,0:T(8,128)(2,1)}, f32[2,1280,5120]{2,1,0:T(8,128)}, f32[2,5120,1280]{2,1,0:T(8,128)})) conditional(s32[]{:T(128)} %convert_element_type.150, (bf16[512,1280]{1,0:T(8,128)(2,1)}, f32[2,1280,5120]{2,1,0:T(8,128)}, f32[2,5120,1280]{2,1,0:T(8,128)}) %tuple.108, (bf16[512,1280]{1,0:T(8,128)(2,1)}, ...), branch_computations={%region_0.1_spmd, %region_1.2_spmd} | conditional | flops 53879767040 | bytes 348651616 | solution.py:55
  71.5 16.2 %fusion.23 = bf16[512,5120]{1,0:T(8,128)(2,1)S(1)} fusion(bf16[1,2,2,512,5120]{4,3,2,1,0:T(8,128)(2,1)} %get-tuple-element.244, s32[]{:T(128)S(6)} %max.8, s32[]{:T(128)S(6)} %add.148, bf16[512,1280]{1,0:T(8,128)(2,1)} %get-tuple-element.242, bf16[2,5120,1280]{2,1,0:T(8,128)(2,1)} %get-tuple-element.243), kind=kOutput, calls=%fused_computation.37 | convolution fusion | flops 6765936640 | bytes 24903688 | tf_op jit(solution)/shard_map/cond/branch_1_fun/td,fd->tf/dot_general | solution.py:13
  87.8 0.0 copy-start
  87.8 12.1 %fusion.59 = bf16[512,1280]{1,0:T(8,128)(2,1)S(1)} fusion(bf16[512,5120]{1,0:T(8,128)(2,1)S(1)} %fusion.23, bf16[2,1280,5120]{2,1,0:T(8,128)(2,1)} %get-tuple-element.246, bf16[512,1280]{1,0:T(8,128)(2,1)} %get-tuple-element.242), kind=kOutput, calls=%fused_computation.63 | convolution fusion | flops 6712852480 | bytes 20971520 | tf_op jit(solution)/shard_map/cond/branch_1_fun/tf,df->td/dot_general | solution.py:15
  99.9 0.0 copy-done
  99.9 18.0 %fusion.20 = bf16[512,5120]{1,0:T(8,128)(2,1)} fusion(bf16[1,2,2,512,5120]{4,3,2,1,0:T(8,128)(2,1)} %get-tuple-element.244, s32[]{:T(128)S(6)} %max.8, bf16[512,1280]{1,0:T(8,128)(2,1)S(1)} %fusion.59, bf16[2,5120,1280]{2,1,0:T(8,128)(2,1)} %get-tuple-element.243), kind=kOutput, calls=%fused_computation.34 | convolution fusion | flops 6765936640 | bytes 24903684 | tf_op jit(solution)/shard_map/cond/branch_1_fun/td,fd->tf/dot_general | solution.py:13
  117.9 18.6 %fusion.3 = f32[2,1280,5120]{2,1,0:T(8,128)} fusion(f32[2,1280,5120]{2,1,0:T(8,128)} %get-tuple-element.247, bf16[512,5120]{1,0:T(8,128)(2,1)} %copy-done, bf16[1,2,2,512,1280]{4,3,2,1,0:T(8,128)(2,1)} %get-tuple-element.248, s32[]{:T(128)S(6)} %max.8, s32[]{:T(128)S(6)} %add.148), kind=kOutput, calls=%fused_computation.7 | convolution fusion | flops 6717440000 | bytes 58982408 | tf_op jit(solution)/shard_map/cond/branch_1_fun/td,tf->df/dot_general | solution.py:16
  136.5 18.9 %fusion.1 = f32[2,1280,5120]{2,1,0:T(8,128)} fusion(f32[2,1280,5120]{2,1,0:T(8,128)} %fusion.3, bf16[512,5120]{1,0:T(8,128)(2,1)} %fusion.20, bf16[1,2,2,512,1280]{4,3,2,1,0:T(8,128)(2,1)} %get-tuple-element.248, s32[]{:T(128)S(6)} %max.8), kind=kOutput, calls=%fused_computation.3 | convolution fusion | flops 6717440000 | bytes 58982404 | tf_op jit(solution)/shard_map/cond/branch_1_fun/td,tf->df/dot_general | solution.py:16
  155.4 19.5 %fusion.2 = f32[2,5120,1280]{2,1,0:T(8,128)} fusion(f32[2,5120,1280]{2,1,0:T(8,128)} %get-tuple-element.249, bf16[512,1280]{1,0:T(8,128)(2,1)} %get-tuple-element.242, bf16[1,2,2,512,5120]{4,3,2,1,0:T(8,128)(2,1)} %get-tuple-element.244, s32[]{:T(128)S(6)} %max.8, s32[]{:T(128)S(6)} %add.148), kind=kOutput, calls=%fused_computation.5 | convolution fusion | flops 6743654400 | bytes 58982408 | tf_op jit(solution)/shard_map/cond/branch_1_fun/tf,td->fd/dot_general | solution.py:17
  175.0 19.2 %fusion = f32[2,5120,1280]{2,1,0:T(8,128)} fusion(f32[2,5120,1280]{2,1,0:T(8,128)} %fusion.2, bf16[512,1280]{1,0:T(8,128)(2,1)S(1)} %fusion.59, bf16[1,2,2,512,5120]{4,3,2,1,0:T(8,128)(2,1)} %get-tuple-element.244, s32[]{:T(128)S(6)} %max.8), kind=kOutput, calls=%fused_computation.1 | convolution fusion | flops 6743654400 | bytes 58982404 | tf_op jit(solution)/shard_map/cond/branch_1_fun/tf,td->fd/dot_general | solution.py:17
  194.2 14.0 %fusion.56 = bf16[512,1280]{1,0:T(8,128)(2,1)} fusion(bf16[512,5120]{1,0:T(8,128)(2,1)} %fusion.20, bf16[2,1280,5120]{2,1,0:T(8,128)(2,1)} %get-tuple-element.246, bf16[512,1280]{1,0:T(8,128)(2,1)S(1)} %fusion.59), kind=kOutput, calls=%fused_computation.62 | convolution fusion | flops 6712852480 | bytes 20971520 | tf_op jit(solution)/shard_map/cond/branch_1_fun/tf,df->td/dot_general | solution.py:15
  208.2 1.3 collective-permute-start
  209.4 6.6 collective-permute-start.1
  216.0 12.5 %conditional.5 = (f32[2,320,5120]{2,1,0:T(8,128)}, f32[2,1280,1280]{2,1,0:T(8,128)}) conditional(s32[]{:T(128)} %convert_element_type.149, () %tuple.81, (f32[2,1280,5120]{2,1,0:T(8,128)}, f32[2,5120,1280]{2,1,0:T(8,128)}) %tuple.84), branch_computations={%region_2.3_spmd, %region_3.6_spmd} | conditional | flops 78643200 | bytes 550502464 | solution.py:56
  216.0 6.6 broadcast_in_dim.16
  222.6 5.8 broadcast_in_dim.17
  228.6 13.1 %collective-permute-done = bf16[512,1280]{1,0:T(8,128)(2,1)S(1)} collective-permute-done((bf16[512,1280]{1,0:T(8,128)(2,1)}, bf16[512,1280]{1,0:T(8,128)(2,1)S(1)}, u32[]{:S(2)}, u32[]{:S(2)}) %collective-permute-start) | collective-permute-done | bytes 1310752 | tf_op jit(solution)/shard_map/ppermute | solution.py:59
  241.7 134.7 %conditional.6 = ((bf16[512,1280]{1,0:T(8,128)(2,1)S(1)}, f32[2,1280,5120]{2,1,0:T(8,128)}, f32[2,5120,1280]{2,1,0:T(8,128)})) conditional(s32[]{:T(128)} %convert_element_type.151, (bf16[512,1280]{1,0:T(8,128)(2,1)S(1)}, f32[2,1280,5120]{2,1,0:T(8,128)}, f32[2,5120,1280]{2,1,0:T(8,128)}) %tuple.85, (bf16[512,1280]{1,0:T(8,128)(2,1)S(1)}, ...), branch_computations={%region_6.7_spmd, %region_7.8_spmd} | conditional | flops 53879767040 | bytes 348651616 | solution.py:55
  241.7 16.0 %fusion.97 = bf16[512,5120]{1,0:T(8,128)(2,1)S(1)} fusion(bf16[1,2,2,512,5120]{4,3,2,1,0:T(8,128)(2,1)} %get-tuple-element.254, s32[]{:T(128)S(6)} %max.9, s32[]{:T(128)S(6)} %add.150, bf16[512,1280]{1,0:T(8,128)(2,1)S(1)} %get-tuple-element.252, bf16[2,5120,1280]{2,1,0:T(8,128)(2,1)} %get-tuple-element.253), kind=kOutput, calls=%fused_computation.119 | convolution fusion | flops 6765936640 | bytes 24903688 | tf_op jit(solution)/shard_map/cond/branch_1_fun/td,fd->tf/dot_general | solution.py:13
  257.7 0.0 copy-start.1
  257.7 11.8 %fusion.133 = bf16[512,1280]{1,0:T(8,128)(2,1)S(1)} fusion(bf16[512,5120]{1,0:T(8,128)(2,1)S(1)} %fusion.97, bf16[2,1280,5120]{2,1,0:T(8,128)(2,1)} %get-tuple-element.256, bf16[512,1280]{1,0:T(8,128)(2,1)S(1)} %get-tuple-element.252), kind=kOutput, calls=%fused_computation.145 | convolution fusion | flops 6712852480 | bytes 20971520 | tf_op jit(solution)/shard_map/cond/branch_1_fun/tf,df->td/dot_general | solution.py:15
  269.5 0.0 copy-done.1
  269.6 17.5 %fusion.94 = bf16[512,5120]{1,0:T(8,128)(2,1)} fusion(bf16[1,2,2,512,5120]{4,3,2,1,0:T(8,128)(2,1)} %get-tuple-element.254, s32[]{:T(128)S(6)} %max.9, bf16[512,1280]{1,0:T(8,128)(2,1)S(1)} %fusion.133, bf16[2,5120,1280]{2,1,0:T(8,128)(2,1)} %get-tuple-element.253), kind=kOutput, calls=%fused_computation.116 | convolution fusion | flops 6765936640 | bytes 24903684 | tf_op jit(solution)/shard_map/cond/branch_1_fun/td,fd->tf/dot_general | solution.py:13
  287.0 18.8 %fusion.77 = f32[2,1280,5120]{2,1,0:T(8,128)} fusion(f32[2,1280,5120]{2,1,0:T(8,128)} %get-tuple-element.257, bf16[512,5120]{1,0:T(8,128)(2,1)} %copy-done.1, bf16[1,2,2,512,1280]{4,3,2,1,0:T(8,128)(2,1)} %get-tuple-element.258, s32[]{:T(128)S(6)} %max.9, s32[]{:T(128)S(6)} %add.150), kind=kOutput, calls=%fused_computation.89 | convolution fusion | flops 6717440000 | bytes 58982408 | tf_op jit(solution)/shard_map/cond/branch_1_fun/td,tf->df/dot_general | solution.py:16
  305.9 18.7 %fusion.75 = f32[2,1280,5120]{2,1,0:T(8,128)} fusion(f32[2,1280,5120]{2,1,0:T(8,128)} %fusion.77, bf16[512,5120]{1,0:T(8,128)(2,1)} %fusion.94, bf16[1,2,2,512,1280]{4,3,2,1,0:T(8,128)(2,1)} %get-tuple-element.258, s32[]{:T(128)S(6)} %max.9), kind=kOutput, calls=%fused_computation.85 | convolution fusion | flops 6717440000 | bytes 58982404 | tf_op jit(solution)/shard_map/cond/branch_1_fun/td,tf->df/dot_general | solution.py:16
  324.6 19.2 %fusion.76 = f32[2,5120,1280]{2,1,0:T(8,128)} fusion(f32[2,5120,1280]{2,1,0:T(8,128)} %get-tuple-element.259, bf16[512,1280]{1,0:T(8,128)(2,1)S(1)} %get-tuple-element.252, bf16[1,2,2,512,5120]{4,3,2,1,0:T(8,128)(2,1)} %get-tuple-element.254, s32[]{:T(128)S(6)} %max.9, s32[]{:T(128)S(6)} %add.150), kind=kOutput, calls=%fused_computation.87 | convolution fusion | flops 6743654400 | bytes 58982408 | tf_op jit(solution)/shard_map/cond/branch_1_fun/tf,td->fd/dot_general | solution.py:17
  343.8 19.6 %fusion.74 = f32[2,5120,1280]{2,1,0:T(8,128)} fusion(f32[2,5120,1280]{2,1,0:T(8,128)} %fusion.76, bf16[512,1280]{1,0:T(8,128)(2,1)S(1)} %fusion.133, bf16[1,2,2,512,5120]{4,3,2,1,0:T(8,128)(2,1)} %get-tuple-element.254, s32[]{:T(128)S(6)} %max.9), kind=kOutput, calls=%fused_computation.83 | convolution fusion | flops 6743654400 | bytes 58982404 | tf_op jit(solution)/shard_map/cond/branch_1_fun/tf,td->fd/dot_general | solution.py:17
  363.5 12.7 %fusion.130 = bf16[512,1280]{1,0:T(8,128)(2,1)S(1)} fusion(bf16[512,5120]{1,0:T(8,128)(2,1)} %fusion.94, bf16[2,1280,5120]{2,1,0:T(8,128)(2,1)} %get-tuple-element.256, bf16[512,1280]{1,0:T(8,128)(2,1)S(1)} %fusion.133), kind=kOutput, calls=%fused_computation.144 | convolution fusion | flops 6712852480 | bytes 20971520 | tf_op jit(solution)/shard_map/cond/branch_1_fun/tf,df->td/dot_general | solution.py:15
  376.4 665.7 %conditional.7 = ((f32[2,320,5120]{2,1,0:T(8,128)}, f32[2,1280,1280]{2,1,0:T(8,128)})) conditional(s32[]{:T(128)} %convert_element_type.148, (f32[2,320,5120]{2,1,0:T(8,128)}, f32[2,1280,1280]{2,1,0:T(8,128)}) %conditional.5, (f32[2,1280,5120]{2,1,0:T(8,128)}, f32[2,5120,1280]{2,1,0:T(8,128)}) %tuple.87), branch_computations={%region_8.9_spmd, %region_9.12_spmd} | conditional | flops 78643200 | bytes 550502464 | solution.py:56
  376.4 26.4 %convert_element_type.142 = bf16[2,5120,1280]{2,1,0:T(8,128)(2,1)} convert(f32[2,5120,1280]{2,1,0:T(8,128)} %get-tuple-element.263) | non-fusion elementwise | flops 13107200 | bytes 78643200 | tf_op jit(solution)/shard_map/cond/branch_1_fun/convert_element_type | solution.py:31
  402.8 21.1 %copy.13 = bf16[2,4,1280,1280]{3,2,0,1:T(8,128)(2,1)} copy(bf16[2,4,1280,1280]{3,2,1,0:T(8,128)(2,1)} %bitcast.151) | data formatting | bytes 52428800 | tf_op jit(solution)/shard_map/cond/branch_1_fun/reshape | solution.py:31
  423.9 8.6 all-to-all-start.3
  432.5 25.6 %convert_element_type.140 = bf16[2,1280,5120]{2,1,0:T(8,128)(2,1)} convert(f32[2,1280,5120]{2,1,0:T(8,128)} %get-tuple-element.262) | non-fusion elementwise | flops 13107200 | bytes 78643200 | tf_op jit(solution)/shard_map/cond/branch_1_fun/convert_element_type | solution.py:31
  458.1 18.1 %copy.12 = bf16[2,4,320,5120]{3,2,0,1:T(8,128)(2,1)} copy(bf16[2,4,320,5120]{3,2,1,0:T(8,128)(2,1)} %bitcast.152) | data formatting | bytes 52428800 | tf_op jit(solution)/shard_map/cond/branch_1_fun/reshape | solution.py:31
  476.2 240.1 %all-to-all-done.3 = bf16[2,4,1280,1280]{3,2,0,1:T(8,128)(2,1)} async-done(((bf16[2,4,1280,1280]{3,2,0,1:T(8,128)(2,1)}), bf16[2,4,1280,1280]{3,2,0,1:T(8,128)(2,1)}, u32[]{:S(2)}, u32[]{:S(2)}) %all-to-all-start.3) | async-done | bytes 26214432 | tf_op jit(solution)/shard_map/cond/branch_1_fun/all_to_all | solution.py:32
  716.3 8.6 all-to-all-start.2
  724.9 20.9 %convert_reduce_fusion.2 = f32[2,1280,1280]{2,1,0:T(8,128)} fusion(bf16[2,4,1280,1280]{3,2,0,1:T(8,128)(2,1)} %all-to-all-done.3), kind=kLoop, calls=%fused_computation.160 | loop fusion | flops 22937600 | bytes 39321600 | tf_op jit(solution)/shard_map/cond/branch_1_fun/reduce_sum | solution.py:33
  745.8 10.5 %broadcast_multiply_fusion.2 = f32[2,1280,1280]{2,1,0:T(8,128)} fusion(f32[2,1280,1280]{2,1,0:T(8,128)} %convert_reduce_fusion.2), kind=kLoop, calls=%fused_computation.162 | loop fusion | flops 3276800 | bytes 26214400 | tf_op jit(solution)/shard_map/cond/branch_1_fun/div | solution.py:33
  756.3 252.4 %all-to-all-done.2 = bf16[2,4,320,5120]{3,2,0,1:T(8,128)(2,1)} async-done(((bf16[2,4,320,5120]{3,2,0,1:T(8,128)(2,1)}), bf16[2,4,320,5120]{3,2,0,1:T(8,128)(2,1)}, u32[]{:S(2)}, u32[]{:S(2)}) %all-to-all-start.2) | async-done | bytes 26214432 | tf_op jit(solution)/shard_map/cond/branch_1_fun/all_to_all | solution.py:32
  1008.8 21.5 %convert_reduce_fusion.3 = f32[2,320,5120]{2,1,0:T(8,128)} fusion(bf16[2,4,320,5120]{3,2,0,1:T(8,128)(2,1)} %all-to-all-done.2), kind=kLoop, calls=%fused_computation.161 | loop fusion | flops 22937600 | bytes 39321600 | tf_op jit(solution)/shard_map/cond/branch_1_fun/reduce_sum | solution.py:33
  1030.3 11.8 %broadcast_multiply_fusion.3 = f32[2,320,5120]{2,1,0:T(8,128)} fusion(f32[2,320,5120]{2,1,0:T(8,128)} %convert_reduce_fusion.3), kind=kLoop, calls=%fused_computation.163 | loop fusion | flops 3276800 | bytes 26214400 | tf_op jit(solution)/shard_map/cond/branch_1_fun/div | solution.py:33
  1042.0 0.0 collective-permute-done.1
  1042.0 2.5 add_bitcast_fusion
Async XLA Ops:
  35.8 34.7 %copy-start.2 = (bf16[1,512,1280]{2,1,0:T(8,128)(2,1)S(1)}, bf16[1,512,1280]{2,1,0:T(8,128)(2,1)}, u32[]{:S(2)}) copy-start(bf16[1,512,1280]{2,1,0:T(8,128)(2,1)} %param.31) | copy-start | bytes 3932164
  87.8 12.1 %copy-start = (bf16[512,5120]{1,0:T(8,128)(2,1)}, bf16[512,5120]{1,0:T(8,128)(2,1)S(1)}, u32[]{:S(2)}) copy-start(bf16[512,5120]{1,0:T(8,128)(2,1)S(1)} %fusion.23) | copy-start | bytes 15728644 | tf_op jit(solution)/shard_map/cond
  208.2 33.5 %collective-permute-start = (bf16[512,1280]{1,0:T(8,128)(2,1)}, bf16[512,1280]{1,0:T(8,128)(2,1)S(1)}, u32[]{:S(2)}, u32[]{:S(2)}) collective-permute-start(bf16[512,1280]{1,0:T(8,128)(2,1)} %get-tuple-element.277), channel_id=1, source_target_pairs={{4,0},{5,1},{6,2},{7,3}} | collective-permute-start | bytes 3932168 | tf_op jit(solution)/shard_map/ppermute | solution.py:59
  209.4 832.6 %collective-permute-start.1 = (bf16[512,1280]{1,0:T(8,128)(2,1)}, bf16[512,1280]{1,0:T(8,128)(2,1)}, u32[]{:S(2)}, u32[]{:S(2)}) collective-permute-start(bf16[512,1280]{1,0:T(8,128)(2,1)} %get-tuple-element.277), channel_id=1, source_target_pairs={{0,4},{1,5},{2,6},{3,7}} | collective-permute-start | bytes 3932168 | tf_op jit(solution)/shard_map/ppermute | solution.py:62
  257.7 11.9 %copy-start.1 = (bf16[512,5120]{1,0:T(8,128)(2,1)}, bf16[512,5120]{1,0:T(8,128)(2,1)S(1)}, u32[]{:S(2)}) copy-start(bf16[512,5120]{1,0:T(8,128)(2,1)S(1)} %fusion.97) | copy-start | bytes 15728644 | tf_op jit(solution)/shard_map/cond
  423.9 292.4 %all-to-all-start.3 = ((bf16[2,4,1280,1280]{3,2,0,1:T(8,128)(2,1)}), bf16[2,4,1280,1280]{3,2,0,1:T(8,128)(2,1)}, u32[]{:S(2)}, u32[]{:S(2)}) async-start(bf16[2,4,1280,1280]{3,2,0,1:T(8,128)(2,1)} %copy.13), calls=%async_computation.3 | async-start | bytes 52428800 | tf_op jit(solution)/shard_map/cond/branch_1_fun/all_to_all | solution.py:32
  716.3 292.4 %all-to-all-start.2 = ((bf16[2,4,320,5120]{3,2,0,1:T(8,128)(2,1)}), bf16[2,4,320,5120]{3,2,0,1:T(8,128)(2,1)}, u32[]{:S(2)}, u32[]{:S(2)}) async-start(bf16[2,4,320,5120]{3,2,0,1:T(8,128)(2,1)} %copy.12), calls=%async_computation.2 | async-start | bytes 52428800 | tf_op jit(solution)/shard_map/cond/branch_1_fun/all_to_all | solution.py:32
where the time goes:
time: 1050 us; the launch traced here: 1040 us
  waiting for transfers between devices  506 us (48%)
  matrix products  271 us (26%)
  local copies, waits for them, and re-layouts  122 us (12%)
  other arithmetic  119 us (11%)
  starting transfers between devices  25 us (2%)
    all_to_all x2, waiting for transfers between devices, reduce_avg(): recv = lax.all_to_all(pieces, 'dp', 1, 1, tiled=True)  493 us
    dot_general x4, matrix products, layer_back(): jnp.einsum('tf,td->fd', act.astype(jnp.bfloat16), g, preferred_element_ty...  77.6 us
    dot_general x4, matrix products, layer_back(): dwa = jnp.einsum('td,tf->df', x, dh, preferred_element_type=jnp.float32)  75.1 us
    unnamed x5, local copies, waits for them, and re-layouts  70.9 us
    dot_general x4, matrix products, layer_back(): u = jnp.einsum('td,fd->tf', g, wb, preferred_element_type=jnp.float32)  67.7 us
    convert_element_type x2, other arithmetic, reduce_avg(): pieces = acc.astype(jnp.bfloat16).reshape(nk, ndp, rows // ndp, cols)  52.1 us
    dot_general x4, matrix products, layer_back(): jnp.einsum('tf,df->td', dh, wa, preferred_element_type=jnp.float32)  50.6 us
    reduce_sum x2, other arithmetic, reduce_avg(): return jnp.sum(recv, axis=1, dtype=jnp.float32) / ndp  42.4 us
  transfers between devices with their start and end apart: 4, of which 3 were waited for; matrix products, arithmetic and copies ran while one was open for 29% of the time, Pallas kernels for 0%

commit v1 on v0

v1 whole, which is shorter than its diff:
```python
import jax
import jax.numpy as jnp
from jax import lax
from jax.experimental import pallas as pl
from jax.sharding import PartitionSpec as P


def gelu_fn(v):
    return jax.nn.gelu(v, approximate=True)


def act_of(h):
    return gelu_fn(h.astype(jnp.float32)).astype(jnp.bfloat16)


def reduce_into(buf, parts, k, shape, scale, br, first, count):
    cols = shape[2]
    n = len(parts)
    steps = count // br

    def kern(*refs):
        total = refs[0][...].astype(jnp.float32)
        for r in refs[1:n]:
            total = total + r[...].astype(jnp.float32)
        refs[-1][0] = total * scale

    def block(off):
        return pl.BlockSpec((br, cols), lambda i: (off // br + i, 0))

    in_specs = [block(off) for _, off in parts]
    args = [p for p, _ in parts]
    aliases = {}
    if buf is not None:
        in_specs.append(pl.BlockSpec(memory_space=pl.ANY))
        args.append(buf)
        aliases = {n: 0}
    return pl.pallas_call(
        kern, grid=(steps,), in_specs=in_specs,
        out_specs=pl.BlockSpec((1, br, cols), lambda i: (k, first // br + i, 0)),
        out_shape=jax.ShapeDtypeStruct(shape, jnp.float32),
        input_output_aliases=aliases,
        cost_estimate=pl.CostEstimate(flops=count * cols * n, bytes_accessed=count * cols * (2 * n + 4), transcendentals=0),
    )(*args)


def solution(mesh):
    npp = mesh.shape['pp']
    ndp = mesh.shape['dp']
    assert npp == 2 and ndp == 4
    both = ('pp', 'dp')

    def hop(p, routes, off):
        return lax.ppermute(p, both, [(a * ndp + i, b * ndp + (i ^ off)) for a, b in routes for i in range(ndp)])

    def body(dy, xs, hs, w1, w2, acc1, acc2):
        s = lax.axis_index('pp')
        d = lax.axis_index('dp')
        nk = w1.shape[1]
        acc1, acc2, w1, w2, xs, hs = acc1[0, 0], acc2[0, 0], w1[0], w2[0], xs[0], hs[0]
        n1, n2 = acc1.shape[1] // ndp, acc2.shape[1] // ndp
        nc = n2 // 4
        nd = 3 * n2 // 10
        slot = (npp - 1 - s, jnp.int32(0))
        tok = [jnp.int32(0)]

        def after(*v):
            tok[0] = lax.optimization_barrier((tok[0], *v))[0]

        def saved(arr, i, k, at=0, count=None):
            count = count or arr.shape[3]
            return lax.dynamic_slice(arr, (slot[i] + tok[0], k, 0, at), (1, 1, arr.shape[2], count))[0, 0]

        def add(acc, k, at, lhs, rhs):
            part = lax.dynamic_slice(acc, (k, at, 0), (1, lhs.shape[1], acc.shape[2]))[0]
            return (part + jnp.einsum('tr,tc->rc', lhs, rhs, preferred_element_type=jnp.float32)).astype(jnp.bfloat16)

        def early(off, first, count):
            at = (d ^ off) * n2 + first + tok[0]
            p = add(acc2, 1, at, act_of(saved(hs, 0, 1, at, count)), dy[0])
            after(p)
            return p

        def both2(k, off, first=0, count=None):
            at = (d ^ off) * n2 + first + tok[0]
            lhs = jnp.concatenate([lax.dynamic_slice_in_dim(v, at, count or n2, 1) for v in act[k]], 0)
            p = add(acc2, k, at, lhs, jnp.concatenate([ga[k], gb[k]], 0))
            after(p)
            return p

        def both1(k, off):
            at = (d ^ off) * n1 + tok[0]
            lhs = jnp.concatenate([saved(xs, i, k, at, n1) for i in range(2)], 0)
            p = add(acc1, k, at, lhs, jnp.concatenate([da[k], db[k]], 0))
            after(p)
            return p

        def up(g, i, k):
            _, act_vjp = jax.vjp(gelu_fn, saved(hs, i, k).astype(jnp.float32))
            u = jnp.einsum('td,fd->tf', g, w2[k], preferred_element_type=jnp.float32)
            v = act_vjp(u)[0].astype(jnp.bfloat16)
            after(v)
            return v

        def out(g, dh, k):
            v = (g.astype(jnp.float32) + jnp.einsum('tf,df->td', dh, w1[k], preferred_element_type=jnp.float32)).astype(jnp.bfloat16)
            after(v)
            return v

        def acts(k):
            act[k] = lax.optimization_barrier([act_of(saved(hs, i, k)) for i in range(2)])
            after(act[k][0])

        ga, gb, da, db, act = {1: dy[0]}, {}, {}, {}, {}
        stay, down, rise = [(0, 0), (1, 1)], [(1, 0)], [(0, 1)]
        near, own = {}, {}

        c0 = early(3, 0, nc)
        e2 = early(2, 0, n2)
        c1 = early(3, nc, n2 - nc)
        far12 = [(hop(e2, [(1, 1)], 2), 0)]
        lane = [hop(hop(p, down, 0), rise, 3) for p in (c0, c1)]
        da[1] = up(ga[1], 0, 1)
        far11 = []

        def early1(off):
            at = (d ^ off) * n1 + tok[0]
            p = add(acc1, 1, at, saved(xs, 0, 1, at, n1), da[1])
            after(p)
            far11.append((hop(p, [(1, 1)], off), 0))

        early1(2)
        dh, _ = lax.optimization_barrier((da[1], tok[0]))
        ga[0] = out(ga[1], dh, 1)
        da[0] = up(ga[0], 0, 0)
        gout = out(ga[0], da[0], 0)
        recv = lax.ppermute(gout, 'pp', [(1, 0)])
        acts(1)
        early1(3)

        recv, _ = lax.optimization_barrier((recv, tok[0]))
        gb[1] = recv
        far12.append((hop(both2(1, 2), [(0, 0)], 2), 0))
        t = hop(hop(both2(1, 3, 0, nd), rise, 0), down, 3)
        u = hop(both2(1, 3, nd, n2 - nd), [(0, 0)], 3)
        db[1] = up(gb[1], 1, 1)
        gb[0] = out(gb[1], db[1], 1)
        gave = lax.ppermute(lax.optimization_barrier((gout, tok[0]))[0], 'pp', [(0, 1)])
        acts(0)
        far02 = [(hop(both2(0, off), stay, off), 0) for off in (2, 3)]
        far11.append((hop(both1(1, 2), [(0, 0)], 2), 0))
        far11.append((hop(hop(both1(1, 3), rise, 0), down, 3), 0))
        near[1, 2] = hop(both2(1, 1), stay, 1)
        near[1, 1] = hop(both1(1, 1), stay, 1)
        own[1, 2] = both2(1, 0)
        own[1, 1] = both1(1, 0)
        db[0] = up(gb[0], 1, 0)
        near[0, 2] = hop(both2(0, 1), stay, 1)
        own[0, 2] = both2(0, 0)
        p012 = both1(0, 2)
        p013 = both1(0, 3)
        cut = 3 * n1 // 4
        far012 = hop(p012, stay, 2)
        p013a, p013b = lax.optimization_barrier((p013[:cut], p013[cut:]))
        far013a = hop(p013a, stay, 3)
        far013b = hop(p013b, stay, 3)
        dh, _ = lax.optimization_barrier((db[0], tok[0]))
        g = out(gb[0], dh, 0)
        near[0, 1] = hop(both1(0, 1), stay, 1)
        own[0, 1] = both1(0, 0)
        dx = jnp.where(s == 0, g, gave)
        lane, _ = lax.optimization_barrier((lane, tok[0]))
        far12.append((jnp.concatenate(lane, 0), 0))
        far12.append((jnp.concatenate([t, u], 0), 0))
        sc = 1.0 / ndp
        sh1, sh2 = (nk, n1, acc1.shape[2]), (nk, n2, acc2.shape[2])

        def base(k, w, off=0):
            return [(own[k, w], off), (near[k, w], off)]

        o2 = reduce_into(None, base(1, 2) + far12, 1, sh2, sc, n2 // 5, 0, n2)
        o1 = reduce_into(None, base(1, 1) + far11, 1, sh1, sc, n1 // 5, 0, n1)
        o2 = reduce_into(o2, base(0, 2) + far02, 0, sh2, sc, n2 // 5, 0, n2)
        o1 = reduce_into(o1, base(0, 1) + [(far012, 0), (far013a, 0)], 0, sh1, sc, cut // 5, 0, cut)
        br = (n1 - cut) // 5
        o1 = reduce_into(o1, base(0, 1, cut) + [(far012, cut), (far013b, 0)], 0, sh1, sc, br, cut, n1 - cut)
        return o1[None], o2[None], dx[None]

    spec_row = P(('grp', 'pp'), 'dp', None)
    spec_saved = P(('grp', 'pp'), None, None, 'dp', None)
    spec_w = P(('grp', 'pp'), None, None, None)
    spec_acc = P(('grp', 'pp'), 'dp', None, None, None)
    spec_g = P(('grp', 'pp'), None, 'dp', None)
    return jax.shard_map(body, mesh=mesh, in_specs=(spec_row, spec_saved, spec_saved, spec_w, spec_w, spec_acc, spec_acc), out_specs=(spec_g, spec_g, spec_row), check_vma=False)
```

time: 1050 us -> 860 us (0.82)
  waiting for transfers between devices: 506 us -> 375 us
  other arithmetic: 119 us -> 32.7 us
  local copies, waits for them, and re-layouts: 122 us -> 57.9 us
  Pallas kernels: 0 us -> 43.8 us
  starting transfers between devices: 25 us -> 56.2 us
  matrix products: 271 us -> 287 us
    all_to_all x2 -> x0, waiting for transfers between devices: 493 us -> none  [reduce_avg(): recv = lax.all_to_all(pieces, 'dp', 1, 1, tiled=True)]
    ppermute x2 -> x25, waiting for transfers between devices: 13.1 us -> 375 us  [the longest x23 367 us: hop(): lax.ppermute(p, both, [(a * ndp + i, b * ndp + (i ^ off)) for a, b in rou...]
    unnamed x5 -> x36, local copies, waits for them, and re-layouts: 70.9 us -> 5.14 us
    ppermute x2 -> x25, starting transfers between devices: 7.88 us -> 56.2 us  [the longest x23 52.3 us: hop(): lax.ppermute(p, both, [(a * ndp + i, b * ndp + (i ^ off)) for a, b in rou...]
    pallas_call x0 -> x5, Pallas kernels: none -> 43.8 us  [reduce_into(): pl.pallas_call(kern, grid=(steps,), in_specs=in_specs, out_specs=pl.Block...]
    reduce_sum x2 -> x0, other arithmetic: 42.4 us -> none  [reduce_avg(): return jnp.sum(recv, axis=1, dtype=jnp.float32) / ndp]
    reshape x2 -> x0, local copies, waits for them, and re-layouts: 39.2 us -> none  [reduce_avg(): pieces = acc.astype(jnp.bfloat16).reshape(nk, ndp, rows // ndp, cols)]
    dynamic_slice x0 -> x17, local copies, waits for them, and re-layouts: none -> 35.1 us  [both2(): lax.dynamic_slice_in_dim(v, at, count or n2, 1)]
  transfers between devices with their start and end apart: 4 -> 25, of which waited for: 3 -> 10; matrix products, arithmetic and copies ran while one was open for 29% -> 43% of each run, Pallas kernels for 0% -> 5%
where the time goes in v1:
time: 860 us; the launch traced here: 853 us
  waiting for transfers between devices  375 us (44%)
  matrix products  287 us (33%)
  local copies, waits for them, and re-layouts  57.9 us (7%)
  starting transfers between devices  56.2 us (7%)
  Pallas kernels  43.8 us (5%)
  other arithmetic  32.7 us (4%)
    ppermute x23, waiting for transfers between devices, hop(): lax.ppermute(p, both, [(a * ndp + i, b * ndp + (i ^ off)) for a, b in rou...  367 us
    dot_general x22, matrix products, add(): jnp.einsum('tr,tc->rc', lhs, rhs, preferred_element_type=jnp.float32)  172 us
    dot_general x4, matrix products, up(): u = jnp.einsum('td,fd->tf', g, w2[k], preferred_element_type=jnp.float32)  67.7 us
    ppermute x23, starting transfers between devices, hop(): lax.ppermute(p, both, [(a * ndp + i, b * ndp + (i ^ off)) for a, b in rou...  52.3 us
    dot_general x4, matrix products, out(): jnp.einsum('tf,df->td', dh, w1[k], preferred_element_type=jnp.float32)  46.9 us
    pallas_call x5, Pallas kernels, reduce_into(): pl.pallas_call(kern, grid=(steps,), in_specs=in_specs, out_specs=pl.Block...  43.8 us
    dynamic_slice x17, local copies, waits for them, and re-layouts, both2(): lax.dynamic_slice_in_dim(v, at, count or n2, 1)  35.1 us
    convert_element_type x2, other arithmetic, act_of(): return gelu_fn(h.astype(jnp.float32)).astype(jnp.bfloat16)  23.8 us
  transfers between devices with their start and end apart: 25, of which 10 were waited for; matrix products, arithmetic and copies ran while one was open for 43% of the time, Pallas kernels for 5%

profile of v1, /device:TPU:0, one launch (start us, length us, event | category | flops | bytes accessed | tf_op | source)
XLA Modules:
  0.0 853.5 jit_solution(13246268807904135086)
XLA Ops:
  0.6 3.8 fusion.131
  5.7 8.1 fusion.91
  13.9 2.3 collective-permute-start.15
  16.2 6.3 fusion.102
  23.9 17.5 %fusion.39 = bf16[512,5120]{1,0:T(8,128)(2,1)} fusion(bf16[1,2,2,512,5120]{4,3,2,1,0:T(8,128)(2,1)} %param.9, s32[]{:T(128)S(6)} %select_n.206, bf16[1,2,5120,1280]{3,2,1,0:T(8,128)(2,1)} %param.11, bf16[1,512,1280]{2,1,0:T(8,128)(2,1)S(1)} %copy-done.5), kind=kOutput, calls=%fused_computation.71 | convolution fusion | flops 6765936640 | bytes 24903684 | tf_op jit(solution)/shard_map/td,fd->tf/dot_general | solution.py:99
  41.4 8.7 %fusion.92 = bf16[320,5120]{1,0:T(8,128)(2,1)} fusion(bf16[512,5120]{1,0:T(8,128)(2,1)} %fusion.39, f32[1,1,2,1280,5120]{4,3,2,1,0:T(8,128)} %param.12, s32[]{:T(128)S(6)} %select_n.207, bf16[1,2,2,512,1280]{4,3,2,1,0:T(8,128)(2,1)} %param.8, s32[]{:T(128)S(6)} %select_n.208), kind=kOutput, calls=%fused_computation.144 | convolution fusion | flops 1680998400 | bytes 15468032 | tf_op jit(solution)/shard_map/tr,tc->rc/dot_general | solution.py:75
  50.1 2.6 collective-permute-start.6
  52.8 9.9 %fusion.127 = bf16[512,1280]{1,0:T(8,128)(2,1)S(1)} fusion(bf16[512,5120]{1,0:T(8,128)(2,1)S(1)} %copy-done, bf16[1,2,1280,5120]{3,2,1,0:T(8,128)(2,1)} %param.10, bf16[1,512,1280]{2,1,0:T(8,128)(2,1)S(1)} %copy-done.5), kind=kOutput, calls=%fused_computation.174 | convolution fusion | flops 6712852480 | bytes 20971520 | tf_op jit(solution)/shard_map/tf,df->td/dot_general | solution.py:105
  63.8 16.0 %fusion.36 = bf16[512,5120]{1,0:T(8,128)(2,1)S(1)} fusion(bf16[1,2,2,512,5120]{4,3,2,1,0:T(8,128)(2,1)} %param.9, s32[]{:T(128)S(6)} %select_n.209, bf16[512,1280]{1,0:T(8,128)(2,1)S(1)} %fusion.127, bf16[1,2,5120,1280]{3,2,1,0:T(8,128)(2,1)} %param.11), kind=kOutput, calls=%fused_computation.68 | convolution fusion | flops 6765936640 | bytes 24903684 | tf_op jit(solution)/shard_map/td,fd->tf/dot_general | solution.py:99
  79.8 12.1 %fusion.124 = bf16[512,1280]{1,0:T(8,128)(2,1)S(1)} fusion(bf16[512,5120]{1,0:T(8,128)(2,1)S(1)} %fusion.36, bf16[1,2,1280,5120]{3,2,1,0:T(8,128)(2,1)} %param.10, bf16[512,1280]{1,0:T(8,128)(2,1)} %copy-done.9), kind=kOutput, calls=%fused_computation.173 | convolution fusion | flops 6712852480 | bytes 20971520 | tf_op jit(solution)/shard_map/tf,df->td/dot_general | solution.py:105
  93.5 12.0 %fusion.61 = (bf16[512,5120]{1,0:T(8,128)(2,1)}, bf16[512,5120]{1,0:T(8,128)(2,1)}) fusion(bf16[1,2,2,512,5120]{4,3,2,1,0:T(8,128)(2,1)} %param.9, s32[]{:T(128)S(6)} %select_n.211, s32[]{:T(128)S(6)} %select_n.210), kind=kLoop, calls=%fused_computation.93 | loop fusion | flops 52428800 | bytes 20971528 | tf_op jit(solution)/shard_map/convert_element_type | solution.py:13
  105.5 8.5 fusion.93
  118.3 12.7 %collective-permute-start.18 = (bf16[320,1280]{1,0:T(8,128)(2,1)}, bf16[320,1280]{1,0:T(8,128)(2,1)}, u32[]{:S(2)}, u32[]{:S(2)}) collective-permute-start(bf16[320,1280]{1,0:T(8,128)(2,1)} %collective-permute-done.17), channel_id=1, source_target_pairs={{0,7},{1,6},{2,5},{3,4}} | collective-permute-start | bytes 2457608 | tf_op jit(solution)/shard_map/ppermute | solution.py:53
  131.0 7.5 fusion.84
  141.0 4.1 fusion.130
  148.7 6.8 fusion.103
  155.5 2.4 collective-permute-start.21
  157.9 16.3 %fusion.33 = bf16[512,5120]{1,0:T(8,128)(2,1)S(1)} fusion(bf16[1,2,2,512,5120]{4,3,2,1,0:T(8,128)(2,1)} %param.9, s32[]{:T(128)S(6)} %select_n.217, bf16[512,1280]{1,0:T(8,128)(2,1)} %collective-permute-done, bf16[1,2,5120,1280]{3,2,1,0:T(8,128)(2,1)} %param.11), kind=kOutput, calls=%fused_computation.65 | convolution fusion | flops 6765936640 | bytes 24903684 | tf_op jit(solution)/shard_map/td,fd->tf/dot_general | solution.py:99
  174.2 2.3 copy-done.8
  176.5 11.3 %add_convert_fusion = bf16[512,1280]{1,0:T(8,128)(2,1)} fusion(bf16[512,1280]{1,0:T(8,128)(2,1)} %collective-permute-done, bf16[512,5120]{1,0:T(8,128)(2,1)S(1)} %fusion.33, bf16[1,2,1280,5120]{3,2,1,0:T(8,128)(2,1)} %param.10), kind=kOutput, calls=%fused_computation.207 | convolution fusion | flops 6712852480 | bytes 20971520 | tf_op jit(solution)/shard_map/tf,df->td/dot_general | solution.py:105
  187.8 11.9 %fusion.78 = (bf16[512,5120]{1,0:T(8,128)(2,1)}, bf16[512,5120]{1,0:T(8,128)(2,1)}) fusion(bf16[1,2,2,512,5120]{4,3,2,1,0:T(8,128)(2,1)} %param.9, s32[]{:T(128)S(6)} %select_n.219, s32[]{:T(128)S(6)} %select_n.218), kind=kLoop, calls=%fused_computation.110 | loop fusion | flops 52428800 | bytes 20971528 | tf_op jit(solution)/shard_map/convert_element_type | solution.py:13
  199.7 2.3 constant_dynamic-slice_fusion.11
  204.2 7.3 fusion.85
  215.7 7.1 fusion.86
  224.3 9.2 %fusion.94 = bf16[320,5120]{1,0:T(8,128)(2,1)} fusion(f32[1,1,2,1280,5120]{4,3,2,1,0:T(8,128)} %param.12, s32[]{:T(128)S(6)} %select_n.222, bf16[512,320]{1,0:T(8,128)(2,1)S(1)} %get-tuple-element.108, bf16[512,320]{1,0:T(8,128)(2,1)S(1)} %get-tuple-element.107, bf16[512,5120]{1,0:T(8,128)(2,1)} %copy-done.8, bf16[512,5120]{1,0:T(8,128)(2,1)} %fusion.39), kind=kOutput, calls=%fused_computation.146 | convolution fusion | flops 3381002240 | bytes 20971524 | tf_op jit(solution)/shard_map/tr,tc->rc/dot_general | solution.py:75
  235.0 9.1 %fusion.95 = bf16[320,5120]{1,0:T(8,128)(2,1)} fusion(f32[1,1,2,1280,5120]{4,3,2,1,0:T(8,128)} %param.12, s32[]{:T(128)S(6)} %select_n.225, bf16[512,320]{1,0:T(8,128)(2,1)S(1)} %get-tuple-element.106, bf16[512,320]{1,0:T(8,128)(2,1)S(1)} %get-tuple-element.105, bf16[512,5120]{1,0:T(8,128)(2,1)} %copy-done.8, bf16[512,5120]{1,0:T(8,128)(2,1)} %fusion.39), kind=kOutput, calls=%fused_computation.147 | convolution fusion | flops 3381002240 | bytes 20971524 | tf_op jit(solution)/shard_map/tr,tc->rc/dot_general | solution.py:75
  248.4 7.9 fusion.87
  257.8 9.2 %fusion.96 = bf16[320,5120]{1,0:T(8,128)(2,1)} fusion(f32[1,1,2,1280,5120]{4,3,2,1,0:T(8,128)} %param.12, s32[]{:T(128)S(6)} %select_n.229, bf16[512,320]{1,0:T(8,128)(2,1)S(1)} %get-tuple-element.104, bf16[512,320]{1,0:T(8,128)(2,1)S(1)} %get-tuple-element.103, bf16[512,5120]{1,0:T(8,128)(2,1)} %copy-done.8, bf16[512,5120]{1,0:T(8,128)(2,1)} %fusion.39), kind=kOutput, calls=%fused_computation.148 | convolution fusion | flops 3381002240 | bytes 20971524 | tf_op jit(solution)/shard_map/tr,tc->rc/dot_general | solution.py:75
  267.0 3.1 constant_dynamic-slice_fusion.4
  270.0 7.5 fusion.88.refs_0_
  279.0 9.4 %fusion.97.refs_0_ = bf16[320,5120]{1,0:T(8,128)(2,1)} fusion(f32[1,1,2,1280,5120]{4,3,2,1,0:T(8,128)} %param.12, s32[]{:T(128)S(6)} %select_n.233, bf16[512,320]{1,0:T(8,128)(2,1)S(1)} %get-tuple-element.102, bf16[512,320]{1,0:T(8,128)(2,1)S(1)} %get-tuple-element.101, bf16[512,5120]{1,0:T(8,128)(2,1)} %copy-done.8, bf16[512,5120]{1,0:T(8,128)(2,1)} %fusion.39), kind=kOutput, calls=%fused_computation.149 | convolution fusion | flops 3381002240 | bytes 20971524 | tf_op jit(solution)/shard_map/tr,tc->rc/dot_general | solution.py:75
  288.5 2.3 collective-permute-start.7
  290.8 2.4 collective-permute-start.24
  294.5 17.9 %fusion.30 = bf16[512,5120]{1,0:T(8,128)(2,1)} fusion(bf16[1,2,2,512,5120]{4,3,2,1,0:T(8,128)(2,1)} %param.9, s32[]{:T(128)S(6)} %select_n.236, bf16[512,1280]{1,0:T(8,128)(2,1)} %add_convert_fusion, bf16[1,2,5120,1280]{3,2,1,0:T(8,128)(2,1)} %param.11), kind=kOutput, calls=%fused_computation.62 | convolution fusion | flops 6765936640 | bytes 24903684 | tf_op jit(solution)/shard_map/td,fd->tf/dot_general | solution.py:99
  312.4 8.2 collective-permute-done.24
  320.6 3.3 collective-permute-start.23
  323.9 3.2 collective-permute-start.16
  331.5 50.9 %collective-permute-done.22 = bf16[384,1280]{1,0:T(8,128)(2,1)} collective-permute-done((bf16[384,1280]{1,0:T(8,128)(2,1)}, bf16[384,1280]{1,0:T(8,128)(2,1)}, u32[]{:S(2)}, u32[]{:S(2)}) %collective-permute-start.22) | collective-permute-done | bytes 983072 | tf_op jit(solution)/shard_map/ppermute | solution.py:53
  382.9 7.2 fusion.89
  394.6 7.1 fusion.90.refs_0_
  403.2 3.3 collective-permute-start.9
  406.5 3.1 collective-permute-start.8
  409.7 9.4 %fusion.98 = bf16[320,5120]{1,0:T(8,128)(2,1)} fusion(f32[1,1,2,1280,5120]{4,3,2,1,0:T(8,128)} %param.12, s32[]{:T(128)S(6)} %select_n.239, bf16[512,320]{1,0:T(8,128)(2,1)S(1)} %get-tuple-element.100, bf16[512,320]{1,0:T(8,128)(2,1)S(1)} %get-tuple-element.99, bf16[512,5120]{1,0:T(8,128)(2,1)} %fusion.30, bf16[512,5120]{1,0:T(8,128)(2,1)} %copy-done.7), kind=kOutput, calls=%fused_computation.150 | convolution fusion | flops 3381002240 | bytes 20971524 | tf_op jit(solution)/shard_map/tr,tc->rc/dot_general | solution.py:75
  420.5 25.9 %collective-permute-done.16.refs_3_ = bf16[1280,1280]{1,0:T(8,128)(2,1)} collective-permute-done((bf16[1280,1280]{1,0:T(8,128)(2,1)}, bf16[1280,1280]{1,0:T(8,128)(2,1)}, u32[]{:S(2)}, u32[]{:S(2)}) %collective-permute-start.16) | collective-permute-done | bytes 3276832 | tf_op jit(solution)/shard_map/ppermute | solution.py:53
  447.1 9.2 %fusion.99 = bf16[320,5120]{1,0:T(8,128)(2,1)} fusion(f32[1,1,2,1280,5120]{4,3,2,1,0:T(8,128)} %param.12, s32[]{:T(128)S(6)} %select_n.242, bf16[512,320]{1,0:T(8,128)(2,1)S(1)} %get-tuple-element.98, bf16[512,320]{1,0:T(8,128)(2,1)S(1)} %get-tuple-element.97, bf16[512,5120]{1,0:T(8,128)(2,1)} %fusion.30, bf16[512,5120]{1,0:T(8,128)(2,1)} %copy-done.7), kind=kOutput, calls=%fused_computation.151 | convolution fusion | flops 3381002240 | bytes 20971524 | tf_op jit(solution)/shard_map/tr,tc->rc/dot_general | solution.py:75
  457.5 13.6 %fusion.121 = bf16[512,1280]{1,0:T(8,128)(2,1)} fusion(bf16[512,5120]{1,0:T(8,128)(2,1)} %fusion.30, bf16[1,2,1280,5120]{3,2,1,0:T(8,128)(2,1)} %param.10, bf16[512,1280]{1,0:T(8,128)(2,1)S(1)} %copy-done.17), kind=kOutput, calls=%fused_computation.172 | convolution fusion | flops 6712852480 | bytes 20971520 | tf_op jit(solution)/shard_map/tf,df->td/dot_general | solution.py:105
  472.6 2.8 collective-permute-done.9
  475.4 6.5 collective-permute-start.20
  481.9 34.6 %collective-permute-done.8.refs_4_ = bf16[320,5120]{1,0:T(8,128)(2,1)S(1)} collective-permute-done((bf16[320,5120]{1,0:T(8,128)(2,1)}, bf16[320,5120]{1,0:T(8,128)(2,1)S(1)}, u32[]{:S(2)}, u32[]{:S(2)}) %collective-permute-start.8) | collective-permute-done | bytes 3276832 | tf_op jit(solution)/shard_map/ppermute | solution.py:53
  517.8 9.6 %fusion.100 = bf16[320,5120]{1,0:T(8,128)(2,1)} fusion(f32[1,1,2,1280,5120]{4,3,2,1,0:T(8,128)} %param.12, s32[]{:T(128)S(6)} %select_n.245, bf16[512,320]{1,0:T(8,128)(2,1)S(1)} %get-tuple-element.96, bf16[512,320]{1,0:T(8,128)(2,1)S(1)} %get-tuple-element.95, bf16[512,5120]{1,0:T(8,128)(2,1)} %fusion.30, bf16[512,5120]{1,0:T(8,128)(2,1)} %copy-done.7), kind=kOutput, calls=%fused_computation.152 | convolution fusion | flops 3381002240 | bytes 20971524 | tf_op jit(solution)/shard_map/tr,tc->rc/dot_general | solution.py:75
  527.5 57.6 %collective-permute-done.13.refs_3_ = bf16[1280,1280]{1,0:T(8,128)(2,1)} collective-permute-done((bf16[1280,1280]{1,0:T(8,128)(2,1)}, bf16[1280,1280]{1,0:T(8,128)(2,1)}, u32[]{:S(2)}, u32[]{:S(2)}) %collective-permute-start.13) | collective-permute-done | bytes 3276832 | tf_op jit(solution)/shard_map/ppermute | solution.py:53
  587.0 70.1 %collective-permute-done.12.refs_2_ = bf16[1280,1280]{1,0:T(8,128)(2,1)} collective-permute-done((bf16[1280,1280]{1,0:T(8,128)(2,1)}, bf16[1280,1280]{1,0:T(8,128)(2,1)}, u32[]{:S(2)}, u32[]{:S(2)}) %collective-permute-start.12) | collective-permute-done | bytes 3276832 | tf_op jit(solution)/shard_map/ppermute | solution.py:53
  659.9 3.5 slice.32
  665.0 9.2 %fusion.101.refs_0_ = bf16[320,5120]{1,0:T(8,128)(2,1)} fusion(f32[1,1,2,1280,5120]{4,3,2,1,0:T(8,128)} %param.12, s32[]{:T(128)S(6)} %select_n.248, bf16[512,320]{1,0:T(8,128)(2,1)S(1)} %get-tuple-element.94, bf16[512,320]{1,0:T(8,128)(2,1)S(1)} %get-tuple-element.93, bf16[512,5120]{1,0:T(8,128)(2,1)} %fusion.30, bf16[512,5120]{1,0:T(8,128)(2,1)} %copy-done.7), kind=kOutput, calls=%fused_computation.153 | convolution fusion | flops 3381002240 | bytes 20971524 | tf_op jit(solution)/shard_map/tr,tc->rc/dot_general | solution.py:75
  675.5 32.5 %collective-permute-done.20 = bf16[960,1280]{1,0:T(8,128)(2,1)} collective-permute-done((bf16[960,1280]{1,0:T(8,128)(2,1)}, bf16[960,1280]{1,0:T(8,128)(2,1)}, u32[]{:S(2)}, u32[]{:S(2)}) %collective-permute-start.20) | collective-permute-done | bytes 2457632 | tf_op jit(solution)/shard_map/ppermute | solution.py:53
  708.0 3.8 pad_maximum_fusion.3.refs_5_
  711.8 3.8 pad_maximum_fusion.2.refs_4_
  715.6 11.0 %shard_map.97.refs_4_ = f32[2,1280,1280]{2,1,0:T(8,128)} custom-call(bf16[1280,1280]{1,0:T(8,128)(2,1)} %fusion.88.refs_0_, bf16[1280,1280]{1,0:T(8,128)(2,1)} %collective-permute-done.14.refs_1_, bf16[1280,1280]{1,0:T(8,128)(2,1)} %collective-permute-done.15.refs_2_, bf16[1280,1280]{1,0:T(8,128)(2,1)} %collective-permute-done.16.refs_3_, ...), custom_call_target="tpu_custom_call" | custom-call | flops 9830400 | bytes 26214400 | tf_op jit(solution)/shard_map/pallas_call | solution.py:37
  726.6 9.2 %shard_map.98 = f32[2,1280,1280]{2,1,0:T(8,128)} custom-call(bf16[1280,1280]{1,0:T(8,128)(2,1)} %fusion.90.refs_0_, bf16[1280,1280]{1,0:T(8,128)(2,1)} %collective-permute-done.11.refs_1_, bf16[1280,1280]{1,0:T(8,128)(2,1)} %collective-permute-done.12.refs_2_, bf16[1280,1280]{1,0:T(8,128)(2,1)} %collective-permute-done.13.refs_3_, ...), custom_call_target="tpu_custom_call", output_to_operand_aliasing={{}: (4, {})} | custom-call | flops 6553600 | bytes 19660800 | tf_op jit(solution)/shard_map/pallas_call | solution.py:37
  735.9 11.0 %shard_map.94.refs_4_ = f32[2,320,5120]{2,1,0:T(8,128)} custom-call(bf16[320,5120]{1,0:T(8,128)(2,1)} %fusion.97.refs_0_, bf16[320,5120]{1,0:T(8,128)(2,1)} %collective-permute-done.5.refs_1_, bf16[320,5120]{1,0:T(8,128)(2,1)} %collective-permute-done.6.refs_2_, bf16[320,5120]{1,0:T(8,128)(2,1)} %collective-permute-done.7.refs_3_, ...), custom_call_target="tpu_custom_call" | custom-call | flops 9830400 | bytes 26214400 | tf_op jit(solution)/shard_map/pallas_call | solution.py:37
  746.9 84.0 %collective-permute-done.4.refs_3_ = bf16[240,5120]{1,0:T(8,128)(2,1)} collective-permute-done((bf16[240,5120]{1,0:T(8,128)(2,1)}, bf16[240,5120]{1,0:T(8,128)(2,1)}, u32[]{:S(2)}, u32[]{:S(2)}) %collective-permute-start.4) | collective-permute-done | bytes 2457632 | tf_op jit(solution)/shard_map/ppermute | solution.py:53
  832.6 7.7 shard_map.95.refs_4_
  840.3 8.1 collective-permute-done.3.refs_3_
  848.4 4.8 shard_map.96
  (89 shorter events, 59.9 us)
Async XLA Ops:
  4.4 113.9 %collective-permute-start.17 = (bf16[320,1280]{1,0:T(8,128)(2,1)}, bf16[320,1280]{1,0:T(8,128)(2,1)}, u32[]{:S(2)}, u32[]{:S(2)}) collective-permute-start(bf16[320,1280]{1,0:T(8,128)(2,1)} %fusion.131), channel_id=1, source_target_pairs={{4,0},{5,1},{6,2},{7,3}} | collective-permute-start | bytes 2457608 | tf_op jit(solution)/shard_map/ppermute | solution.py:53
  5.7 10.5 %copy-start.5 = (bf16[1,512,1280]{2,1,0:T(8,128)(2,1)S(1)}, bf16[1,512,1280]{2,1,0:T(8,128)(2,1)}, u32[]{:S(2)}) copy-start(bf16[1,512,1280]{2,1,0:T(8,128)(2,1)} %param.7) | copy-start | bytes 3932164
  13.9 310.1 %collective-permute-start.15 = (bf16[1280,1280]{1,0:T(8,128)(2,1)}, bf16[1280,1280]{1,0:T(8,128)(2,1)}, u32[]{:S(2)}, u32[]{:S(2)}) collective-permute-start(bf16[1280,1280]{1,0:T(8,128)(2,1)} %fusion.91), channel_id=1, source_target_pairs={{4,6},{5,7},{6,4},{7,5}} | collective-permute-start | bytes 9830408 | tf_op jit(solution)/shard_map/ppermute | solution.py:53
  22.5 270.7 %collective-permute-start.19 = (bf16[960,1280]{1,0:T(8,128)(2,1)}, bf16[960,1280]{1,0:T(8,128)(2,1)}, u32[]{:S(2)}, u32[]{:S(2)}) collective-permute-start(bf16[960,1280]{1,0:T(8,128)(2,1)} %fusion.102), channel_id=1, source_target_pairs={{4,0},{5,1},{6,2},{7,3}} | collective-permute-start | bytes 7372808 | tf_op jit(solution)/shard_map/ppermute | solution.py:53
  41.4 11.3 %copy-start = (bf16[512,5120]{1,0:T(8,128)(2,1)S(1)}, bf16[512,5120]{1,0:T(8,128)(2,1)}, u32[]{:S(2)}) copy-start(bf16[512,5120]{1,0:T(8,128)(2,1)} %fusion.39) | copy-start | bytes 15728644
  50.1 277.0 %collective-permute-start.6 = (bf16[320,5120]{1,0:T(8,128)(2,1)}, bf16[320,5120]{1,0:T(8,128)(2,1)}, u32[]{:S(2)}, u32[]{:S(2)}) collective-permute-start(bf16[320,5120]{1,0:T(8,128)(2,1)} %fusion.92), channel_id=1, source_target_pairs={{4,6},{5,7},{6,4},{7,5}} | collective-permute-start | bytes 9830408 | tf_op jit(solution)/shard_map/ppermute | solution.py:53
  62.7 1.1 copy-start.9
  79.8 12.1 %copy-start.7 = (bf16[512,5120]{1,0:T(8,128)(2,1)}, bf16[512,5120]{1,0:T(8,128)(2,1)S(1)}, u32[]{:S(2)}) copy-start(bf16[512,5120]{1,0:T(8,128)(2,1)S(1)} %fusion.36) | copy-start | bytes 15728644
  92.0 13.5 %copy-start.6 = (bf16[512,1280]{1,0:T(8,128)(2,1)}, bf16[512,1280]{1,0:T(8,128)(2,1)S(1)}, u32[]{:S(2)}) copy-start(bf16[512,1280]{1,0:T(8,128)(2,1)S(1)} %fusion.124) | copy-start | bytes 3932164
  92.0 39.0 %collective-permute-start = (bf16[512,1280]{1,0:T(8,128)(2,1)S(1)}, bf16[512,1280]{1,0:T(8,128)(2,1)}, u32[]{:S(2)}, u32[]{:S(2)}) collective-permute-start(bf16[512,1280]{1,0:T(8,128)(2,1)S(1)} %fusion.124), channel_id=1, source_target_pairs={{4,0},{5,1},{6,2},{7,3}} | collective-permute-start | bytes 3932168 | tf_op jit(solution)/shard_map/ppermute | solution.py:136
  118.3 170.2 %collective-permute-start.18 = (bf16[320,1280]{1,0:T(8,128)(2,1)}, bf16[320,1280]{1,0:T(8,128)(2,1)}, u32[]{:S(2)}, u32[]{:S(2)}) collective-permute-start(bf16[320,1280]{1,0:T(8,128)(2,1)} %collective-permute-done.17), channel_id=1, source_target_pairs={{0,7},{1,6},{2,5},{3,4}} | collective-permute-start | bytes 2457608 | tf_op jit(solution)/shard_map/ppermute | solution.py:53
  155.5 135.3 %collective-permute-start.21 = (bf16[384,1280]{1,0:T(8,128)(2,1)}, bf16[384,1280]{1,0:T(8,128)(2,1)}, u32[]{:S(2)}, u32[]{:S(2)}) collective-permute-start(bf16[384,1280]{1,0:T(8,128)(2,1)} %fusion.130), channel_id=1, source_target_pairs={{0,4},{1,5},{2,6},{3,7}} | collective-permute-start | bytes 2949128 | tf_op jit(solution)/shard_map/ppermute | solution.py:53
  174.2 2.3 copy-start.8
  199.7 4.4 copy-start.10
  199.7 4.5 copy-start.13
  211.4 4.3 copy-start.14
  279.0 9.4 %copy-start.2 = (bf16[320,5120]{1,0:T(8,128)(2,1)S(1)}, bf16[320,5120]{1,0:T(8,128)(2,1)}, u32[]{:S(2)}) copy-start(bf16[320,5120]{1,0:T(8,128)(2,1)} %fusion.93) | copy-start | bytes 9830404
  288.5 114.8 %collective-permute-start.7 = (bf16[320,5120]{1,0:T(8,128)(2,1)S(1)}, bf16[320,5120]{1,0:T(8,128)(2,1)}, u32[]{:S(2)}, u32[]{:S(2)}) collective-permute-start(bf16[320,5120]{1,0:T(8,128)(2,1)S(1)} %copy-done.2), channel_id=1, source_target_pairs={{4,7},{5,6},{6,5},{7,4}} | collective-permute-start | bytes 9830408 | tf_op jit(solution)/shard_map/ppermute | solution.py:53
  290.8 29.7 %collective-permute-start.24 = (bf16[512,1280]{1,0:T(8,128)(2,1)}, bf16[512,1280]{1,0:T(8,128)(2,1)}, u32[]{:S(2)}, u32[]{:S(2)}) collective-permute-start(bf16[512,1280]{1,0:T(8,128)(2,1)} %copy-done.6), channel_id=1, source_target_pairs={{0,4},{1,5},{2,6},{3,7}} | collective-permute-start | bytes 3932168 | tf_op jit(solution)/shard_map/ppermute | solution.py:147
  293.2 89.2 %collective-permute-start.22 = (bf16[384,1280]{1,0:T(8,128)(2,1)}, bf16[384,1280]{1,0:T(8,128)(2,1)}, u32[]{:S(2)}, u32[]{:S(2)}) collective-permute-start(bf16[384,1280]{1,0:T(8,128)(2,1)} %collective-permute-done.21), channel_id=1, source_target_pairs={{4,3},{5,2},{6,1},{7,0}} | collective-permute-start | bytes 2949128 | tf_op jit(solution)/shard_map/ppermute | solution.py:53
  312.4 70.6 %copy-start.11 = (bf16[512,1280]{1,0:T(8,128)(2,1)S(1)}, bf16[512,1280]{1,0:T(8,128)(2,1)}, u32[]{:S(2)}) copy-start(bf16[512,1280]{1,0:T(8,128)(2,1)} %copy-done.9) | copy-start | bytes 3932164
  312.4 70.6 %copy-start.15 = (bf16[512,1280]{1,0:T(8,128)(2,1)S(1)}, bf16[512,1280]{1,0:T(8,128)(2,1)}, u32[]{:S(2)}) copy-start(bf16[512,1280]{1,0:T(8,128)(2,1)} %add_convert_fusion) | copy-start | bytes 3932164
  320.6 86.0 %collective-permute-start.23 = (bf16[896,1280]{1,0:T(8,128)(2,1)}, bf16[896,1280]{1,0:T(8,128)(2,1)}, u32[]{:S(2)}, u32[]{:S(2)}) collective-permute-start(bf16[896,1280]{1,0:T(8,128)(2,1)} %fusion.103), channel_id=1, source_target_pairs={{0,3},{1,2},{2,1},{3,0}} | collective-permute-start | bytes 6881288 | tf_op jit(solution)/shard_map/ppermute | solution.py:53
  323.9 122.5 %collective-permute-start.16 = (bf16[1280,1280]{1,0:T(8,128)(2,1)}, bf16[1280,1280]{1,0:T(8,128)(2,1)}, u32[]{:S(2)}, u32[]{:S(2)}) collective-permute-start(bf16[1280,1280]{1,0:T(8,128)(2,1)} %fusion.84), channel_id=1, source_target_pairs={{0,2},{1,3},{2,0},{3,1}} | collective-permute-start | bytes 9830408 | tf_op jit(solution)/shard_map/ppermute | solution.py:53
  327.2 119.7 %collective-permute-start.5 = (bf16[320,5120]{1,0:T(8,128)(2,1)}, bf16[320,5120]{1,0:T(8,128)(2,1)}, u32[]{:S(2)}, u32[]{:S(2)}) collective-permute-start(bf16[320,5120]{1,0:T(8,128)(2,1)} %fusion.96), channel_id=1, source_target_pairs={{0,1},{1,0},{2,3},{3,2},{4,5},{5,4},{6,7},{7,6}} | collective-permute-start | bytes 9830408 | tf_op jit(solution)/shard_map/ppermute | solution.py:53
  382.4 73.9 %collective-permute-start.14 = (bf16[1280,1280]{1,0:T(8,128)(2,1)}, bf16[1280,1280]{1,0:T(8,128)(2,1)}, u32[]{:S(2)}, u32[]{:S(2)}) collective-permute-start(bf16[1280,1280]{1,0:T(8,128)(2,1)} %fusion.87), channel_id=1, source_target_pairs={{0,1},{1,0},{2,3},{3,2},{4,5},{5,4},{6,7},{7,6}} | collective-permute-start | bytes 9830408 | tf_op jit(solution)/shard_map/ppermute | solution.py:53
  390.2 4.4 copy-start.12
  390.2 4.4 copy-start.16
  403.2 72.2 %collective-permute-start.9 = (bf16[320,5120]{1,0:T(8,128)(2,1)}, bf16[320,5120]{1,0:T(8,128)(2,1)}, u32[]{:S(2)}, u32[]{:S(2)}) collective-permute-start(bf16[320,5120]{1,0:T(8,128)(2,1)} %fusion.95), channel_id=1, source_target_pairs={{0,4},{1,5},{2,6},{3,7}} | collective-permute-start | bytes 9830408 | tf_op jit(solution)/shard_map/ppermute | solution.py:53
  406.5 110.0 %collective-permute-start.8 = (bf16[320,5120]{1,0:T(8,128)(2,1)}, bf16[320,5120]{1,0:T(8,128)(2,1)S(1)}, u32[]{:S(2)}, u32[]{:S(2)}) collective-permute-start(bf16[320,5120]{1,0:T(8,128)(2,1)} %fusion.94), channel_id=1, source_target_pairs={{0,2},{1,3},{2,0},{3,1}} | collective-permute-start | bytes 9830408 | tf_op jit(solution)/shard_map/ppermute | solution.py:53
  446.4 138.7 %collective-permute-start.13 = (bf16[1280,1280]{1,0:T(8,128)(2,1)}, bf16[1280,1280]{1,0:T(8,128)(2,1)}, u32[]{:S(2)}, u32[]{:S(2)}) collective-permute-start(bf16[1280,1280]{1,0:T(8,128)(2,1)} %fusion.86), channel_id=1, source_target_pairs={{0,3},{1,2},{2,1},{3,0},{4,7},{5,6},{6,5},{7,4}} | collective-permute-start | bytes 9830408 | tf_op jit(solution)/shard_map/ppermute | solution.py:53
  446.9 210.2 %collective-permute-start.12 = (bf16[1280,1280]{1,0:T(8,128)(2,1)}, bf16[1280,1280]{1,0:T(8,128)(2,1)}, u32[]{:S(2)}, u32[]{:S(2)}) collective-permute-start(bf16[1280,1280]{1,0:T(8,128)(2,1)} %fusion.85), channel_id=1, source_target_pairs={{0,2},{1,3},{2,0},{3,1},{4,6},{5,7},{6,4},{7,5}} | collective-permute-start | bytes 9830408 | tf_op jit(solution)/shard_map/ppermute | solution.py:53
  447.1 10.4 %copy-start.17 = (bf16[512,1280]{1,0:T(8,128)(2,1)S(1)}, bf16[512,1280]{1,0:T(8,128)(2,1)}, u32[]{:S(2)}) copy-start(bf16[512,1280]{1,0:T(8,128)(2,1)} %add_convert_fusion) | copy-start | bytes 3932164
  456.3 208.6 %collective-permute-start.11 = (bf16[1280,1280]{1,0:T(8,128)(2,1)}, bf16[1280,1280]{1,0:T(8,128)(2,1)}, u32[]{:S(2)}, u32[]{:S(2)}) collective-permute-start(bf16[1280,1280]{1,0:T(8,128)(2,1)} %fusion.89), channel_id=1, source_target_pairs={{0,1},{1,0},{2,3},{3,2},{4,5},{5,4},{6,7},{7,6}} | collective-permute-start | bytes 9830408 | tf_op jit(solution)/shard_map/ppermute | solution.py:53
  475.4 232.6 %collective-permute-start.20 = (bf16[960,1280]{1,0:T(8,128)(2,1)}, bf16[960,1280]{1,0:T(8,128)(2,1)}, u32[]{:S(2)}, u32[]{:S(2)}) collective-permute-start(bf16[960,1280]{1,0:T(8,128)(2,1)} %collective-permute-done.19), channel_id=1, source_target_pairs={{0,7},{1,6},{2,5},{3,4}} | collective-permute-start | bytes 7372808 | tf_op jit(solution)/shard_map/ppermute | solution.py:53
  516.5 10.9 %copy-start.3 = (bf16[320,5120]{1,0:T(8,128)(2,1)}, bf16[320,5120]{1,0:T(8,128)(2,1)S(1)}, u32[]{:S(2)}) copy-start(bf16[320,5120]{1,0:T(8,128)(2,1)S(1)} %collective-permute-done.8.refs_4_) | copy-start | bytes 9830404
  516.5 219.3 %collective-permute-start.10 = (bf16[320,5120]{1,0:T(8,128)(2,1)}, bf16[320,5120]{1,0:T(8,128)(2,1)}, u32[]{:S(2)}, u32[]{:S(2)}) collective-permute-start(bf16[320,5120]{1,0:T(8,128)(2,1)} %collective-permute-done.9), channel_id=1, source_target_pairs={{4,3},{5,2},{6,1},{7,0}} | collective-permute-start | bytes 9830408 | tf_op jit(solution)/shard_map/ppermute | solution.py:53
  585.1 245.8 %collective-permute-start.1 = (bf16[320,5120]{1,0:T(8,128)(2,1)}, bf16[320,5120]{1,0:T(8,128)(2,1)S(1)}, u32[]{:S(2)}, u32[]{:S(2)}) collective-permute-start(bf16[320,5120]{1,0:T(8,128)(2,1)} %fusion.100), channel_id=1, source_target_pairs={{0,1},{1,0},{2,3},{3,2},{4,5},{5,4},{6,7},{7,6}} | collective-permute-start | bytes 9830408 | tf_op jit(solution)/shard_map/ppermute | solution.py:53
  657.1 173.8 %collective-permute-start.2 = (bf16[320,5120]{1,0:T(8,128)(2,1)}, bf16[320,5120]{1,0:T(8,128)(2,1)}, u32[]{:S(2)}, u32[]{:S(2)}) collective-permute-start(bf16[320,5120]{1,0:T(8,128)(2,1)} %fusion.98), channel_id=1, source_target_pairs={{0,2},{1,3},{2,0},{3,1},{4,6},{5,7},{6,4},{7,5}} | collective-permute-start | bytes 9830408 | tf_op jit(solution)/shard_map/ppermute | solution.py:53
  664.9 165.9 %collective-permute-start.4 = (bf16[240,5120]{1,0:T(8,128)(2,1)}, bf16[240,5120]{1,0:T(8,128)(2,1)}, u32[]{:S(2)}, u32[]{:S(2)}) collective-permute-start(bf16[240,5120]{1,0:T(8,128)(2,1)} %slice.32), channel_id=1, source_target_pairs={{0,3},{1,2},{2,1},{3,0},{4,7},{5,6},{6,5},{7,4}} | collective-permute-start | bytes 7372808 | tf_op jit(solution)/shard_map/ppermute | solution.py:53
  665.0 9.2 %copy-start.4 = (bf16[512,1280]{1,0:T(8,128)(2,1)S(1)}, bf16[512,1280]{1,0:T(8,128)(2,1)}, u32[]{:S(2)}) copy-start(bf16[512,1280]{1,0:T(8,128)(2,1)} %fusion.121) | copy-start | bytes 3932164
  708.0 140.4 %collective-permute-start.3 = (bf16[80,5120]{1,0:T(8,128)(2,1)}, bf16[80,5120]{1,0:T(8,128)(2,1)}, u32[]{:S(2)}, u32[]{:S(2)}) collective-permute-start(bf16[80,5120]{1,0:T(8,128)(2,1)} %slice.33), channel_id=1, source_target_pairs={{0,3},{1,2},{2,1},{3,0},{4,7},{5,6},{6,5},{7,4}} | collective-permute-start | bytes 2457608 | tf_op jit(solution)/shard_map/ppermute | solution.py:53
  830.9 1.7 copy-start.1

commit v2 on v1

v2 whole, which is shorter than its diff:
```python
import jax
import jax.numpy as jnp
from jax import lax
from jax.experimental import pallas as pl
from jax.experimental.pallas import tpu as pltpu
from jax.sharding import PartitionSpec as P


C0 = 0.7978845608028654
C1 = C0 * 0.044715


def gelu_tile(h):
    h = h.astype(jnp.float32)
    return (h * (0.5 + 0.5 * jnp.tanh(h * (C0 + C1 * (h * h))))).astype(jnp.bfloat16)


def nt(lhs, rhs):
    return lax.dot_general(lhs, rhs, (((1,), (1,)), ((), ())), preferred_element_type=jnp.float32)


def tn(lhs, rhs):
    return lax.dot_general(lhs, rhs, (((0,), (0,)), ((), ())), preferred_element_type=jnp.float32)


def layer(slot, g, hs, wb, wa, k, bf=1024):
    toks, dm = g.shape
    ff = wb.shape[1]
    nb = ff // bf

    def kern(p, g_ref, h_ref, wb_ref, wa_ref, dh_ref, o_ref, acc):
        i = pl.program_id(0)
        u = nt(g_ref[...], wb_ref[0])
        h = h_ref[0, 0].astype(jnp.float32)
        h2 = h * h
        t = jnp.tanh(h * (C0 + C1 * h2))
        slope = (0.5 + 0.5 * t) + (0.5 * h) * (1.0 - t * t) * (C0 + 3.0 * C1 * h2)
        dh = (slope * u).astype(jnp.bfloat16)
        dh_ref[...] = dh
        v = nt(dh, wa_ref[0])

        @pl.when(i == 0)
        def _():
            acc[...] = v

        @pl.when(i > 0)
        def _():
            acc[...] += v

        @pl.when(i == nb - 1)
        def _():
            o_ref[...] = (g_ref[...].astype(jnp.float32) + acc[...]).astype(jnp.bfloat16)

    return pl.pallas_call(
        kern,
        grid_spec=pltpu.PrefetchScalarGridSpec(
            num_scalar_prefetch=1, grid=(nb,),
            in_specs=[pl.BlockSpec((toks, dm), lambda i, p: (0, 0)), pl.BlockSpec((1, 1, toks, bf), lambda i, p: (p[0], k, 0, i)),
                      pl.BlockSpec((1, bf, dm), lambda i, p: (k, i, 0)), pl.BlockSpec((1, dm, bf), lambda i, p: (k, 0, i))],
            out_specs=[pl.BlockSpec((toks, bf), lambda i, p: (0, i)), pl.BlockSpec((toks, dm), lambda i, p: (0, 0))],
            scratch_shapes=[pltpu.VMEM((toks, dm), jnp.float32)]),
        out_shape=[jax.ShapeDtypeStruct((toks, ff), jnp.bfloat16), jax.ShapeDtypeStruct((toks, dm), jnp.bfloat16)],
        cost_estimate=pl.CostEstimate(flops=4 * toks * dm * ff, bytes_accessed=4 * dm * ff, transcendentals=toks * ff),
        compiler_params=pltpu.CompilerParams(vmem_limit_bytes=48 << 20),
    )(slot.reshape(1), g, hs, wb, wa)


def grad2(at, slots, acc, k, hs, kb, cots, count, bm=256):
    n = len(cots)
    toks, cols = cots[0].shape

    def kern(*refs):
        acc_ref, o_ref = refs[1 + 2 * n], refs[2 + 2 * n]
        total = acc_ref[0]
        for i in range(n):
            total = total + tn(gelu_tile(refs[1 + i][0, 0]), refs[1 + n + i][...])
        o_ref[...] = total.astype(jnp.bfloat16)

    def hspec(j):
        return pl.BlockSpec((1, 1, toks, bm), lambda i, p: (p[1 + j], kb, 0, p[0] + i))

    sp = jnp.stack([at // bm, *slots]).astype(jnp.int32)
    return pl.pallas_call(
        kern,
        grid_spec=pltpu.PrefetchScalarGridSpec(
            num_scalar_prefetch=1, grid=(count // bm,),
            in_specs=[hspec(j) for j in range(n)] + [pl.BlockSpec((toks, cols), lambda i, p: (0, 0))] * n
            + [pl.BlockSpec((1, bm, cols), lambda i, p: (k, p[0] + i, 0))],
            out_specs=pl.BlockSpec((bm, cols), lambda i, p: (i, 0))),
        out_shape=jax.ShapeDtypeStruct((count, cols), jnp.bfloat16),
        cost_estimate=pl.CostEstimate(flops=2 * count * cols * toks * n, bytes_accessed=6 * count * cols, transcendentals=0),
        compiler_params=pltpu.CompilerParams(vmem_limit_bytes=48 << 20),
    )(sp, *[hs] * n, *cots, acc)


def grad1(q, acc, k, lhs, dhs, first=0, count=None):
    bn = 1024
    n = len(lhs)
    rows, toks = lhs[0].shape
    cols = count or dhs[0].shape[1]
    b0 = first // bn

    def kern(*refs):
        acc_ref, o_ref = refs[1 + 2 * n], refs[2 + 2 * n]
        total = acc_ref[0]
        for i in range(n):
            total = total + jnp.dot(refs[1 + i][...], refs[1 + n + i][...], preferred_element_type=jnp.float32)
        o_ref[...] = total.astype(jnp.bfloat16)

    return pl.pallas_call(
        kern,
        grid_spec=pltpu.PrefetchScalarGridSpec(
            num_scalar_prefetch=1, grid=(cols // bn,),
            in_specs=[pl.BlockSpec((rows, toks), lambda i, p: (0, 0))] * n + [pl.BlockSpec((toks, bn), lambda i, p: (0, b0 + i))] * n
            + [pl.BlockSpec((1, rows, bn), lambda i, p: (k, p[0], b0 + i))],
            out_specs=pl.BlockSpec((rows, bn), lambda i, p: (0, i))),
        out_shape=jax.ShapeDtypeStruct((rows, cols), jnp.bfloat16),
        cost_estimate=pl.CostEstimate(flops=2 * rows * cols * toks * n, bytes_accessed=6 * rows * cols, transcendentals=0),
        compiler_params=pltpu.CompilerParams(vmem_limit_bytes=48 << 20),
    )(q.reshape(1), *lhs, *dhs, acc)


def reduce_into(buf, parts, k, shape, scale, br, first, count):
    cols = shape[2]
    n = len(parts)
    steps = count // br

    def kern(*refs):
        total = refs[0][...].astype(jnp.float32)
        for r in refs[1:n]:
            total = total + r[...].astype(jnp.float32)
        refs[-1][0] = total * scale

    def block(off):
        return pl.BlockSpec((br, cols), lambda i: (off // br + i, 0))

    in_specs = [block(off) for _, off in parts]
    args = [p for p, _ in parts]
    aliases = {}
    if buf is not None:
        in_specs.append(pl.BlockSpec(memory_space=pl.ANY))
        args.append(buf)
        aliases = {n: 0}
    return pl.pallas_call(
        kern, grid=(steps,), in_specs=in_specs,
        out_specs=pl.BlockSpec((1, br, cols), lambda i: (k, first // br + i, 0)),
        out_shape=jax.ShapeDtypeStruct(shape, jnp.float32),
        input_output_aliases=aliases,
        cost_estimate=pl.CostEstimate(flops=count * cols * n, bytes_accessed=count * cols * (2 * n + 4), transcendentals=0),
    )(*args)


def solution(mesh):
    npp = mesh.shape['pp']
    ndp = mesh.shape['dp']
    assert npp == 2 and ndp == 4
    both = ('pp', 'dp')

    def hop(p, routes, off):
        return lax.ppermute(p, both, [(a * ndp + i, b * ndp + (i ^ off)) for a, b in routes for i in range(ndp)])

    def body(dy, xs, hs, w1, w2, acc1, acc2):
        s = lax.axis_index('pp')
        d = lax.axis_index('dp')
        nk = w1.shape[1]
        acc1, acc2, w1, w2, xs, hs = acc1[0, 0], acc2[0, 0], w1[0], w2[0], xs[0], hs[0]
        n1, n2 = acc1.shape[1] // ndp, acc2.shape[1] // ndp
        nc = n2 // 5
        nd = 7 * n2 // 10
        slot = (npp - 1 - s, jnp.int32(0))

        def rows_of(i, k, off, arr):
            return lax.dynamic_slice(arr, (slot[i], k, 0, (d ^ off) * n1), (1, 1, arr.shape[2], n1))[0, 0].T

        def early(off, first, count, bm):
            return grad2((d ^ off) * n2 + first, [slot[0]], acc2, 1, hs, 1, [dy[0]], count, bm)

        def both2(k, off, first=0, count=None, bm=640):
            return grad2((d ^ off) * n2 + first, slot, acc2, k, hs, k, [ga[k], gb[k]], count or n2, bm)

        def both1(k, off):
            return grad1(d ^ off, acc1, k, [rows_of(i, k, off, xlate) for i in range(2)], [da[k], db[k]])

        def back(g, i, k):
            return layer(slot[i], g, hs, w2, w1, k)

        ga, gb, da, db = {1: dy[0]}, {}, {}, {}
        stay, down, rise = [(0, 0), (1, 1)], [(1, 0)], [(0, 1)]
        near, own = {}, {}

        c0 = early(3, 0, nc, nc)
        e2 = early(2, 0, n2, n2 // 2)
        c1 = early(3, nc, 2 * nc, nc)
        c2 = early(3, 3 * nc, 2 * nc, nc)
        far12 = [(hop(e2, [(1, 1)], 2), 0)]

        def detour(p, off):
            return hop(hop(p, down, 0), rise, off)

        lane = [detour(p, 3) for p in (c0, c1, c2)]
        da[1], ga[0] = back(ga[1], 0, 1)
        far11 = []

        def early1(off, arr, first=0, count=None):
            return grad1(d ^ off, acc1, 1, [rows_of(0, 1, off, arr)], [da[1]], first, count)

        side = 3 * acc1.shape[2] // 5
        e112 = [detour(early1(2, xs, side, acc1.shape[2] - side), 2)]
        e112.insert(0, hop(early1(2, xs, 0, side), [(1, 1)], 2))
        da[0], gout = back(ga[0], 0, 0)
        gout, xmid = lax.optimization_barrier((gout, xs))
        recv = lax.ppermute(gout, 'pp', [(1, 0)])
        far11.append((hop(early1(3, xmid), [(1, 1)], 3), 0))
        p = grad2((d ^ 2) * n2, [slot[0]], acc2, 0, hs, 0, [ga[0]], n2, n2 // 2)
        far02 = [(hop(p, [(1, 1)], 2), 0)]

        gb[1], xlate = lax.optimization_barrier((recv, xmid))
        recv = gb[1]
        u = hop(both2(1, 3, nd, n2 - nd, nc // 2), [(0, 0)], 3)
        far12.append((hop(both2(1, 2), [(0, 0)], 2), 0))
        t = hop(hop(both2(1, 3, 0, nd, nc // 2), rise, 0), down, 3)
        db[1], gb[0] = back(gb[1], 1, 1)
        gave = lax.ppermute(gout, 'pp', [(0, 1)])
        far02.append((hop(both2(0, 2), [(0, 0)], 2), 0))
        far02.append((hop(both2(0, 3), stay, 3), 0))
        far11.append((hop(both1(1, 2), [(0, 0)], 2), 0))
        far11.append((hop(hop(both1(1, 3), rise, 0), down, 3), 0))
        near[1, 2] = hop(both2(1, 1), stay, 1)
        near[1, 1] = hop(both1(1, 1), stay, 1)
        own[1, 2] = both2(1, 0)
        own[1, 1] = both1(1, 0)
        db[0], g = back(gb[0], 1, 0)
        near[0, 2] = hop(both2(0, 1), stay, 1)
        own[0, 2] = both2(0, 0)
        p012 = both1(0, 2)
        p013 = both1(0, 3)
        cut = 4 * n1 // 5
        p012a, p012b, p013a, p013b = lax.optimization_barrier((p012[:cut], p012[cut:], p013[:cut], p013[cut:]))
        far012a = hop(p012a, stay, 2)
        far013a = hop(p013a, stay, 3)
        near[0, 1] = hop(both1(0, 1), stay, 1)
        own[0, 1] = both1(0, 0)
        dx = jnp.where(s == 0, g, gave)
        far12.append((jnp.concatenate(lane, 0), 0))
        far12.append((jnp.concatenate([t, u], 0), 0))
        far11.append((jnp.concatenate(e112, 1), 0))
        sc = 1.0 / ndp
        sh1, sh2 = (nk, n1, acc1.shape[2]), (nk, n2, acc2.shape[2])

        def base(k, w, off=0):
            return [(own[k, w], off), (near[k, w], off)]

        o2 = reduce_into(None, base(1, 2) + far12, 1, sh2, sc, n2 // 5, 0, n2)
        o1 = reduce_into(None, base(1, 1) + far11, 1, sh1, sc, n1 // 5, 0, n1)
        o2 = reduce_into(o2, base(0, 2) + far02, 0, sh2, sc, n2 // 5, 0, n2)
        far012a, far013a, p012b, p013b, o1, o2 = lax.optimization_barrier((far012a, far013a, p012b, p013b, o1, o2))
        far012b, far013b = hop(p012b, stay, 2), hop(p013b, stay, 3)
        o1 = reduce_into(o1, base(0, 1) + [(far012a, 0), (far013a, 0)], 0, sh1, sc, cut // 8, 0, cut)
        o1 = reduce_into(o1, base(0, 1, cut) + [(far012b, 0), (far013b, 0)], 0, sh1, sc, 16, cut, n1 - cut)
        return o1[None], o2[None], dx[None]

    spec_row = P(('grp', 'pp'), 'dp', None)
    spec_saved = P(('grp', 'pp'), None, None, 'dp', None)
    spec_w = P(('grp', 'pp'), None, None, None)
    spec_acc = P(('grp', 'pp'), 'dp', None, None, None)
    spec_g = P(('grp', 'pp'), None, 'dp', None)
    return jax.shard_map(body, mesh=mesh, in_specs=(spec_row, spec_saved, spec_saved, spec_w, spec_w, spec_acc, spec_acc), out_specs=(spec_g, spec_g, spec_row), check_vma=False)
```

time: 860 us -> 762 us (0.89)
  the two profiles are of different devices: /device:TPU:0 before, /device:TPU:5 now
where the time goes in v2:
time: 762 us; the launch traced here: 752 us
  Pallas kernels  328 us (43%)
  waiting for transfers between devices  297 us (39%)
  starting transfers between devices  65 us (9%)
  local copies, waits for them, and re-layouts  46.2 us (6%)
  other arithmetic  14.4 us (2%)
    ppermute x29, waiting for transfers between devices, hop(): lax.ppermute(p, both, [(a * ndp + i, b * ndp + (i ^ off)) for a, b in rou...  297 us
    pallas_call x14, Pallas kernels, grad2(): pl.pallas_call(kern, grid_spec=pltpu.PrefetchScalarGridSpec(num_scalar_pr...  97.3 us
    pallas_call x11, Pallas kernels, grad1(): pl.pallas_call(kern, grid_spec=pltpu.PrefetchScalarGridSpec(num_scalar_pr...  93.5 us
    pallas_call x4, Pallas kernels, layer(): pl.pallas_call(kern, grid_spec=pltpu.PrefetchScalarGridSpec(num_scalar_pr...  92.7 us
    ppermute x29, starting transfers between devices, hop(): lax.ppermute(p, both, [(a * ndp + i, b * ndp + (i ^ off)) for a, b in rou...  61.3 us
    pallas_call x5, Pallas kernels, reduce_into(): pl.pallas_call(kern, grid=(steps,), in_specs=in_specs, out_specs=pl.Block...  44.7 us
    dynamic_slice x21, local copies, waits for them, and re-layouts, rows_of(): lax.dynamic_slice(arr, (slot[i], k, 0, (d ^ off) * n1), (1, 1, arr.shape[...  26.2 us
  transfers between devices with their start and end apart: 31, of which 13 were waited for; matrix products, arithmetic and copies ran while one was open for 6% of the time, Pallas kernels for 37%

profile of v2, /device:TPU:5, one launch (start us, length us, event | category | flops | bytes accessed | tf_op | source)
XLA Modules:
  0.0 751.9 jit_solution(7538234872009398805)
XLA Ops:
  2.0 22.7 %shard_map.94 = (bf16[512,5120]{1,0:T(8,128)(2,1)}, bf16[512,1280]{1,0:T(8,128)(2,1)S(1)}) custom-call(s32[1]{0:T(128)} %bitcast.1.p, bf16[512,1280]{1,0:T(8,128)(2,1)S(1)} %bitcast.79, bf16[2,2,512,5120]{3,2,1,0:T(8,128)(2,1)} %bitcast.108, bf16[2,5120,1280]{2,1,0:T(8,128)(2,1)} %bitcast.160, bf16[2,1280,5120]{2,1,0:T(8,128)(2,1)} %bitcast.164), custom_call_target="tpu_custom_call" | custom-call | flops 13421772800 | bytes 26214400 | tf_op jit(solution)/shard_map/pallas_call | solution.py:54
  24.7 23.3 %shard_map.95 = (bf16[512,5120]{1,0:T(8,128)(2,1)}, bf16[512,1280]{1,0:T(8,128)(2,1)}) custom-call(s32[1]{0:T(128)} %bitcast.1.p, bf16[512,1280]{1,0:T(8,128)(2,1)S(1)} %get-tuple-element.25.g_ref.refs_3_.refs_2_, bf16[2,2,512,5120]{3,2,1,0:T(8,128)(2,1)} %bitcast.109, bf16[2,5120,1280]{2,1,0:T(8,128)(2,1)} %bitcast.161, bf16[2,1280,5120]{2,1,0:T(8,128)(2,1)} %bitcast.165), custom_call_target="tpu_custom_call" | custom-call | flops 13421772800 | bytes 26214400 | tf_op jit(solution)/shard_map/pallas_call | solution.py:54
  48.0 2.5 collective-permute-start
  50.5 4.2 shard_map.120
  54.8 2.4 collective-permute-start.21
  57.2 3.5 shard_map.119
  62.9 4.2 shard_map.121
  67.1 2.4 collective-permute-start.23
  70.9 3.8 shard_map.108
  74.7 2.3 collective-permute-start.10
  77.0 5.7 shard_map.107
  82.7 36.9 %collective-permute-done.19 = bf16[256,1280]{1,0:T(8,128)(2,1)} collective-permute-done((bf16[256,1280]{1,0:T(8,128)(2,1)}, bf16[256,1280]{1,0:T(8,128)(2,1)}, u32[]{:S(2)}, u32[]{:S(2)}) %collective-permute-start.19) | collective-permute-done | bytes 655392 | tf_op jit(solution)/shard_map/ppermute | solution.py:160
  119.6 3.5 collective-permute-start.9
  124.7 6.7 shard_map.117
  133.3 6.7 shard_map.112
  140.0 7.7 %collective-permute-done.23 = bf16[512,1280]{1,0:T(8,128)(2,1)} collective-permute-done((bf16[512,1280]{1,0:T(8,128)(2,1)}, bf16[512,1280]{1,0:T(8,128)(2,1)}, u32[]{:S(2)}, u32[]{:S(2)}) %collective-permute-start.23) | collective-permute-done | bytes 1310752 | tf_op jit(solution)/shard_map/ppermute | solution.py:160
  147.7 3.5 collective-permute-start.13
  151.3 5.6 shard_map.123
  158.5 17.2 %collective-permute-done.10 = bf16[320,2048]{1,0:T(8,128)(2,1)} collective-permute-done((bf16[320,2048]{1,0:T(8,128)(2,1)}, bf16[320,2048]{1,0:T(8,128)(2,1)}, u32[]{:S(2)}, u32[]{:S(2)}) %collective-permute-start.10) | collective-permute-done | bytes 1310752 | tf_op jit(solution)/shard_map/ppermute | solution.py:160
  178.9 8.4 %shard_map.104 = bf16[320,5120]{1,0:T(8,128)(2,1)} custom-call(s32[1]{0:T(128)} %bitcast.22.refs_0_, bf16[320,512]{1,0:T(8,128)(2,1)S(1)} %bitcast.107, bf16[512,5120]{1,0:T(8,128)(2,1)} %get-tuple-element.38.refs_3_.refs_2_, f32[2,1280,5120]{2,1,0:T(8,128)} %bitcast.151), custom_call_target="tpu_custom_call" | custom-call | flops 1677721600 | bytes 9830400 | tf_op jit(solution)/shard_map/pallas_call | solution.py:110
  187.3 8.9 %shard_map.118 = bf16[1280,1280]{1,0:T(8,128)(2,1)} custom-call(s32[3]{0:T(128)S(1)} %pad_add_fusion.3.refs_0_, bf16[2,2,512,5120]{3,2,1,0:T(8,128)(2,1)} %bitcast.117, bf16[2,2,512,5120]{3,2,1,0:T(8,128)(2,1)} %bitcast.118, bf16[512,1280]{1,0:T(8,128)(2,1)S(1)} %bitcast.85, bf16[512,1280]{1,0:T(8,128)(2,1)} %collective-permute-done.g_ref.refs_4_, ...), custom_call_target="tpu_custom_call" | custom-call | flops 3355443200 | bytes 9830400 | tf_op jit(solution)/shard_map/pallas_call | solution.py:83
  198.8 8.8 %shard_map.116 = bf16[1280,1280]{1,0:T(8,128)(2,1)} custom-call(s32[3]{0:T(128)S(1)} %pad_add_fusion.4.refs_0_, bf16[2,2,512,5120]{3,2,1,0:T(8,128)(2,1)} %bitcast.119, bf16[2,2,512,5120]{3,2,1,0:T(8,128)(2,1)} %bitcast.120, bf16[512,1280]{1,0:T(8,128)(2,1)S(1)} %bitcast.86, bf16[512,1280]{1,0:T(8,128)(2,1)} %collective-permute-done.g_ref.refs_4_, ...), custom_call_target="tpu_custom_call" | custom-call | flops 3355443200 | bytes 9830400 | tf_op jit(solution)/shard_map/pallas_call | solution.py:83
  207.6 7.1 collective-permute-done.22
  214.6 3.4 collective-permute-start.5
  218.1 23.8 %shard_map.96 = (bf16[512,5120]{1,0:T(8,128)(2,1)}, bf16[512,1280]{1,0:T(8,128)(2,1)S(1)}) custom-call(s32[1]{0:T(128)} %constant.90.clone.1.p, bf16[512,1280]{1,0:T(8,128)(2,1)} %collective-permute-done.g_ref.refs_4_, bf16[2,2,512,5120]{3,2,1,0:T(8,128)(2,1)} %bitcast.121, bf16[2,5120,1280]{2,1,0:T(8,128)(2,1)} %bitcast.162, bf16[2,1280,5120]{2,1,0:T(8,128)(2,1)} %bitcast.166), custom_call_target="tpu_custom_call" | custom-call | flops 13421772800 | bytes 26214400 | tf_op jit(solution)/shard_map/pallas_call | solution.py:54
  242.4 2.6 collective-permute-start.18
  245.0 23.5 %collective-permute-done.11 = bf16[320,2048]{1,0:T(8,128)(2,1)S(1)} collective-permute-done((bf16[320,2048]{1,0:T(8,128)(2,1)}, bf16[320,2048]{1,0:T(8,128)(2,1)S(1)}, u32[]{:S(2)}, u32[]{:S(2)}) %collective-permute-start.11) | collective-permute-done | bytes 1310752 | tf_op jit(solution)/shard_map/ppermute | solution.py:160
  268.5 2.7 collective-permute-start.16
  271.2 8.3 %shard_map.114 = bf16[1280,1280]{1,0:T(8,128)(2,1)} custom-call(s32[3]{0:T(128)S(1)} %pad_add_fusion.2.refs_0_, bf16[2,2,512,5120]{3,2,1,0:T(8,128)(2,1)} %bitcast.122, bf16[2,2,512,5120]{3,2,1,0:T(8,128)(2,1)} %bitcast.123, bf16[512,1280]{1,0:T(8,128)(2,1)S(1)} %get-tuple-element.25.g_ref.refs_3_.refs_2_, ...), custom_call_target="tpu_custom_call" | custom-call | flops 3355443200 | bytes 9830400 | tf_op jit(solution)/shard_map/pallas_call | solution.py:83
  280.4 9.4 %shard_map.122 = bf16[896,1280]{1,0:T(8,128)(2,1)} custom-call(s32[3]{0:T(128)S(1)} %pad_add_fusion.1.refs_0_, bf16[2,2,512,5120]{3,2,1,0:T(8,128)(2,1)} %bitcast.124, bf16[2,2,512,5120]{3,2,1,0:T(8,128)(2,1)} %bitcast.125, bf16[512,1280]{1,0:T(8,128)(2,1)S(1)} %bitcast.87, bf16[512,1280]{1,0:T(8,128)(2,1)} %collective-permute-done.g_ref.refs_4_, ...), custom_call_target="tpu_custom_call" | custom-call | flops 2348810240 | bytes 6881280 | tf_op jit(solution)/shard_map/pallas_call | solution.py:83
  289.8 14.5 %collective-permute-done.13.refs_2_ = bf16[1280,1280]{1,0:T(8,128)(2,1)} collective-permute-done((bf16[1280,1280]{1,0:T(8,128)(2,1)}, bf16[1280,1280]{1,0:T(8,128)(2,1)}, u32[]{:S(2)}, u32[]{:S(2)}) %collective-permute-start.13) | collective-permute-done | bytes 3276832 | tf_op jit(solution)/shard_map/ppermute | solution.py:160
  307.0 8.2 %shard_map.113 = bf16[1280,1280]{1,0:T(8,128)(2,1)} custom-call(s32[3]{0:T(128)S(1)} %pad_add_fusion.3.refs_0_, bf16[2,2,512,5120]{3,2,1,0:T(8,128)(2,1)} %bitcast.126, bf16[2,2,512,5120]{3,2,1,0:T(8,128)(2,1)} %bitcast.127, bf16[512,1280]{1,0:T(8,128)(2,1)S(1)} %get-tuple-element.25.g_ref.refs_3_.refs_2_, bf16[512,1280]{1,0:T(8,128)(2,1)S(1)} %copy-done.3, ...), custom_call_target="tpu_custom_call" | custom-call | flops 3355443200 | bytes 9830400 | tf_op jit(solution)/shard_map/pallas_call | solution.py:83
  315.2 65.1 %collective-permute-done.5.refs_2_ = bf16[320,5120]{1,0:T(8,128)(2,1)} collective-permute-done((bf16[320,5120]{1,0:T(8,128)(2,1)}, bf16[320,5120]{1,0:T(8,128)(2,1)}, u32[]{:S(2)}, u32[]{:S(2)}) %collective-permute-start.5) | collective-permute-done | bytes 3276832 | tf_op jit(solution)/shard_map/ppermute | solution.py:160
  380.3 2.3 collective-permute-start.14
  382.6 10.2 %constant_dynamic-slice_fusion.1 = (bf16[1,1,512,320]{3,2,1,0:T(8,128)(2,1)}, bf16[1,1,512,320]{3,2,1,0:T(8,128)(2,1)S(1)}, bf16[1,1,512,320]{3,2,1,0:T(8,128)(2...) fusion(bf16[2,2,512,1280]{3,2,1,0:T(8,128)(2,1)} %bitcast.171, ...), kind=kLoop, calls=%fused_computation.5 | loop fusion | bytes 10485780 | tf_op jit(solution)/shard_map/dynamic_slice | solution.py:173
  394.1 10.5 %shard_map.106 = bf16[320,5120]{1,0:T(8,128)(2,1)} custom-call(s32[1]{0:T(128)} %bitcast.22.refs_0_, bf16[320,512]{1,0:T(8,128)(2,1)S(1)} %bitcast.105, bf16[320,512]{1,0:T(8,128)(2,1)S(1)} %bitcast.106, bf16[512,5120]{1,0:T(8,128)(2,1)} %get-tuple-element.38.refs_3_.refs_2_, bf16[512,5120]{1,0:T(8,128)(2,1)} %get-tuple-element.39.refs_4_, ...), custom_call_target="tpu_custom_call" | custom-call | flops 3355443200 | bytes 9830400 | tf_op jit(solution)/shard_map/pallas_call | solution.py:110
  411.8 8.2 %shard_map.111 = bf16[1280,1280]{1,0:T(8,128)(2,1)} custom-call(s32[3]{0:T(128)S(1)} %pad_add_fusion.4.refs_0_, bf16[2,2,512,5120]{3,2,1,0:T(8,128)(2,1)} %bitcast.128, bf16[2,2,512,5120]{3,2,1,0:T(8,128)(2,1)} %bitcast.129, bf16[512,1280]{1,0:T(8,128)(2,1)S(1)} %get-tuple-element.25.g_ref.refs_3_.refs_2_, bf16[512,1280]{1,0:T(8,128)(2,1)S(1)} %copy-done.4, ...), custom_call_target="tpu_custom_call" | custom-call | flops 3355443200 | bytes 9830400 | tf_op jit(solution)/shard_map/pallas_call | solution.py:83
  420.0 8.7 %shard_map.105 = bf16[320,5120]{1,0:T(8,128)(2,1)S(1)} custom-call(s32[1]{0:T(128)} %bitcast.17.refs_0_, bf16[320,512]{1,0:T(8,128)(2,1)S(1)} %bitcast.103, bf16[320,512]{1,0:T(8,128)(2,1)S(1)} %bitcast.104, bf16[512,5120]{1,0:T(8,128)(2,1)} %get-tuple-element.38.refs_3_.refs_2_, bf16[512,5120]{1,0:T(8,128)(2,1)} %get-tuple-element.39.refs_4_, ...), custom_call_target="tpu_custom_call" | custom-call | flops 3355443200 | bytes 9830400 | tf_op jit(solution)/shard_map/pallas_call | solution.py:110
  431.6 2.3 collective-permute-start.6
  433.9 10.5 %shard_map.103 = bf16[320,5120]{1,0:T(8,128)(2,1)} custom-call(s32[1]{0:T(128)} %bitcast.12.refs_0_, bf16[320,512]{1,0:T(8,128)(2,1)S(1)} %bitcast.93, bf16[320,512]{1,0:T(8,128)(2,1)S(1)} %bitcast.100, bf16[512,5120]{1,0:T(8,128)(2,1)} %get-tuple-element.38.refs_3_.refs_2_, bf16[512,5120]{1,0:T(8,128)(2,1)} %get-tuple-element.39.refs_4_, ...), custom_call_target="tpu_custom_call" | custom-call | flops 3355443200 | bytes 9830400 | tf_op jit(solution)/shard_map/pallas_call | solution.py:110
  444.4 3.2 collective-permute-done.15.refs_4_
  451.4 22.8 %shard_map.97 = (bf16[512,5120]{1,0:T(8,128)(2,1)}, bf16[512,1280]{1,0:T(8,128)(2,1)S(1)}) custom-call(s32[1]{0:T(128)} %constant.90.clone.1.p, bf16[512,1280]{1,0:T(8,128)(2,1)S(1)} %copy-done.5, bf16[2,2,512,5120]{3,2,1,0:T(8,128)(2,1)} %bitcast.130, bf16[2,5120,1280]{2,1,0:T(8,128)(2,1)} %bitcast.163, bf16[2,1280,5120]{2,1,0:T(8,128)(2,1)} %bitcast.167), custom_call_target="tpu_custom_call" | custom-call | flops 13421772800 | bytes 26214400 | tf_op jit(solution)/shard_map/pallas_call | solution.py:54
  475.3 9.2 %collective-permute-start.26 = (bf16[896,1280]{1,0:T(8,128)(2,1)}, bf16[896,1280]{1,0:T(8,128)(2,1)}, u32[]{:S(2)}, u32[]{:S(2)}) collective-permute-start(bf16[896,1280]{1,0:T(8,128)(2,1)} %collective-permute-done.25), channel_id=1, source_target_pairs={{4,3},{5,2},{6,1},{7,0}} | collective-permute-start | bytes 6881288 | tf_op jit(solution)/shard_map/ppermute | solution.py:160
  484.5 8.8 %shard_map.101 = bf16[320,5120]{1,0:T(8,128)(2,1)S(1)} custom-call(s32[1]{0:T(128)} %bitcast.22.refs_0_, bf16[320,512]{1,0:T(8,128)(2,1)S(1)} %bitcast.96, bf16[320,512]{1,0:T(8,128)(2,1)S(1)} %bitcast.97, bf16[512,5120]{1,0:T(8,128)(2,1)} %get-tuple-element.30.refs_3_, bf16[512,5120]{1,0:T(8,128)(2,1)} %get-tuple-element.33.refs_4_, f32[2,1280,5120]{2,1,0:T(8,128)} %bitcast.155), custom_call_target="tpu_custom_call" | custom-call | flops 3355443200 | bytes 9830400 | tf_op jit(solution)/shard_map/pallas_call | solution.py:110
  497.3 3.1 collective-permute-start.8
  500.4 8.9 %shard_map.100 = bf16[320,5120]{1,0:T(8,128)(2,1)S(1)} custom-call(s32[1]{0:T(128)} %bitcast.17.refs_0_, bf16[320,512]{1,0:T(8,128)(2,1)S(1)} %bitcast.98, bf16[320,512]{1,0:T(8,128)(2,1)S(1)} %bitcast.99, bf16[512,5120]{1,0:T(8,128)(2,1)} %get-tuple-element.30.refs_3_, bf16[512,5120]{1,0:T(8,128)(2,1)} %get-tuple-element.33.refs_4_, f32[2,1280,5120]{2,1,0:T(8,128)} %bitcast.156), custom_call_target="tpu_custom_call" | custom-call | flops 3355443200 | bytes 9830400 | tf_op jit(solution)/shard_map/pallas_call | solution.py:110
  515.9 7.6 %shard_map.115.refs_0_ = bf16[1280,1280]{1,0:T(8,128)(2,1)S(1)} custom-call(s32[3]{0:T(128)S(1)} %pad_add_fusion.5.refs_0_, bf16[2,2,512,5120]{3,2,1,0:T(8,128)(2,1)} %bitcast.131, bf16[2,2,512,5120]{3,2,1,0:T(8,128)(2,1)} %bitcast.132, bf16[512,1280]{1,0:T(8,128)(2,1)S(1)} %bitcast.88, bf16[512,1280]{1,0:T(8,128)(2,1)} %collective-permute-done.g_ref.refs_4_, ...), custom_call_target="tpu_custom_call" | custom-call | flops 3355443200 | bytes 9830400 | tf_op jit(solution)/shard_map/pallas_call | solution.py:83
  528.9 10.6 %shard_map.99 = bf16[320,5120]{1,0:T(8,128)(2,1)} custom-call(s32[1]{0:T(128)} %bitcast.12.refs_0_, bf16[320,512]{1,0:T(8,128)(2,1)S(1)} %bitcast.94, bf16[320,512]{1,0:T(8,128)(2,1)S(1)} %bitcast.95, bf16[512,5120]{1,0:T(8,128)(2,1)} %get-tuple-element.30.refs_3_, bf16[512,5120]{1,0:T(8,128)(2,1)} %get-tuple-element.33.refs_4_, f32[2,1280,5120]{2,1,0:T(8,128)} %bitcast.157), custom_call_target="tpu_custom_call" | custom-call | flops 3355443200 | bytes 9830400 | tf_op jit(solution)/shard_map/pallas_call | solution.py:110
  539.6 7.0 shard_map.110.refs_0_
  549.1 8.8 %shard_map.102.refs_0_ = bf16[320,5120]{1,0:T(8,128)(2,1)S(1)} custom-call(s32[1]{0:T(128)} %bitcast.refs_0_, bf16[320,512]{1,0:T(8,128)(2,1)S(1)} %bitcast.101, bf16[320,512]{1,0:T(8,128)(2,1)S(1)} %bitcast.102, bf16[512,5120]{1,0:T(8,128)(2,1)} %get-tuple-element.38.refs_3_.refs_2_, bf16[512,5120]{1,0:T(8,128)(2,1)} %get-tuple-element.39.refs_4_, ...), custom_call_target="tpu_custom_call" | custom-call | flops 3355443200 | bytes 9830400 | tf_op jit(solution)/shard_map/pallas_call | solution.py:110
  558.0 3.7 pad_maximum_fusion.1.refs_4_
  563.0 3.5 pad_maximum_fusion.refs_5_
  566.5 3.9 pad_maximum_fusion.2.refs_5_
  570.4 11.0 %shard_map.124.refs_5_ = f32[2,1280,1280]{2,1,0:T(8,128)} custom-call(bf16[1280,1280]{1,0:T(8,128)(2,1)} %copy-done.10, bf16[1280,1280]{1,0:T(8,128)(2,1)} %collective-permute-done.16.refs_1_, bf16[1280,1280]{1,0:T(8,128)(2,1)} %collective-permute-done.17.refs_2_, bf16[1280,1280]{1,0:T(8,128)(2,1)} %collective-permute-done.18.refs_3_, ...), custom_call_target="tpu_custom_call" | custom-call | flops 9830400 | bytes 26214400 | tf_op jit(solution)/shard_map/pallas_call | solution.py:144
  581.4 10.1 %shard_map.125 = f32[2,1280,1280]{2,1,0:T(8,128)} custom-call(bf16[1280,1280]{1,0:T(8,128)(2,1)} %copy-done.11, bf16[1280,1280]{1,0:T(8,128)(2,1)} %collective-permute-done.12.refs_1_, bf16[1280,1280]{1,0:T(8,128)(2,1)} %collective-permute-done.13.refs_2_, bf16[1280,1280]{1,0:T(8,128)(2,1)} %collective-permute-done.14.refs_3_, ...), custom_call_target="tpu_custom_call", output_to_operand_aliasing={{}: (5, {})} | custom-call | flops 8192000 | bytes 22937600 | tf_op jit(solution)/shard_map/pallas_call | solution.py:144
  591.6 9.5 %collective-permute-done.8.refs_4_ = bf16[320,5120]{1,0:T(8,128)(2,1)} collective-permute-done((bf16[320,5120]{1,0:T(8,128)(2,1)}, bf16[320,5120]{1,0:T(8,128)(2,1)}, u32[]{:S(2)}, u32[]{:S(2)}) %collective-permute-start.8) | collective-permute-done | bytes 3276832 | tf_op jit(solution)/shard_map/ppermute | solution.py:160
  601.0 11.0 %shard_map.109.refs_4_ = f32[2,320,5120]{2,1,0:T(8,128)} custom-call(bf16[320,5120]{1,0:T(8,128)(2,1)} %copy-done.12, bf16[320,5120]{1,0:T(8,128)(2,1)} %collective-permute-done.4.refs_1_, bf16[320,5120]{1,0:T(8,128)(2,1)} %collective-permute-done.5.refs_2_, bf16[320,5120]{1,0:T(8,128)(2,1)} %collective-permute-done.6.refs_3_, ...), custom_call_target="tpu_custom_call" | custom-call | flops 9830400 | bytes 26214400 | tf_op jit(solution)/shard_map/pallas_call | solution.py:144
  612.1 50.0 %collective-permute-done.2.refs_2_ = bf16[256,5120]{1,0:T(8,128)(2,1)} collective-permute-done((bf16[256,5120]{1,0:T(8,128)(2,1)}, bf16[256,5120]{1,0:T(8,128)(2,1)}, u32[]{:S(2)}, u32[]{:S(2)}) %collective-permute-start.2) | collective-permute-done | bytes 2621472 | tf_op jit(solution)/shard_map/ppermute | solution.py:160
  662.0 55.0 %collective-permute-done.3.refs_3_ = bf16[256,5120]{1,0:T(8,128)(2,1)} collective-permute-done((bf16[256,5120]{1,0:T(8,128)(2,1)}, bf16[256,5120]{1,0:T(8,128)(2,1)}, u32[]{:S(2)}, u32[]{:S(2)}) %collective-permute-start.3) | collective-permute-done | bytes 2621472 | tf_op jit(solution)/shard_map/ppermute | solution.py:160
  719.8 8.8 %shard_map.98.refs_0_ = bf16[320,5120]{1,0:T(8,128)(2,1)S(1)} custom-call(s32[1]{0:T(128)} %bitcast.refs_0_, bf16[320,512]{1,0:T(8,128)(2,1)S(1)} %bitcast.92, bf16[320,512]{1,0:T(8,128)(2,1)S(1)} %bitcast.91, bf16[512,5120]{1,0:T(8,128)(2,1)} %get-tuple-element.30.refs_3_, bf16[512,5120]{1,0:T(8,128)(2,1)} %get-tuple-element.33.refs_4_, ...), custom_call_target="tpu_custom_call" | custom-call | flops 3355443200 | bytes 9830400 | tf_op jit(solution)/shard_map/pallas_call | solution.py:110
  730.3 2.5 select_bitcast_fusion
  732.8 8.6 %shard_map.126.refs_4_ = f32[2,320,5120]{2,1,0:T(8,128)} custom-call(bf16[320,5120]{1,0:T(8,128)(2,1)} %copy-done.7, bf16[320,5120]{1,0:T(8,128)(2,1)} %collective-permute-done.1.refs_1_, bf16[256,5120]{1,0:T(8,128)(2,1)} %collective-permute-done.2.refs_2_, bf16[256,5120]{1,0:T(8,128)(2,1)} %collective-permute-done.3.refs_3_, ...), custom_call_target="tpu_custom_call", output_to_operand_aliasing={{}: (4, {})} | custom-call | flops 5242880 | bytes 15728640 | tf_op jit(solution)/shard_map/pallas_call | solution.py:144
  741.4 6.4 collective-permute-done.29.refs_3_
  747.8 3.9 shard_map.127
  (129 shorter events, 60.1 us)
Async XLA Ops:
  0.6 1.3 copy-start
  24.7 25.8 %copy-start.1 = (bf16[1,512,1280]{2,1,0:T(8,128)(2,1)S(1)}, bf16[1,512,1280]{2,1,0:T(8,128)(2,1)}, u32[]{:S(2)}) copy-start(bf16[1,512,1280]{2,1,0:T(8,128)(2,1)} %param.7) | copy-start | bytes 3932164
  48.0 75.1 %collective-permute-start = (bf16[512,1280]{1,0:T(8,128)(2,1)}, bf16[512,1280]{1,0:T(8,128)(2,1)}, u32[]{:S(2)}, u32[]{:S(2)}) collective-permute-start(bf16[512,1280]{1,0:T(8,128)(2,1)} %get-tuple-element.27), channel_id=1, source_target_pairs={{4,0},{5,1},{6,2},{7,3}} | collective-permute-start | bytes 3932168 | tf_op jit(solution)/shard_map/ppermute | solution.py:212
  54.8 76.6 %collective-permute-start.21 = (bf16[512,1280]{1,0:T(8,128)(2,1)}, bf16[512,1280]{1,0:T(8,128)(2,1)}, u32[]{:S(2)}, u32[]{:S(2)}) collective-permute-start(bf16[512,1280]{1,0:T(8,128)(2,1)} %shard_map.120), channel_id=1, source_target_pairs={{4,0},{5,1},{6,2},{7,3}} | collective-permute-start | bytes 3932168 | tf_op jit(solution)/shard_map/ppermute | solution.py:160
  60.7 59.0 %collective-permute-start.19 = (bf16[256,1280]{1,0:T(8,128)(2,1)}, bf16[256,1280]{1,0:T(8,128)(2,1)}, u32[]{:S(2)}, u32[]{:S(2)}) collective-permute-start(bf16[256,1280]{1,0:T(8,128)(2,1)} %shard_map.119), channel_id=1, source_target_pairs={{4,0},{5,1},{6,2},{7,3}} | collective-permute-start | bytes 1966088 | tf_op jit(solution)/shard_map/ppermute | solution.py:160
  67.1 80.6 %collective-permute-start.23 = (bf16[512,1280]{1,0:T(8,128)(2,1)}, bf16[512,1280]{1,0:T(8,128)(2,1)}, u32[]{:S(2)}, u32[]{:S(2)}) collective-permute-start(bf16[512,1280]{1,0:T(8,128)(2,1)} %shard_map.121), channel_id=1, source_target_pairs={{4,0},{5,1},{6,2},{7,3}} | collective-permute-start | bytes 3932168 | tf_op jit(solution)/shard_map/ppermute | solution.py:160
  74.7 101.1 %collective-permute-start.10 = (bf16[320,2048]{1,0:T(8,128)(2,1)}, bf16[320,2048]{1,0:T(8,128)(2,1)}, u32[]{:S(2)}, u32[]{:S(2)}) collective-permute-start(bf16[320,2048]{1,0:T(8,128)(2,1)} %shard_map.108), channel_id=1, source_target_pairs={{4,0},{5,1},{6,2},{7,3}} | collective-permute-start | bytes 3932168 | tf_op jit(solution)/shard_map/ppermute | solution.py:160
  119.6 76.6 %collective-permute-start.9 = (bf16[320,3072]{1,0:T(8,128)(2,1)}, bf16[320,3072]{1,0:T(8,128)(2,1)}, u32[]{:S(2)}, u32[]{:S(2)}) collective-permute-start(bf16[320,3072]{1,0:T(8,128)(2,1)} %shard_map.107), channel_id=1, source_target_pairs={{4,6},{5,7},{6,4},{7,5}} | collective-permute-start | bytes 5898248 | tf_op jit(solution)/shard_map/ppermute | solution.py:160
  123.1 33.7 %collective-permute-start.20 = (bf16[256,1280]{1,0:T(8,128)(2,1)}, bf16[256,1280]{1,0:T(8,128)(2,1)S(1)}, u32[]{:S(2)}, u32[]{:S(2)}) collective-permute-start(bf16[256,1280]{1,0:T(8,128)(2,1)} %collective-permute-done.19), channel_id=1, source_target_pairs={{0,7},{1,6},{2,5},{3,4}} | collective-permute-start | bytes 1966088 | tf_op jit(solution)/shard_map/ppermute | solution.py:160
  131.4 148.1 %collective-permute-start.17 = (bf16[1280,1280]{1,0:T(8,128)(2,1)}, bf16[1280,1280]{1,0:T(8,128)(2,1)}, u32[]{:S(2)}, u32[]{:S(2)}) collective-permute-start(bf16[1280,1280]{1,0:T(8,128)(2,1)} %shard_map.117), channel_id=1, source_target_pairs={{4,6},{5,7},{6,4},{7,5}} | collective-permute-start | bytes 9830408 | tf_op jit(solution)/shard_map/ppermute | solution.py:160
  147.7 156.7 %collective-permute-start.13 = (bf16[1280,1280]{1,0:T(8,128)(2,1)}, bf16[1280,1280]{1,0:T(8,128)(2,1)}, u32[]{:S(2)}, u32[]{:S(2)}) collective-permute-start(bf16[1280,1280]{1,0:T(8,128)(2,1)} %shard_map.112), channel_id=1, source_target_pairs={{4,6},{5,7},{6,4},{7,5}} | collective-permute-start | bytes 9830408 | tf_op jit(solution)/shard_map/ppermute | solution.py:160
  156.9 18.9 %copy-start.26 = (bf16[256,1280]{1,0:T(8,128)(2,1)}, bf16[256,1280]{1,0:T(8,128)(2,1)S(1)}, u32[]{:S(2)}) copy-start(bf16[256,1280]{1,0:T(8,128)(2,1)S(1)} %collective-permute-done.20) | copy-start | bytes 1966084
  156.9 40.6 %collective-permute-start.27 = (bf16[384,1280]{1,0:T(8,128)(2,1)}, bf16[384,1280]{1,0:T(8,128)(2,1)}, u32[]{:S(2)}, u32[]{:S(2)}) collective-permute-start(bf16[384,1280]{1,0:T(8,128)(2,1)} %shard_map.123), channel_id=1, source_target_pairs={{0,3},{1,2},{2,1},{3,0}} | collective-permute-start | bytes 2949128 | tf_op jit(solution)/shard_map/ppermute | solution.py:160
  175.8 38.8 %collective-permute-start.22 = (bf16[512,1280]{1,0:T(8,128)(2,1)}, bf16[512,1280]{1,0:T(8,128)(2,1)}, u32[]{:S(2)}, u32[]{:S(2)}) collective-permute-start(bf16[512,1280]{1,0:T(8,128)(2,1)} %collective-permute-done.21), channel_id=1, source_target_pairs={{0,7},{1,6},{2,5},{3,4}} | collective-permute-start | bytes 3932168 | tf_op jit(solution)/shard_map/ppermute | solution.py:160
  196.2 46.3 %collective-permute-start.24 = (bf16[512,1280]{1,0:T(8,128)(2,1)}, bf16[512,1280]{1,0:T(8,128)(2,1)S(1)}, u32[]{:S(2)}, u32[]{:S(2)}) collective-permute-start(bf16[512,1280]{1,0:T(8,128)(2,1)} %collective-permute-done.23), channel_id=1, source_target_pairs={{0,7},{1,6},{2,5},{3,4}} | collective-permute-start | bytes 3932168 | tf_op jit(solution)/shard_map/ppermute | solution.py:160
  197.5 71.0 %collective-permute-start.11 = (bf16[320,2048]{1,0:T(8,128)(2,1)}, bf16[320,2048]{1,0:T(8,128)(2,1)S(1)}, u32[]{:S(2)}, u32[]{:S(2)}) collective-permute-start(bf16[320,2048]{1,0:T(8,128)(2,1)} %collective-permute-done.10), channel_id=1, source_target_pairs={{0,6},{1,7},{2,4},{3,5}} | collective-permute-start | bytes 3932168 | tf_op jit(solution)/shard_map/ppermute | solution.py:160
  214.6 165.7 %collective-permute-start.5 = (bf16[320,5120]{1,0:T(8,128)(2,1)}, bf16[320,5120]{1,0:T(8,128)(2,1)}, u32[]{:S(2)}, u32[]{:S(2)}) collective-permute-start(bf16[320,5120]{1,0:T(8,128)(2,1)} %shard_map.104), channel_id=1, source_target_pairs={{4,7},{5,6},{6,5},{7,4}} | collective-permute-start | bytes 9830408 | tf_op jit(solution)/shard_map/ppermute | solution.py:160
  241.9 37.6 %copy-start.2 = (bf16[512,1280]{1,0:T(8,128)(2,1)}, bf16[512,1280]{1,0:T(8,128)(2,1)S(1)}, u32[]{:S(2)}) copy-start(bf16[512,1280]{1,0:T(8,128)(2,1)S(1)} %get-tuple-element.32.g_ref.refs_4_) | copy-start | bytes 3932164
  242.4 37.1 %copy-start.24 = (bf16[512,1280]{1,0:T(8,128)(2,1)}, bf16[512,1280]{1,0:T(8,128)(2,1)S(1)}, u32[]{:S(2)}) copy-start(bf16[512,1280]{1,0:T(8,128)(2,1)S(1)} %collective-permute-done.24) | copy-start | bytes 3932164
  242.4 188.0 %collective-permute-start.18 = (bf16[1280,1280]{1,0:T(8,128)(2,1)}, bf16[1280,1280]{1,0:T(8,128)(2,1)}, u32[]{:S(2)}, u32[]{:S(2)}) collective-permute-start(bf16[1280,1280]{1,0:T(8,128)(2,1)} %shard_map.118), channel_id=1, source_target_pairs={{0,2},{1,3},{2,0},{3,1}} | collective-permute-start | bytes 9830408 | tf_op jit(solution)/shard_map/ppermute | solution.py:160
  268.5 11.0 %copy-start.22 = (bf16[320,2048]{1,0:T(8,128)(2,1)}, bf16[320,2048]{1,0:T(8,128)(2,1)S(1)}, u32[]{:S(2)}) copy-start(bf16[320,2048]{1,0:T(8,128)(2,1)S(1)} %collective-permute-done.11) | copy-start | bytes 3932164
  268.5 163.1 %collective-permute-start.16 = (bf16[1280,1280]{1,0:T(8,128)(2,1)}, bf16[1280,1280]{1,0:T(8,128)(2,1)}, u32[]{:S(2)}, u32[]{:S(2)}) collective-permute-start(bf16[1280,1280]{1,0:T(8,128)(2,1)} %shard_map.116), channel_id=1, source_target_pairs={{0,1},{1,0},{2,3},{3,2},{4,5},{5,4},{6,7},{7,6}} | collective-permute-start | bytes 9830408 | tf_op jit(solution)/shard_map/ppermute | solution.py:160
  279.5 168.1 %collective-permute-start.15 = (bf16[1280,1280]{1,0:T(8,128)(2,1)}, bf16[1280,1280]{1,0:T(8,128)(2,1)}, u32[]{:S(2)}, u32[]{:S(2)}) collective-permute-start(bf16[1280,1280]{1,0:T(8,128)(2,1)} %shard_map.114), channel_id=1, source_target_pairs={{0,3},{1,2},{2,1},{3,0},{4,7},{5,6},{6,5},{7,4}} | collective-permute-start | bytes 9830408 | tf_op jit(solution)/shard_map/ppermute | solution.py:160
  304.4 100.2 %collective-permute-start.25 = (bf16[896,1280]{1,0:T(8,128)(2,1)}, bf16[896,1280]{1,0:T(8,128)(2,1)}, u32[]{:S(2)}, u32[]{:S(2)}) collective-permute-start(bf16[896,1280]{1,0:T(8,128)(2,1)} %shard_map.122), channel_id=1, source_target_pairs={{0,4},{1,5},{2,6},{3,7}} | collective-permute-start | bytes 6881288 | tf_op jit(solution)/shard_map/ppermute | solution.py:160
  305.7 1.3 copy-start.3
  380.3 95.0 %collective-permute-start.14 = (bf16[1280,1280]{1,0:T(8,128)(2,1)}, bf16[1280,1280]{1,0:T(8,128)(2,1)}, u32[]{:S(2)}, u32[]{:S(2)}) collective-permute-start(bf16[1280,1280]{1,0:T(8,128)(2,1)} %shard_map.113), channel_id=1, source_target_pairs={{0,2},{1,3},{2,0},{3,1}} | collective-permute-start | bytes 9830408 | tf_op jit(solution)/shard_map/ppermute | solution.py:160
  404.6 92.7 %collective-permute-start.7 = (bf16[320,5120]{1,0:T(8,128)(2,1)}, bf16[320,5120]{1,0:T(8,128)(2,1)}, u32[]{:S(2)}, u32[]{:S(2)}) collective-permute-start(bf16[320,5120]{1,0:T(8,128)(2,1)} %shard_map.106), channel_id=1, source_target_pairs={{0,4},{1,5},{2,6},{3,7}} | collective-permute-start | bytes 9830408 | tf_op jit(solution)/shard_map/ppermute | solution.py:160
  410.5 1.3 copy-start.4
  411.8 8.2 %copy-start.14 = (bf16[1,1,512,320]{2,3,1,0:T(8,128)(2,1)S(1)}, bf16[1,1,512,320]{2,3,1,0:T(8,128)(2,1)}, u32[]{:S(2)}) copy-start(bf16[1,1,512,320]{2,3,1,0:T(8,128)(2,1)} %copy.27) | copy-start | bytes 983044
  428.7 1.7 copy-start.13
  430.4 94.8 %collective-permute-start.12 = (bf16[1280,1280]{1,0:T(8,128)(2,1)}, bf16[1280,1280]{1,0:T(8,128)(2,1)}, u32[]{:S(2)}, u32[]{:S(2)}) collective-permute-start(bf16[1280,1280]{1,0:T(8,128)(2,1)} %shard_map.111), channel_id=1, source_target_pairs={{0,1},{1,0},{2,3},{3,2},{4,5},{5,4},{6,7},{7,6}} | collective-permute-start | bytes 9830408 | tf_op jit(solution)/shard_map/ppermute | solution.py:160
  431.6 95.9 %collective-permute-start.6 = (bf16[320,5120]{1,0:T(8,128)(2,1)}, bf16[320,5120]{1,0:T(8,128)(2,1)}, u32[]{:S(2)}, u32[]{:S(2)}) collective-permute-start(bf16[320,5120]{1,0:T(8,128)(2,1)} %copy-done.13), channel_id=1, source_target_pairs={{0,2},{1,3},{2,0},{3,1}} | collective-permute-start | bytes 9830408 | tf_op jit(solution)/shard_map/ppermute | solution.py:160
  447.7 91.8 %collective-permute-start.4 = (bf16[320,5120]{1,0:T(8,128)(2,1)}, bf16[320,5120]{1,0:T(8,128)(2,1)}, u32[]{:S(2)}, u32[]{:S(2)}) collective-permute-start(bf16[320,5120]{1,0:T(8,128)(2,1)} %shard_map.103), channel_id=1, source_target_pairs={{0,1},{1,0},{2,3},{3,2},{4,5},{5,4},{6,7},{7,6}} | collective-permute-start | bytes 9830408 | tf_op jit(solution)/shard_map/ppermute | solution.py:160
  450.1 1.3 copy-start.5
  474.2 1.1 copy-start.15
  475.3 86.4 %collective-permute-start.26 = (bf16[896,1280]{1,0:T(8,128)(2,1)}, bf16[896,1280]{1,0:T(8,128)(2,1)}, u32[]{:S(2)}, u32[]{:S(2)}) collective-permute-start(bf16[896,1280]{1,0:T(8,128)(2,1)} %collective-permute-done.25), channel_id=1, source_target_pairs={{4,3},{5,2},{6,1},{7,0}} | collective-permute-start | bytes 6881288 | tf_op jit(solution)/shard_map/ppermute | solution.py:160
  493.3 1.7 copy-start.8
  497.3 103.8 %collective-permute-start.8 = (bf16[320,5120]{1,0:T(8,128)(2,1)}, bf16[320,5120]{1,0:T(8,128)(2,1)}, u32[]{:S(2)}, u32[]{:S(2)}) collective-permute-start(bf16[320,5120]{1,0:T(8,128)(2,1)} %collective-permute-done.7), channel_id=1, source_target_pairs={{4,3},{5,2},{6,1},{7,0}} | collective-permute-start | bytes 9830408 | tf_op jit(solution)/shard_map/ppermute | solution.py:160
  500.4 9.0 %copy-start.9 = (bf16[320,5120]{1,0:T(8,128)(2,1)S(1)}, bf16[320,5120]{1,0:T(8,128)(2,1)}, u32[]{:S(2)}) copy-start(bf16[320,5120]{1,0:T(8,128)(2,1)} %copy-done.8) | copy-start | bytes 9830404
  512.0 2.6 copy-start.21
  523.6 1.7 copy-start.10
  525.3 136.8 %collective-permute-start.2 = (bf16[256,5120]{1,0:T(8,128)(2,1)}, bf16[256,5120]{1,0:T(8,128)(2,1)}, u32[]{:S(2)}, u32[]{:S(2)}) collective-permute-start(bf16[256,5120]{1,0:T(8,128)(2,1)} %slice.16), channel_id=1, source_target_pairs={{0,2},{1,3},{2,0},{3,1},{4,6},{5,7},{6,4},{7,5}} | collective-permute-start | bytes 7864328 | tf_op jit(solution)/shard_map/ppermute | solution.py:160
  527.5 189.5 %collective-permute-start.3 = (bf16[256,5120]{1,0:T(8,128)(2,1)}, bf16[256,5120]{1,0:T(8,128)(2,1)}, u32[]{:S(2)}, u32[]{:S(2)}) collective-permute-start(bf16[256,5120]{1,0:T(8,128)(2,1)} %slice.18), channel_id=1, source_target_pairs={{0,3},{1,2},{2,1},{3,0},{4,7},{5,6},{6,5},{7,4}} | collective-permute-start | bytes 7864328 | tf_op jit(solution)/shard_map/ppermute | solution.py:160
  528.9 10.6 %copy-start.6 = (bf16[512,1280]{1,0:T(8,128)(2,1)S(1)}, bf16[512,1280]{1,0:T(8,128)(2,1)}, u32[]{:S(2)}) copy-start(bf16[512,1280]{1,0:T(8,128)(2,1)} %copy-done.2) | copy-start | bytes 3932164
  539.5 8.8 %copy-start.20 = (bf16[1,1,512,320]{3,2,1,0:T(8,128)(2,1)S(1)}, bf16[1,1,512,320]{3,2,1,0:T(8,128)(2,1)}, u32[]{:S(2)}) copy-start(bf16[1,1,512,320]{3,2,1,0:T(8,128)(2,1)} %get-tuple-element.54) | copy-start | bytes 983044
  539.5 9.0 %copy-start.19 = (bf16[1,1,512,320]{3,2,1,0:T(8,128)(2,1)S(1)}, bf16[1,1,512,320]{3,2,1,0:T(8,128)(2,1)}, u32[]{:S(2)}) copy-start(bf16[1,1,512,320]{3,2,1,0:T(8,128)(2,1)} %get-tuple-element.53) | copy-start | bytes 983044
  539.5 9.2 %copy-start.18 = (bf16[1,1,512,320]{3,2,1,0:T(8,128)(2,1)S(1)}, bf16[1,1,512,320]{3,2,1,0:T(8,128)(2,1)}, u32[]{:S(2)}) copy-start(bf16[1,1,512,320]{3,2,1,0:T(8,128)(2,1)} %get-tuple-element.61) | copy-start | bytes 983044
  539.5 9.4 %copy-start.17 = (bf16[1,1,512,320]{3,2,1,0:T(8,128)(2,1)S(1)}, bf16[1,1,512,320]{3,2,1,0:T(8,128)(2,1)}, u32[]{:S(2)}) copy-start(bf16[1,1,512,320]{3,2,1,0:T(8,128)(2,1)} %get-tuple-element.62) | copy-start | bytes 983044
  539.5 193.3 %collective-permute-start.1 = (bf16[320,5120]{1,0:T(8,128)(2,1)}, bf16[320,5120]{1,0:T(8,128)(2,1)}, u32[]{:S(2)}, u32[]{:S(2)}) collective-permute-start(bf16[320,5120]{1,0:T(8,128)(2,1)} %shard_map.99), channel_id=1, source_target_pairs={{0,1},{1,0},{2,3},{3,2},{4,5},{5,4},{6,7},{7,6}} | collective-permute-start | bytes 9830408 | tf_op jit(solution)/shard_map/ppermute | solution.py:160
  546.6 1.7 copy-start.11
  549.1 8.9 %copy-start.25 = (bf16[512,1280]{1,0:T(8,128)(2,1)S(1)}, bf16[512,1280]{1,0:T(8,128)(2,1)}, u32[]{:S(2)}) copy-start(bf16[512,1280]{1,0:T(8,128)(2,1)} %copy-done.24) | copy-start | bytes 3932164
  549.1 8.9 %copy-start.27 = (bf16[256,1280]{1,0:T(8,128)(2,1)S(1)}, bf16[256,1280]{1,0:T(8,128)(2,1)}, u32[]{:S(2)}) copy-start(bf16[256,1280]{1,0:T(8,128)(2,1)} %copy-done.26) | copy-start | bytes 1966084
  557.9 8.5 %copy-start.12 = (bf16[320,5120]{1,0:T(8,128)(2,1)}, bf16[320,5120]{1,0:T(8,128)(2,1)S(1)}, u32[]{:S(2)}) copy-start(bf16[320,5120]{1,0:T(8,128)(2,1)S(1)} %shard_map.102.refs_0_) | copy-start | bytes 9830404
  558.0 5.0 copy-start.23
  561.7 168.6 %collective-permute-start.30 = (bf16[512,1280]{1,0:T(8,128)(2,1)}, bf16[512,1280]{1,0:T(8,128)(2,1)}, u32[]{:S(2)}, u32[]{:S(2)}) collective-permute-start(bf16[512,1280]{1,0:T(8,128)(2,1)} %get-tuple-element.27), channel_id=1, source_target_pairs={{0,4},{1,5},{2,6},{3,7}} | collective-permute-start | bytes 3932168 | tf_op jit(solution)/shard_map/ppermute | solution.py:223
  591.6 125.9 %copy-start.28 = (bf16[64,5120]{1,0:T(8,128)(2,1)S(1)}, bf16[64,5120]{1,0:T(8,128)(2,1)}, u32[]{:S(2)}) copy-start(bf16[64,5120]{1,0:T(8,128)(2,1)} %slice.19) | copy-start | bytes 1966084
  717.0 24.4 %collective-permute-start.28 = (bf16[64,5120]{1,0:T(8,128)(2,1)}, bf16[64,5120]{1,0:T(8,128)(2,1)}, u32[]{:S(2)}, u32[]{:S(2)}) collective-permute-start(bf16[64,5120]{1,0:T(8,128)(2,1)} %slice.17), channel_id=1, source_target_pairs={{0,2},{1,3},{2,0},{3,1},{4,6},{5,7},{6,4},{7,5}} | collective-permute-start | bytes 1966088 | tf_op jit(solution)/shard_map/ppermute | solution.py:160
  717.5 30.3 %collective-permute-start.29 = (bf16[64,5120]{1,0:T(8,128)(2,1)S(1)}, bf16[64,5120]{1,0:T(8,128)(2,1)}, u32[]{:S(2)}, u32[]{:S(2)}) collective-permute-start(bf16[64,5120]{1,0:T(8,128)(2,1)S(1)} %copy-done.28), channel_id=1, source_target_pairs={{0,3},{1,2},{2,1},{3,0},{4,7},{5,6},{6,5},{7,4}} | collective-permute-start | bytes 1966088 | tf_op jit(solution)/shard_map/ppermute | solution.py:160
  719.8 10.5 %copy-start.16 = (bf16[512,1280]{1,0:T(8,128)(2,1)S(1)}, bf16[512,1280]{1,0:T(8,128)(2,1)}, u32[]{:S(2)}) copy-start(bf16[512,1280]{1,0:T(8,128)(2,1)} %copy-done.15) | copy-start | bytes 3932164
  728.6 1.7 copy-start.7

commit v3 on v2

--- a/solution.py
+++ b/solution.py
@@ -67,14 +67,22 @@
 
 def grad2(at, slots, acc, k, hs, kb, cots, count, bm=256):
     n = len(cots)
+    sub = 256 if n == 1 and bm % 256 == 0 else 128
+    assert bm % sub == 0 and count % bm == 0
     toks, cols = cots[0].shape
 
     def kern(*refs):
         acc_ref, o_ref = refs[1 + 2 * n], refs[2 + 2 * n]
-        total = acc_ref[0]
-        for i in range(n):
-            total = total + tn(gelu_tile(refs[1 + i][0, 0]), refs[1 + n + i][...])
-        o_ref[...] = total.astype(jnp.bfloat16)
+
+        def part(j, _):
+            at = pl.ds(pl.multiple_of(j * sub, sub), sub)
+            total = acc_ref[0, at]
+            for i in range(n):
+                total = total + tn(gelu_tile(refs[1 + i][0, 0, :, at]), refs[1 + n + i][...])
+            o_ref[at] = total.astype(jnp.bfloat16)
+            return 0
+
+        lax.fori_loop(0, bm // sub, part, 0)
 
     def hspec(j):
         return pl.BlockSpec((1, 1, toks, bm), lambda i, p: (p[1 + j], kb, 0, p[0] + i))
@@ -96,16 +104,24 @@
 def grad1(q, acc, k, lhs, dhs, first=0, count=None):
     bn = 1024
     n = len(lhs)
+    sub = 256 if n == 1 else 128
     rows, toks = lhs[0].shape
     cols = count or dhs[0].shape[1]
+    assert cols % bn == 0 and bn % sub == 0 and first % bn == 0
     b0 = first // bn
 
     def kern(*refs):
         acc_ref, o_ref = refs[1 + 2 * n], refs[2 + 2 * n]
-        total = acc_ref[0]
-        for i in range(n):
-            total = total + jnp.dot(refs[1 + i][...], refs[1 + n + i][...], preferred_element_type=jnp.float32)
-        o_ref[...] = total.astype(jnp.bfloat16)
+
+        def part(j, _):
+            at = pl.ds(pl.multiple_of(j * sub, sub), sub)
+            total = acc_ref[0, :, at]
+            for i in range(n):
+                total = total + jnp.dot(refs[1 + i][...], refs[1 + n + i][:, at], preferred_element_type=jnp.float32)
+            o_ref[:, at] = total.astype(jnp.bfloat16)
+            return 0
+
+        lax.fori_loop(0, bn // sub, part, 0)
 
     return pl.pallas_call(
         kern,
@@ -126,10 +142,15 @@
     steps = count // br
 
     def kern(*refs):
-        total = refs[0][...].astype(jnp.float32)
-        for r in refs[1:n]:
-            total = total + r[...].astype(jnp.float32)
-        refs[-1][0] = total * scale
+        def some(j, _):
+            at = pl.ds(pl.multiple_of(j * 16, 16), 16)
+            total = refs[0][at].astype(jnp.float32)
+            for r in refs[1:n]:
+                total = total + r[at].astype(jnp.float32)
+            refs[-1][0, at] = total * scale
+            return 0
+
+        lax.fori_loop(0, br // 16, some, 0)
 
     def block(off):
         return pl.BlockSpec((br, cols), lambda i: (off // br + i, 0))
@@ -182,7 +203,7 @@
             return grad1(d ^ off, acc1, k, [rows_of(i, k, off, xlate) for i in range(2)], [da[k], db[k]])
 
         def back(g, i, k):
-            return layer(slot[i], g, hs, w2, w1, k)
+            return layer(slot[i], g, hs, w2, w1, k, 512)
 
         ga, gb, da, db = {1: dy[0]}, {}, {}, {}
         stay, down, rise = [(0, 0), (1, 1)], [(1, 0)], [(0, 1)]
@@ -255,7 +276,7 @@
         o2 = reduce_into(o2, base(0, 2) + far02, 0, sh2, sc, n2 // 5, 0, n2)
         far012a, far013a, p012b, p013b, o1, o2 = lax.optimization_barrier((far012a, far013a, p012b, p013b, o1, o2))
         far012b, far013b = hop(p012b, stay, 2), hop(p013b, stay, 3)
-        o1 = reduce_into(o1, base(0, 1) + [(far012a, 0), (far013a, 0)], 0, sh1, sc, cut // 8, 0, cut)
+        o1 = reduce_into(o1, base(0, 1) + [(far012a, 0), (far013a, 0)], 0, sh1, sc, cut // 4, 0, cut)
         o1 = reduce_into(o1, base(0, 1, cut) + [(far012b, 0), (far013b, 0)], 0, sh1, sc, 16, cut, n1 - cut)
         return o1[None], o2[None], dx[None]
 

time: 762 us -> 777 us (1.020); the launches traced: 752 us -> 775 us
  Pallas kernels: 328 us -> 410 us
  waiting for transfers between devices: 297 us -> 241 us
    pallas_call x11, Pallas kernels: 93.5 us -> 154 us  [grad1(): pl.pallas_call(kern, grid_spec=pltpu.PrefetchScalarGridSpec(num_scalar_pr...]
    ppermute x29, waiting for transfers between devices: 297 us -> 241 us  [hop(): lax.ppermute(p, both, [(a * ndp + i, b * ndp + (i ^ off)) for a, b in rou...]
    pallas_call x14, Pallas kernels: 97.3 us -> 114 us  [grad2(): pl.pallas_call(kern, grid_spec=pltpu.PrefetchScalarGridSpec(num_scalar_pr...]
  transfers between devices with their start and end apart: 31 -> 31, of which waited for: 13 -> 10; matrix products, arithmetic and copies ran while one was open for 6% -> 6% of each run, Pallas kernels for 37% -> 46%
where the time goes in v3:
time: 777 us; the launch traced here: 775 us
  Pallas kernels  410 us (53%)
  waiting for transfers between devices  241 us (31%)
  starting transfers between devices  62.1 us (8%)
  local copies, waits for them, and re-layouts  46.2 us (6%)
  other arithmetic  14.4 us (2%)
    ppermute x29, waiting for transfers between devices, hop(): lax.ppermute(p, both, [(a * ndp + i, b * ndp + (i ^ off)) for a, b in rou...  241 us
    pallas_call x11, Pallas kernels, grad1(): pl.pallas_call(kern, grid_spec=pltpu.PrefetchScalarGridSpec(num_scalar_pr...  154 us
    pallas_call x14, Pallas kernels, grad2(): pl.pallas_call(kern, grid_spec=pltpu.PrefetchScalarGridSpec(num_scalar_pr...  114 us
    pallas_call x4, Pallas kernels, layer(): pl.pallas_call(kern, grid_spec=pltpu.PrefetchScalarGridSpec(num_scalar_pr...  97.8 us
    ppermute x29, starting transfers between devices, hop(): lax.ppermute(p, both, [(a * ndp + i, b * ndp + (i ^ off)) for a, b in rou...  58.4 us
    pallas_call x5, Pallas kernels, reduce_into(): pl.pallas_call(kern, grid=(steps,), in_specs=in_specs, out_specs=pl.Block...  43.8 us
    dynamic_slice x21, local copies, waits for them, and re-layouts, rows_of(): lax.dynamic_slice(arr, (slot[i], k, 0, (d ^ off) * n1), (1, 1, arr.shape[...  26.2 us
  transfers between devices with their start and end apart: 31, of which 10 were waited for; matrix products, arithmetic and copies ran while one was open for 6% of the time, Pallas kernels for 46%

profile of v3, /device:TPU:5, one launch (start us, length us, event | category | flops | bytes accessed | tf_op | source)
XLA Modules:
  0.0 775.4 jit_solution(4068129596095545098)
XLA Ops:
  2.0 24.1 %shard_map.94 = (bf16[512,5120]{1,0:T(8,128)(2,1)}, bf16[512,1280]{1,0:T(8,128)(2,1)S(1)}) custom-call(s32[1]{0:T(128)} %bitcast.1.p, bf16[512,1280]{1,0:T(8,128)(2,1)S(1)} %bitcast.79, bf16[2,2,512,5120]{3,2,1,0:T(8,128)(2,1)} %bitcast.108, bf16[2,5120,1280]{2,1,0:T(8,128)(2,1)} %bitcast.160, bf16[2,1280,5120]{2,1,0:T(8,128)(2,1)} %bitcast.164), custom_call_target="tpu_custom_call" | custom-call | flops 13421772800 | bytes 26214400 | tf_op jit(solution)/shard_map/pallas_call | solution.py:54
  26.1 24.6 %shard_map.95 = (bf16[512,5120]{1,0:T(8,128)(2,1)}, bf16[512,1280]{1,0:T(8,128)(2,1)}) custom-call(s32[1]{0:T(128)} %bitcast.1.p, bf16[512,1280]{1,0:T(8,128)(2,1)S(1)} %get-tuple-element.25.g_ref.refs_3_.refs_2_, bf16[2,2,512,5120]{3,2,1,0:T(8,128)(2,1)} %bitcast.109, bf16[2,5120,1280]{2,1,0:T(8,128)(2,1)} %bitcast.161, bf16[2,1280,5120]{2,1,0:T(8,128)(2,1)} %bitcast.165), custom_call_target="tpu_custom_call" | custom-call | flops 13421772800 | bytes 26214400 | tf_op jit(solution)/shard_map/pallas_call | solution.py:54
  50.7 2.4 collective-permute-start
  53.2 4.2 shard_map.120
  57.4 2.4 collective-permute-start.21
  59.8 3.5 shard_map.119
  63.3 2.2 collective-permute-start.19
  65.6 4.2 shard_map.121
  69.7 2.4 collective-permute-start.23
  73.5 4.7 shard_map.108
  78.2 2.3 collective-permute-start.10
  80.6 6.4 shard_map.107
  87.0 35.2 %collective-permute-done.19 = bf16[256,1280]{1,0:T(8,128)(2,1)} collective-permute-done((bf16[256,1280]{1,0:T(8,128)(2,1)}, bf16[256,1280]{1,0:T(8,128)(2,1)}, u32[]{:S(2)}, u32[]{:S(2)}) %collective-permute-start.19) | collective-permute-done | bytes 655392 | tf_op jit(solution)/shard_map/ppermute | solution.py:181
  122.2 3.6 collective-permute-start.9
  127.3 8.3 %shard_map.117 = bf16[1280,1280]{1,0:T(8,128)(2,1)} custom-call(s32[2]{0:T(128)S(1)} %pad_add_fusion.6.refs_0_, bf16[2,2,512,5120]{3,2,1,0:T(8,128)(2,1)} %bitcast.113, bf16[512,1280]{1,0:T(8,128)(2,1)S(1)} %bitcast.83, f32[2,5120,1280]{2,1,0:T(8,128)} %bitcast.138), custom_call_target="tpu_custom_call" | custom-call | flops 1677721600 | bytes 9830400 | tf_op jit(solution)/shard_map/pallas_call | solution.py:91
  135.6 1.9 collective-permute-start.17
  137.5 8.4 %shard_map.112 = bf16[1280,1280]{1,0:T(8,128)(2,1)} custom-call(s32[2]{0:T(128)S(1)} %pad_add_fusion.6.refs_0_, bf16[2,2,512,5120]{3,2,1,0:T(8,128)(2,1)} %bitcast.114, bf16[512,1280]{1,0:T(8,128)(2,1)S(1)} %get-tuple-element.25.g_ref.refs_3_.refs_2_, f32[2,5120,1280]{2,1,0:T(8,128)} %bitcast.139), custom_call_target="tpu_custom_call" | custom-call | flops 1677721600 | bytes 9830400 | tf_op jit(solution)/shard_map/pallas_call | solution.py:91
  145.9 4.4 collective-permute-done.23
  150.3 3.6 collective-permute-start.13
  154.0 5.6 shard_map.123
  161.3 17.1 %collective-permute-done.10 = bf16[320,2048]{1,0:T(8,128)(2,1)} collective-permute-done((bf16[320,2048]{1,0:T(8,128)(2,1)}, bf16[320,2048]{1,0:T(8,128)(2,1)}, u32[]{:S(2)}, u32[]{:S(2)}) %collective-permute-start.10) | collective-permute-done | bytes 1310752 | tf_op jit(solution)/shard_map/ppermute | solution.py:181
  181.4 9.5 %shard_map.104 = bf16[320,5120]{1,0:T(8,128)(2,1)} custom-call(s32[1]{0:T(128)} %bitcast.22.refs_0_, bf16[320,512]{1,0:T(8,128)(2,1)S(1)} %bitcast.107, bf16[512,5120]{1,0:T(8,128)(2,1)} %get-tuple-element.38.refs_3_.refs_2_, f32[2,1280,5120]{2,1,0:T(8,128)} %bitcast.151), custom_call_target="tpu_custom_call" | custom-call | flops 1677721600 | bytes 9830400 | tf_op jit(solution)/shard_map/pallas_call | solution.py:126
  190.9 10.9 %shard_map.118 = bf16[1280,1280]{1,0:T(8,128)(2,1)} custom-call(s32[3]{0:T(128)S(1)} %pad_add_fusion.3.refs_0_, bf16[2,2,512,5120]{3,2,1,0:T(8,128)(2,1)} %bitcast.117, bf16[2,2,512,5120]{3,2,1,0:T(8,128)(2,1)} %bitcast.118, bf16[512,1280]{1,0:T(8,128)(2,1)S(1)} %bitcast.85, bf16[512,1280]{1,0:T(8,128)(2,1)} %collective-permute-done.g_ref.refs_4_, ...), custom_call_target="tpu_custom_call" | custom-call | flops 3355443200 | bytes 9830400 | tf_op jit(solution)/shard_map/pallas_call | solution.py:91
  204.4 10.8 %shard_map.116 = bf16[1280,1280]{1,0:T(8,128)(2,1)} custom-call(s32[3]{0:T(128)S(1)} %pad_add_fusion.4.refs_0_, bf16[2,2,512,5120]{3,2,1,0:T(8,128)(2,1)} %bitcast.119, bf16[2,2,512,5120]{3,2,1,0:T(8,128)(2,1)} %bitcast.120, bf16[512,1280]{1,0:T(8,128)(2,1)S(1)} %bitcast.86, bf16[512,1280]{1,0:T(8,128)(2,1)} %collective-permute-done.g_ref.refs_4_, ...), custom_call_target="tpu_custom_call" | custom-call | flops 3355443200 | bytes 9830400 | tf_op jit(solution)/shard_map/pallas_call | solution.py:91
  215.2 2.2 collective-permute-done.22
  217.4 3.6 collective-permute-start.5
  221.0 24.9 %shard_map.96 = (bf16[512,5120]{1,0:T(8,128)(2,1)}, bf16[512,1280]{1,0:T(8,128)(2,1)S(1)}) custom-call(s32[1]{0:T(128)} %constant.90.clone.1.p, bf16[512,1280]{1,0:T(8,128)(2,1)} %collective-permute-done.g_ref.refs_4_, bf16[2,2,512,5120]{3,2,1,0:T(8,128)(2,1)} %bitcast.121, bf16[2,5120,1280]{2,1,0:T(8,128)(2,1)} %bitcast.162, bf16[2,1280,5120]{2,1,0:T(8,128)(2,1)} %bitcast.166), custom_call_target="tpu_custom_call" | custom-call | flops 13421772800 | bytes 26214400 | tf_op jit(solution)/shard_map/pallas_call | solution.py:54
  246.0 2.5 collective-permute-start.18
  248.4 22.8 %collective-permute-done.11 = bf16[320,2048]{1,0:T(8,128)(2,1)S(1)} collective-permute-done((bf16[320,2048]{1,0:T(8,128)(2,1)}, bf16[320,2048]{1,0:T(8,128)(2,1)S(1)}, u32[]{:S(2)}, u32[]{:S(2)}) %collective-permute-start.11) | collective-permute-done | bytes 1310752 | tf_op jit(solution)/shard_map/ppermute | solution.py:181
  271.2 2.7 collective-permute-start.16
  273.9 10.3 %shard_map.114 = bf16[1280,1280]{1,0:T(8,128)(2,1)} custom-call(s32[3]{0:T(128)S(1)} %pad_add_fusion.2.refs_0_, bf16[2,2,512,5120]{3,2,1,0:T(8,128)(2,1)} %bitcast.122, bf16[2,2,512,5120]{3,2,1,0:T(8,128)(2,1)} %bitcast.123, bf16[512,1280]{1,0:T(8,128)(2,1)S(1)} %get-tuple-element.25.g_ref.refs_3_.refs_2_, ...), custom_call_target="tpu_custom_call" | custom-call | flops 3355443200 | bytes 9830400 | tf_op jit(solution)/shard_map/pallas_call | solution.py:91
  285.1 9.4 %shard_map.122 = bf16[896,1280]{1,0:T(8,128)(2,1)} custom-call(s32[3]{0:T(128)S(1)} %pad_add_fusion.1.refs_0_, bf16[2,2,512,5120]{3,2,1,0:T(8,128)(2,1)} %bitcast.124, bf16[2,2,512,5120]{3,2,1,0:T(8,128)(2,1)} %bitcast.125, bf16[512,1280]{1,0:T(8,128)(2,1)S(1)} %bitcast.87, bf16[512,1280]{1,0:T(8,128)(2,1)} %collective-permute-done.g_ref.refs_4_, ...), custom_call_target="tpu_custom_call" | custom-call | flops 2348810240 | bytes 6881280 | tf_op jit(solution)/shard_map/pallas_call | solution.py:91
  294.5 12.6 %collective-permute-done.13.refs_2_ = bf16[1280,1280]{1,0:T(8,128)(2,1)} collective-permute-done((bf16[1280,1280]{1,0:T(8,128)(2,1)}, bf16[1280,1280]{1,0:T(8,128)(2,1)}, u32[]{:S(2)}, u32[]{:S(2)}) %collective-permute-start.13) | collective-permute-done | bytes 3276832 | tf_op jit(solution)/shard_map/ppermute | solution.py:181
  309.7 10.2 %shard_map.113 = bf16[1280,1280]{1,0:T(8,128)(2,1)} custom-call(s32[3]{0:T(128)S(1)} %pad_add_fusion.3.refs_0_, bf16[2,2,512,5120]{3,2,1,0:T(8,128)(2,1)} %bitcast.126, bf16[2,2,512,5120]{3,2,1,0:T(8,128)(2,1)} %bitcast.127, bf16[512,1280]{1,0:T(8,128)(2,1)S(1)} %get-tuple-element.25.g_ref.refs_3_.refs_2_, bf16[512,1280]{1,0:T(8,128)(2,1)S(1)} %copy-done.3, ...), custom_call_target="tpu_custom_call" | custom-call | flops 3355443200 | bytes 9830400 | tf_op jit(solution)/shard_map/pallas_call | solution.py:91
  319.9 63.1 %collective-permute-done.5.refs_2_ = bf16[320,5120]{1,0:T(8,128)(2,1)} collective-permute-done((bf16[320,5120]{1,0:T(8,128)(2,1)}, bf16[320,5120]{1,0:T(8,128)(2,1)}, u32[]{:S(2)}, u32[]{:S(2)}) %collective-permute-start.5) | collective-permute-done | bytes 3276832 | tf_op jit(solution)/shard_map/ppermute | solution.py:181
  383.0 2.3 collective-permute-start.14
  385.3 10.2 %constant_dynamic-slice_fusion.1 = (bf16[1,1,512,320]{3,2,1,0:T(8,128)(2,1)}, bf16[1,1,512,320]{3,2,1,0:T(8,128)(2,1)S(1)}, bf16[1,1,512,320]{3,2,1,0:T(8,128)(2...) fusion(bf16[2,2,512,1280]{3,2,1,0:T(8,128)(2,1)} %bitcast.171, ...), kind=kLoop, calls=%fused_computation.5 | loop fusion | bytes 10485780 | tf_op jit(solution)/shard_map/dynamic_slice | solution.py:194
  396.8 17.1 %shard_map.106 = bf16[320,5120]{1,0:T(8,128)(2,1)} custom-call(s32[1]{0:T(128)} %bitcast.22.refs_0_, bf16[320,512]{1,0:T(8,128)(2,1)S(1)} %bitcast.105, bf16[320,512]{1,0:T(8,128)(2,1)S(1)} %bitcast.106, bf16[512,5120]{1,0:T(8,128)(2,1)} %get-tuple-element.38.refs_3_.refs_2_, bf16[512,5120]{1,0:T(8,128)(2,1)} %get-tuple-element.39.refs_4_, ...), custom_call_target="tpu_custom_call" | custom-call | flops 3355443200 | bytes 9830400 | tf_op jit(solution)/shard_map/pallas_call | solution.py:126
  416.4 1.9 copy.27
  420.7 10.2 %shard_map.111 = bf16[1280,1280]{1,0:T(8,128)(2,1)} custom-call(s32[3]{0:T(128)S(1)} %pad_add_fusion.4.refs_0_, bf16[2,2,512,5120]{3,2,1,0:T(8,128)(2,1)} %bitcast.128, bf16[2,2,512,5120]{3,2,1,0:T(8,128)(2,1)} %bitcast.129, bf16[512,1280]{1,0:T(8,128)(2,1)S(1)} %get-tuple-element.25.g_ref.refs_3_.refs_2_, bf16[512,1280]{1,0:T(8,128)(2,1)S(1)} %copy-done.4, ...), custom_call_target="tpu_custom_call" | custom-call | flops 3355443200 | bytes 9830400 | tf_op jit(solution)/shard_map/pallas_call | solution.py:91
  430.9 16.4 %shard_map.105 = bf16[320,5120]{1,0:T(8,128)(2,1)S(1)} custom-call(s32[1]{0:T(128)} %bitcast.17.refs_0_, bf16[320,512]{1,0:T(8,128)(2,1)S(1)} %bitcast.103, bf16[320,512]{1,0:T(8,128)(2,1)S(1)} %bitcast.104, bf16[512,5120]{1,0:T(8,128)(2,1)} %get-tuple-element.38.refs_3_.refs_2_, bf16[512,5120]{1,0:T(8,128)(2,1)} %get-tuple-element.39.refs_4_, ...), custom_call_target="tpu_custom_call" | custom-call | flops 3355443200 | bytes 9830400 | tf_op jit(solution)/shard_map/pallas_call | solution.py:126
  450.2 2.3 collective-permute-start.6
  452.5 17.1 %shard_map.103 = bf16[320,5120]{1,0:T(8,128)(2,1)} custom-call(s32[1]{0:T(128)} %bitcast.12.refs_0_, bf16[320,512]{1,0:T(8,128)(2,1)S(1)} %bitcast.93, bf16[320,512]{1,0:T(8,128)(2,1)S(1)} %bitcast.100, bf16[512,5120]{1,0:T(8,128)(2,1)} %get-tuple-element.38.refs_3_.refs_2_, bf16[512,5120]{1,0:T(8,128)(2,1)} %get-tuple-element.39.refs_4_, ...), custom_call_target="tpu_custom_call" | custom-call | flops 3355443200 | bytes 9830400 | tf_op jit(solution)/shard_map/pallas_call | solution.py:126
  473.8 24.1 %shard_map.97 = (bf16[512,5120]{1,0:T(8,128)(2,1)}, bf16[512,1280]{1,0:T(8,128)(2,1)S(1)}) custom-call(s32[1]{0:T(128)} %constant.90.clone.1.p, bf16[512,1280]{1,0:T(8,128)(2,1)S(1)} %copy-done.5, bf16[2,2,512,5120]{3,2,1,0:T(8,128)(2,1)} %bitcast.130, bf16[2,5120,1280]{2,1,0:T(8,128)(2,1)} %bitcast.163, bf16[2,1280,5120]{2,1,0:T(8,128)(2,1)} %bitcast.167), custom_call_target="tpu_custom_call" | custom-call | flops 13421772800 | bytes 26214400 | tf_op jit(solution)/shard_map/pallas_call | solution.py:54
  499.0 8.4 %collective-permute-start.26 = (bf16[896,1280]{1,0:T(8,128)(2,1)}, bf16[896,1280]{1,0:T(8,128)(2,1)}, u32[]{:S(2)}, u32[]{:S(2)}) collective-permute-start(bf16[896,1280]{1,0:T(8,128)(2,1)} %collective-permute-done.25), channel_id=1, source_target_pairs={{4,3},{5,2},{6,1},{7,0}} | collective-permute-start | bytes 6881288 | tf_op jit(solution)/shard_map/ppermute | solution.py:181
  507.4 16.4 %shard_map.101 = bf16[320,5120]{1,0:T(8,128)(2,1)S(1)} custom-call(s32[1]{0:T(128)} %bitcast.22.refs_0_, bf16[320,512]{1,0:T(8,128)(2,1)S(1)} %bitcast.96, bf16[320,512]{1,0:T(8,128)(2,1)S(1)} %bitcast.97, bf16[512,5120]{1,0:T(8,128)(2,1)} %get-tuple-element.30.refs_3_, bf16[512,5120]{1,0:T(8,128)(2,1)} %get-tuple-element.33.refs_4_, f32[2,1280,5120]{2,1,0:T(8,128)} %bitcast.155), custom_call_target="tpu_custom_call" | custom-call | flops 3355443200 | bytes 9830400 | tf_op jit(solution)/shard_map/pallas_call | solution.py:126
  527.8 3.0 collective-permute-start.8
  530.8 16.6 %shard_map.100 = bf16[320,5120]{1,0:T(8,128)(2,1)S(1)} custom-call(s32[1]{0:T(128)} %bitcast.17.refs_0_, bf16[320,512]{1,0:T(8,128)(2,1)S(1)} %bitcast.98, bf16[320,512]{1,0:T(8,128)(2,1)S(1)} %bitcast.99, bf16[512,5120]{1,0:T(8,128)(2,1)} %get-tuple-element.30.refs_3_, bf16[512,5120]{1,0:T(8,128)(2,1)} %get-tuple-element.33.refs_4_, f32[2,1280,5120]{2,1,0:T(8,128)} %bitcast.156), custom_call_target="tpu_custom_call" | custom-call | flops 3355443200 | bytes 9830400 | tf_op jit(solution)/shard_map/pallas_call | solution.py:126
  554.0 9.6 %shard_map.115.refs_0_ = bf16[1280,1280]{1,0:T(8,128)(2,1)S(1)} custom-call(s32[3]{0:T(128)S(1)} %pad_add_fusion.5.refs_0_, bf16[2,2,512,5120]{3,2,1,0:T(8,128)(2,1)} %bitcast.131, bf16[2,2,512,5120]{3,2,1,0:T(8,128)(2,1)} %bitcast.132, bf16[512,1280]{1,0:T(8,128)(2,1)S(1)} %bitcast.88, bf16[512,1280]{1,0:T(8,128)(2,1)} %collective-permute-done.g_ref.refs_4_, ...), custom_call_target="tpu_custom_call" | custom-call | flops 3355443200 | bytes 9830400 | tf_op jit(solution)/shard_map/pallas_call | solution.py:91
  567.4 17.2 %shard_map.99 = bf16[320,5120]{1,0:T(8,128)(2,1)} custom-call(s32[1]{0:T(128)} %bitcast.12.refs_0_, bf16[320,512]{1,0:T(8,128)(2,1)S(1)} %bitcast.94, bf16[320,512]{1,0:T(8,128)(2,1)S(1)} %bitcast.95, bf16[512,5120]{1,0:T(8,128)(2,1)} %get-tuple-element.30.refs_3_, bf16[512,5120]{1,0:T(8,128)(2,1)} %get-tuple-element.33.refs_4_, f32[2,1280,5120]{2,1,0:T(8,128)} %bitcast.157), custom_call_target="tpu_custom_call" | custom-call | flops 3355443200 | bytes 9830400 | tf_op jit(solution)/shard_map/pallas_call | solution.py:126
  585.0 9.0 %shard_map.110.refs_0_ = bf16[1280,1280]{1,0:T(8,128)(2,1)S(1)} custom-call(s32[3]{0:T(128)S(1)} %pad_add_fusion.5.refs_0_, bf16[2,2,512,5120]{3,2,1,0:T(8,128)(2,1)} %bitcast.133, bf16[2,2,512,5120]{3,2,1,0:T(8,128)(2,1)} %bitcast.134, bf16[512,1280]{1,0:T(8,128)(2,1)S(1)} %get-tuple-element.25.g_ref.refs_3_.refs_2_, bf16[512,1280]{1,0:T(8,128)(2,1)S(1)} %copy-done.6, ...), custom_call_target="tpu_custom_call" | custom-call | flops 3355443200 | bytes 9830400 | tf_op jit(solution)/shard_map/pallas_call | solution.py:91
  596.5 16.6 %shard_map.102.refs_0_ = bf16[320,5120]{1,0:T(8,128)(2,1)S(1)} custom-call(s32[1]{0:T(128)} %bitcast.refs_0_, bf16[320,512]{1,0:T(8,128)(2,1)S(1)} %bitcast.101, bf16[320,512]{1,0:T(8,128)(2,1)S(1)} %bitcast.102, bf16[512,5120]{1,0:T(8,128)(2,1)} %get-tuple-element.38.refs_3_.refs_2_, bf16[512,5120]{1,0:T(8,128)(2,1)} %get-tuple-element.39.refs_4_, ...), custom_call_target="tpu_custom_call" | custom-call | flops 3355443200 | bytes 9830400 | tf_op jit(solution)/shard_map/pallas_call | solution.py:126
  613.2 3.7 pad_maximum_fusion.1.refs_4_
  618.1 3.5 pad_maximum_fusion.refs_5_
  621.7 3.9 pad_maximum_fusion.2.refs_5_
  625.6 11.3 %shard_map.124.refs_5_ = f32[2,1280,1280]{2,1,0:T(8,128)} custom-call(bf16[1280,1280]{1,0:T(8,128)(2,1)} %copy-done.10, bf16[1280,1280]{1,0:T(8,128)(2,1)} %collective-permute-done.16.refs_1_, bf16[1280,1280]{1,0:T(8,128)(2,1)} %collective-permute-done.17.refs_2_, bf16[1280,1280]{1,0:T(8,128)(2,1)} %collective-permute-done.18.refs_3_, ...), custom_call_target="tpu_custom_call" | custom-call | flops 9830400 | bytes 26214400 | tf_op jit(solution)/shard_map/pallas_call | solution.py:165
  636.9 10.4 %shard_map.125 = f32[2,1280,1280]{2,1,0:T(8,128)} custom-call(bf16[1280,1280]{1,0:T(8,128)(2,1)} %copy-done.11, bf16[1280,1280]{1,0:T(8,128)(2,1)} %collective-permute-done.12.refs_1_, bf16[1280,1280]{1,0:T(8,128)(2,1)} %collective-permute-done.13.refs_2_, bf16[1280,1280]{1,0:T(8,128)(2,1)} %collective-permute-done.14.refs_3_, ...), custom_call_target="tpu_custom_call", output_to_operand_aliasing={{}: (5, {})} | custom-call | flops 8192000 | bytes 22937600 | tf_op jit(solution)/shard_map/pallas_call | solution.py:165
  647.3 11.1 %shard_map.109.refs_4_ = f32[2,320,5120]{2,1,0:T(8,128)} custom-call(bf16[320,5120]{1,0:T(8,128)(2,1)} %copy-done.12, bf16[320,5120]{1,0:T(8,128)(2,1)} %collective-permute-done.4.refs_1_, bf16[320,5120]{1,0:T(8,128)(2,1)} %collective-permute-done.5.refs_2_, bf16[320,5120]{1,0:T(8,128)(2,1)} %collective-permute-done.6.refs_3_, ...), custom_call_target="tpu_custom_call" | custom-call | flops 9830400 | bytes 26214400 | tf_op jit(solution)/shard_map/pallas_call | solution.py:165
  658.5 25.6 %collective-permute-done.2.refs_2_ = bf16[256,5120]{1,0:T(8,128)(2,1)} collective-permute-done((bf16[256,5120]{1,0:T(8,128)(2,1)}, bf16[256,5120]{1,0:T(8,128)(2,1)}, u32[]{:S(2)}, u32[]{:S(2)}) %collective-permute-start.2) | collective-permute-done | bytes 2621472 | tf_op jit(solution)/shard_map/ppermute | solution.py:181
  684.1 56.5 %collective-permute-done.3.refs_3_ = bf16[256,5120]{1,0:T(8,128)(2,1)} collective-permute-done((bf16[256,5120]{1,0:T(8,128)(2,1)}, bf16[256,5120]{1,0:T(8,128)(2,1)}, u32[]{:S(2)}, u32[]{:S(2)}) %collective-permute-start.3) | collective-permute-done | bytes 2621472 | tf_op jit(solution)/shard_map/ppermute | solution.py:181
  742.3 16.5 %shard_map.98.refs_0_ = bf16[320,5120]{1,0:T(8,128)(2,1)S(1)} custom-call(s32[1]{0:T(128)} %bitcast.refs_0_, bf16[320,512]{1,0:T(8,128)(2,1)S(1)} %bitcast.92, bf16[320,512]{1,0:T(8,128)(2,1)S(1)} %bitcast.91, bf16[512,5120]{1,0:T(8,128)(2,1)} %get-tuple-element.30.refs_3_, bf16[512,5120]{1,0:T(8,128)(2,1)} %get-tuple-element.33.refs_4_, ...), custom_call_target="tpu_custom_call" | custom-call | flops 3355443200 | bytes 9830400 | tf_op jit(solution)/shard_map/pallas_call | solution.py:126
  760.6 2.5 select_bitcast_fusion
  763.1 7.0 shard_map.126.refs_4_
  771.5 3.9 shard_map.127
  (129 shorter events, 52.7 us)
Async XLA Ops:
  0.6 1.3 copy-start
  26.1 27.1 %copy-start.1 = (bf16[1,512,1280]{2,1,0:T(8,128)(2,1)S(1)}, bf16[1,512,1280]{2,1,0:T(8,128)(2,1)}, u32[]{:S(2)}) copy-start(bf16[1,512,1280]{2,1,0:T(8,128)(2,1)} %param.7) | copy-start | bytes 3932164
  50.7 75.1 %collective-permute-start = (bf16[512,1280]{1,0:T(8,128)(2,1)}, bf16[512,1280]{1,0:T(8,128)(2,1)}, u32[]{:S(2)}, u32[]{:S(2)}) collective-permute-start(bf16[512,1280]{1,0:T(8,128)(2,1)} %get-tuple-element.27), channel_id=1, source_target_pairs={{4,0},{5,1},{6,2},{7,3}} | collective-permute-start | bytes 3932168 | tf_op jit(solution)/shard_map/ppermute | solution.py:233
  57.4 78.2 %collective-permute-start.21 = (bf16[512,1280]{1,0:T(8,128)(2,1)}, bf16[512,1280]{1,0:T(8,128)(2,1)}, u32[]{:S(2)}, u32[]{:S(2)}) collective-permute-start(bf16[512,1280]{1,0:T(8,128)(2,1)} %shard_map.120), channel_id=1, source_target_pairs={{4,0},{5,1},{6,2},{7,3}} | collective-permute-start | bytes 3932168 | tf_op jit(solution)/shard_map/ppermute | solution.py:181
  63.3 58.9 %collective-permute-start.19 = (bf16[256,1280]{1,0:T(8,128)(2,1)}, bf16[256,1280]{1,0:T(8,128)(2,1)}, u32[]{:S(2)}, u32[]{:S(2)}) collective-permute-start(bf16[256,1280]{1,0:T(8,128)(2,1)} %shard_map.119), channel_id=1, source_target_pairs={{4,0},{5,1},{6,2},{7,3}} | collective-permute-start | bytes 1966088 | tf_op jit(solution)/shard_map/ppermute | solution.py:181
  69.7 80.5 %collective-permute-start.23 = (bf16[512,1280]{1,0:T(8,128)(2,1)}, bf16[512,1280]{1,0:T(8,128)(2,1)}, u32[]{:S(2)}, u32[]{:S(2)}) collective-permute-start(bf16[512,1280]{1,0:T(8,128)(2,1)} %shard_map.121), channel_id=1, source_target_pairs={{4,0},{5,1},{6,2},{7,3}} | collective-permute-start | bytes 3932168 | tf_op jit(solution)/shard_map/ppermute | solution.py:181
  78.2 100.2 %collective-permute-start.10 = (bf16[320,2048]{1,0:T(8,128)(2,1)}, bf16[320,2048]{1,0:T(8,128)(2,1)}, u32[]{:S(2)}, u32[]{:S(2)}) collective-permute-start(bf16[320,2048]{1,0:T(8,128)(2,1)} %shard_map.108), channel_id=1, source_target_pairs={{4,0},{5,1},{6,2},{7,3}} | collective-permute-start | bytes 3932168 | tf_op jit(solution)/shard_map/ppermute | solution.py:181
  122.2 79.6 %collective-permute-start.9 = (bf16[320,3072]{1,0:T(8,128)(2,1)}, bf16[320,3072]{1,0:T(8,128)(2,1)}, u32[]{:S(2)}, u32[]{:S(2)}) collective-permute-start(bf16[320,3072]{1,0:T(8,128)(2,1)} %shard_map.107), channel_id=1, source_target_pairs={{4,6},{5,7},{6,4},{7,5}} | collective-permute-start | bytes 5898248 | tf_op jit(solution)/shard_map/ppermute | solution.py:181
  125.8 33.7 %collective-permute-start.20 = (bf16[256,1280]{1,0:T(8,128)(2,1)}, bf16[256,1280]{1,0:T(8,128)(2,1)S(1)}, u32[]{:S(2)}, u32[]{:S(2)}) collective-permute-start(bf16[256,1280]{1,0:T(8,128)(2,1)} %collective-permute-done.19), channel_id=1, source_target_pairs={{0,7},{1,6},{2,5},{3,4}} | collective-permute-start | bytes 1966088 | tf_op jit(solution)/shard_map/ppermute | solution.py:181
  135.6 148.6 %collective-permute-start.17 = (bf16[1280,1280]{1,0:T(8,128)(2,1)}, bf16[1280,1280]{1,0:T(8,128)(2,1)}, u32[]{:S(2)}, u32[]{:S(2)}) collective-permute-start(bf16[1280,1280]{1,0:T(8,128)(2,1)} %shard_map.117), channel_id=1, source_target_pairs={{4,6},{5,7},{6,4},{7,5}} | collective-permute-start | bytes 9830408 | tf_op jit(solution)/shard_map/ppermute | solution.py:181
  150.3 156.8 %collective-permute-start.13 = (bf16[1280,1280]{1,0:T(8,128)(2,1)}, bf16[1280,1280]{1,0:T(8,128)(2,1)}, u32[]{:S(2)}, u32[]{:S(2)}) collective-permute-start(bf16[1280,1280]{1,0:T(8,128)(2,1)} %shard_map.112), channel_id=1, source_target_pairs={{4,6},{5,7},{6,4},{7,5}} | collective-permute-start | bytes 9830408 | tf_op jit(solution)/shard_map/ppermute | solution.py:181
  159.6 18.8 %copy-start.26 = (bf16[256,1280]{1,0:T(8,128)(2,1)}, bf16[256,1280]{1,0:T(8,128)(2,1)S(1)}, u32[]{:S(2)}) copy-start(bf16[256,1280]{1,0:T(8,128)(2,1)S(1)} %collective-permute-done.20) | copy-start | bytes 1966084
  159.6 43.5 %collective-permute-start.27 = (bf16[384,1280]{1,0:T(8,128)(2,1)}, bf16[384,1280]{1,0:T(8,128)(2,1)}, u32[]{:S(2)}, u32[]{:S(2)}) collective-permute-start(bf16[384,1280]{1,0:T(8,128)(2,1)} %shard_map.123), channel_id=1, source_target_pairs={{0,3},{1,2},{2,1},{3,0}} | collective-permute-start | bytes 2949128 | tf_op jit(solution)/shard_map/ppermute | solution.py:181
  178.4 39.0 %collective-permute-start.22 = (bf16[512,1280]{1,0:T(8,128)(2,1)}, bf16[512,1280]{1,0:T(8,128)(2,1)}, u32[]{:S(2)}, u32[]{:S(2)}) collective-permute-start(bf16[512,1280]{1,0:T(8,128)(2,1)} %collective-permute-done.21), channel_id=1, source_target_pairs={{0,7},{1,6},{2,5},{3,4}} | collective-permute-start | bytes 3932168 | tf_op jit(solution)/shard_map/ppermute | solution.py:181
  201.8 44.2 %collective-permute-start.24 = (bf16[512,1280]{1,0:T(8,128)(2,1)}, bf16[512,1280]{1,0:T(8,128)(2,1)S(1)}, u32[]{:S(2)}, u32[]{:S(2)}) collective-permute-start(bf16[512,1280]{1,0:T(8,128)(2,1)} %collective-permute-done.23), channel_id=1, source_target_pairs={{0,7},{1,6},{2,5},{3,4}} | collective-permute-start | bytes 3932168 | tf_op jit(solution)/shard_map/ppermute | solution.py:181
  203.1 68.1 %collective-permute-start.11 = (bf16[320,2048]{1,0:T(8,128)(2,1)}, bf16[320,2048]{1,0:T(8,128)(2,1)S(1)}, u32[]{:S(2)}, u32[]{:S(2)}) collective-permute-start(bf16[320,2048]{1,0:T(8,128)(2,1)} %collective-permute-done.10), channel_id=1, source_target_pairs={{0,6},{1,7},{2,4},{3,5}} | collective-permute-start | bytes 3932168 | tf_op jit(solution)/shard_map/ppermute | solution.py:181
  217.4 165.7 %collective-permute-start.5 = (bf16[320,5120]{1,0:T(8,128)(2,1)}, bf16[320,5120]{1,0:T(8,128)(2,1)}, u32[]{:S(2)}, u32[]{:S(2)}) collective-permute-start(bf16[320,5120]{1,0:T(8,128)(2,1)} %shard_map.104), channel_id=1, source_target_pairs={{4,7},{5,6},{6,5},{7,4}} | collective-permute-start | bytes 9830408 | tf_op jit(solution)/shard_map/ppermute | solution.py:181
  245.9 38.3 %copy-start.2 = (bf16[512,1280]{1,0:T(8,128)(2,1)}, bf16[512,1280]{1,0:T(8,128)(2,1)S(1)}, u32[]{:S(2)}) copy-start(bf16[512,1280]{1,0:T(8,128)(2,1)S(1)} %get-tuple-element.32.g_ref.refs_4_) | copy-start | bytes 3932164
  245.9 38.3 %copy-start.24 = (bf16[512,1280]{1,0:T(8,128)(2,1)}, bf16[512,1280]{1,0:T(8,128)(2,1)S(1)}, u32[]{:S(2)}) copy-start(bf16[512,1280]{1,0:T(8,128)(2,1)S(1)} %collective-permute-done.24) | copy-start | bytes 3932164
  246.0 203.1 %collective-permute-start.18 = (bf16[1280,1280]{1,0:T(8,128)(2,1)}, bf16[1280,1280]{1,0:T(8,128)(2,1)}, u32[]{:S(2)}, u32[]{:S(2)}) collective-permute-start(bf16[1280,1280]{1,0:T(8,128)(2,1)} %shard_map.118), channel_id=1, source_target_pairs={{0,2},{1,3},{2,0},{3,1}} | collective-permute-start | bytes 9830408 | tf_op jit(solution)/shard_map/ppermute | solution.py:181
  271.2 13.0 %copy-start.22 = (bf16[320,2048]{1,0:T(8,128)(2,1)}, bf16[320,2048]{1,0:T(8,128)(2,1)S(1)}, u32[]{:S(2)}) copy-start(bf16[320,2048]{1,0:T(8,128)(2,1)S(1)} %collective-permute-done.11) | copy-start | bytes 3932164
  271.2 179.0 %collective-permute-start.16 = (bf16[1280,1280]{1,0:T(8,128)(2,1)}, bf16[1280,1280]{1,0:T(8,128)(2,1)}, u32[]{:S(2)}, u32[]{:S(2)}) collective-permute-start(bf16[1280,1280]{1,0:T(8,128)(2,1)} %shard_map.116), channel_id=1, source_target_pairs={{0,1},{1,0},{2,3},{3,2},{4,5},{5,4},{6,7},{7,6}} | collective-permute-start | bytes 9830408 | tf_op jit(solution)/shard_map/ppermute | solution.py:181
  284.2 185.4 %collective-permute-start.15 = (bf16[1280,1280]{1,0:T(8,128)(2,1)}, bf16[1280,1280]{1,0:T(8,128)(2,1)}, u32[]{:S(2)}, u32[]{:S(2)}) collective-permute-start(bf16[1280,1280]{1,0:T(8,128)(2,1)} %shard_map.114), channel_id=1, source_target_pairs={{0,3},{1,2},{2,1},{3,0},{4,7},{5,6},{6,5},{7,4}} | collective-permute-start | bytes 9830408 | tf_op jit(solution)/shard_map/ppermute | solution.py:181
  307.1 106.8 %collective-permute-start.25 = (bf16[896,1280]{1,0:T(8,128)(2,1)}, bf16[896,1280]{1,0:T(8,128)(2,1)}, u32[]{:S(2)}, u32[]{:S(2)}) collective-permute-start(bf16[896,1280]{1,0:T(8,128)(2,1)} %shard_map.122), channel_id=1, source_target_pairs={{0,4},{1,5},{2,6},{3,7}} | collective-permute-start | bytes 6881288 | tf_op jit(solution)/shard_map/ppermute | solution.py:181
  308.4 1.3 copy-start.3
  383.0 116.0 %collective-permute-start.14 = (bf16[1280,1280]{1,0:T(8,128)(2,1)}, bf16[1280,1280]{1,0:T(8,128)(2,1)}, u32[]{:S(2)}, u32[]{:S(2)}) collective-permute-start(bf16[1280,1280]{1,0:T(8,128)(2,1)} %shard_map.113), channel_id=1, source_target_pairs={{0,2},{1,3},{2,0},{3,1}} | collective-permute-start | bytes 9830408 | tf_op jit(solution)/shard_map/ppermute | solution.py:181
  413.9 113.9 %collective-permute-start.7 = (bf16[320,5120]{1,0:T(8,128)(2,1)}, bf16[320,5120]{1,0:T(8,128)(2,1)}, u32[]{:S(2)}, u32[]{:S(2)}) collective-permute-start(bf16[320,5120]{1,0:T(8,128)(2,1)} %shard_map.106), channel_id=1, source_target_pairs={{0,4},{1,5},{2,6},{3,7}} | collective-permute-start | bytes 9830408 | tf_op jit(solution)/shard_map/ppermute | solution.py:181
  419.4 1.3 copy-start.4
  420.7 10.2 %copy-start.14 = (bf16[1,1,512,320]{2,3,1,0:T(8,128)(2,1)S(1)}, bf16[1,1,512,320]{2,3,1,0:T(8,128)(2,1)}, u32[]{:S(2)}) copy-start(bf16[1,1,512,320]{2,3,1,0:T(8,128)(2,1)} %copy.27) | copy-start | bytes 983044
  447.3 1.7 copy-start.13
  449.0 116.3 %collective-permute-start.12 = (bf16[1280,1280]{1,0:T(8,128)(2,1)}, bf16[1280,1280]{1,0:T(8,128)(2,1)}, u32[]{:S(2)}, u32[]{:S(2)}) collective-permute-start(bf16[1280,1280]{1,0:T(8,128)(2,1)} %shard_map.111), channel_id=1, source_target_pairs={{0,1},{1,0},{2,3},{3,2},{4,5},{5,4},{6,7},{7,6}} | collective-permute-start | bytes 9830408 | tf_op jit(solution)/shard_map/ppermute | solution.py:181
  450.2 116.8 %collective-permute-start.6 = (bf16[320,5120]{1,0:T(8,128)(2,1)}, bf16[320,5120]{1,0:T(8,128)(2,1)}, u32[]{:S(2)}, u32[]{:S(2)}) collective-permute-start(bf16[320,5120]{1,0:T(8,128)(2,1)} %copy-done.13), channel_id=1, source_target_pairs={{0,2},{1,3},{2,0},{3,1}} | collective-permute-start | bytes 9830408 | tf_op jit(solution)/shard_map/ppermute | solution.py:181
  469.6 115.0 %collective-permute-start.4 = (bf16[320,5120]{1,0:T(8,128)(2,1)}, bf16[320,5120]{1,0:T(8,128)(2,1)}, u32[]{:S(2)}, u32[]{:S(2)}) collective-permute-start(bf16[320,5120]{1,0:T(8,128)(2,1)} %shard_map.103), channel_id=1, source_target_pairs={{0,1},{1,0},{2,3},{3,2},{4,5},{5,4},{6,7},{7,6}} | collective-permute-start | bytes 9830408 | tf_op jit(solution)/shard_map/ppermute | solution.py:181
  472.5 1.3 copy-start.5
  497.9 1.1 copy-start.15
  499.0 117.8 %collective-permute-start.26 = (bf16[896,1280]{1,0:T(8,128)(2,1)}, bf16[896,1280]{1,0:T(8,128)(2,1)}, u32[]{:S(2)}, u32[]{:S(2)}) collective-permute-start(bf16[896,1280]{1,0:T(8,128)(2,1)} %collective-permute-done.25), channel_id=1, source_target_pairs={{4,3},{5,2},{6,1},{7,0}} | collective-permute-start | bytes 6881288 | tf_op jit(solution)/shard_map/ppermute | solution.py:181
  523.8 1.7 copy-start.8
  527.8 119.5 %collective-permute-start.8 = (bf16[320,5120]{1,0:T(8,128)(2,1)}, bf16[320,5120]{1,0:T(8,128)(2,1)}, u32[]{:S(2)}, u32[]{:S(2)}) collective-permute-start(bf16[320,5120]{1,0:T(8,128)(2,1)} %collective-permute-done.7), channel_id=1, source_target_pairs={{4,3},{5,2},{6,1},{7,0}} | collective-permute-start | bytes 9830408 | tf_op jit(solution)/shard_map/ppermute | solution.py:181
  530.8 16.6 %copy-start.9 = (bf16[320,5120]{1,0:T(8,128)(2,1)S(1)}, bf16[320,5120]{1,0:T(8,128)(2,1)}, u32[]{:S(2)}) copy-start(bf16[320,5120]{1,0:T(8,128)(2,1)} %copy-done.8) | copy-start | bytes 9830404
  550.1 2.6 copy-start.21
  563.6 1.7 copy-start.10
  565.3 118.8 %collective-permute-start.2 = (bf16[256,5120]{1,0:T(8,128)(2,1)}, bf16[256,5120]{1,0:T(8,128)(2,1)}, u32[]{:S(2)}, u32[]{:S(2)}) collective-permute-start(bf16[256,5120]{1,0:T(8,128)(2,1)} %slice.16), channel_id=1, source_target_pairs={{0,2},{1,3},{2,0},{3,1},{4,6},{5,7},{6,4},{7,5}} | collective-permute-start | bytes 7864328 | tf_op jit(solution)/shard_map/ppermute | solution.py:181
  567.0 173.6 %collective-permute-start.3 = (bf16[256,5120]{1,0:T(8,128)(2,1)}, bf16[256,5120]{1,0:T(8,128)(2,1)}, u32[]{:S(2)}, u32[]{:S(2)}) collective-permute-start(bf16[256,5120]{1,0:T(8,128)(2,1)} %slice.18), channel_id=1, source_target_pairs={{0,3},{1,2},{2,1},{3,0},{4,7},{5,6},{6,5},{7,4}} | collective-permute-start | bytes 7864328 | tf_op jit(solution)/shard_map/ppermute | solution.py:181
  567.4 17.6 %copy-start.6 = (bf16[512,1280]{1,0:T(8,128)(2,1)S(1)}, bf16[512,1280]{1,0:T(8,128)(2,1)}, u32[]{:S(2)}) copy-start(bf16[512,1280]{1,0:T(8,128)(2,1)} %copy-done.2) | copy-start | bytes 3932164
  584.6 11.2 %copy-start.20 = (bf16[1,1,512,320]{3,2,1,0:T(8,128)(2,1)S(1)}, bf16[1,1,512,320]{3,2,1,0:T(8,128)(2,1)}, u32[]{:S(2)}) copy-start(bf16[1,1,512,320]{3,2,1,0:T(8,128)(2,1)} %get-tuple-element.54) | copy-start | bytes 983044
  584.6 11.4 %copy-start.19 = (bf16[1,1,512,320]{3,2,1,0:T(8,128)(2,1)S(1)}, bf16[1,1,512,320]{3,2,1,0:T(8,128)(2,1)}, u32[]{:S(2)}) copy-start(bf16[1,1,512,320]{3,2,1,0:T(8,128)(2,1)} %get-tuple-element.53) | copy-start | bytes 983044
  584.6 11.6 %copy-start.18 = (bf16[1,1,512,320]{3,2,1,0:T(8,128)(2,1)S(1)}, bf16[1,1,512,320]{3,2,1,0:T(8,128)(2,1)}, u32[]{:S(2)}) copy-start(bf16[1,1,512,320]{3,2,1,0:T(8,128)(2,1)} %get-tuple-element.61) | copy-start | bytes 983044
  584.6 11.7 %copy-start.17 = (bf16[1,1,512,320]{3,2,1,0:T(8,128)(2,1)S(1)}, bf16[1,1,512,320]{3,2,1,0:T(8,128)(2,1)}, u32[]{:S(2)}) copy-start(bf16[1,1,512,320]{3,2,1,0:T(8,128)(2,1)} %get-tuple-element.62) | copy-start | bytes 983044
  584.6 178.4 %collective-permute-start.1 = (bf16[320,5120]{1,0:T(8,128)(2,1)}, bf16[320,5120]{1,0:T(8,128)(2,1)}, u32[]{:S(2)}, u32[]{:S(2)}) collective-permute-start(bf16[320,5120]{1,0:T(8,128)(2,1)} %shard_map.99), channel_id=1, source_target_pairs={{0,1},{1,0},{2,3},{3,2},{4,5},{5,4},{6,7},{7,6}} | collective-permute-start | bytes 9830408 | tf_op jit(solution)/shard_map/ppermute | solution.py:181
  594.1 1.7 copy-start.11
  596.5 16.6 %copy-start.25 = (bf16[512,1280]{1,0:T(8,128)(2,1)S(1)}, bf16[512,1280]{1,0:T(8,128)(2,1)}, u32[]{:S(2)}) copy-start(bf16[512,1280]{1,0:T(8,128)(2,1)} %copy-done.24) | copy-start | bytes 3932164
  596.5 16.6 %copy-start.27 = (bf16[256,1280]{1,0:T(8,128)(2,1)S(1)}, bf16[256,1280]{1,0:T(8,128)(2,1)}, u32[]{:S(2)}) copy-start(bf16[256,1280]{1,0:T(8,128)(2,1)} %copy-done.26) | copy-start | bytes 1966084
  613.1 8.5 %copy-start.12 = (bf16[320,5120]{1,0:T(8,128)(2,1)}, bf16[320,5120]{1,0:T(8,128)(2,1)S(1)}, u32[]{:S(2)}) copy-start(bf16[320,5120]{1,0:T(8,128)(2,1)S(1)} %shard_map.102.refs_0_) | copy-start | bytes 9830404
  613.1 5.0 copy-start.23
  616.8 143.7 %collective-permute-start.30 = (bf16[512,1280]{1,0:T(8,128)(2,1)}, bf16[512,1280]{1,0:T(8,128)(2,1)}, u32[]{:S(2)}, u32[]{:S(2)}) collective-permute-start(bf16[512,1280]{1,0:T(8,128)(2,1)} %get-tuple-element.27), channel_id=1, source_target_pairs={{0,4},{1,5},{2,6},{3,7}} | collective-permute-start | bytes 3932168 | tf_op jit(solution)/shard_map/ppermute | solution.py:244
  647.3 93.3 %copy-start.28 = (bf16[64,5120]{1,0:T(8,128)(2,1)S(1)}, bf16[64,5120]{1,0:T(8,128)(2,1)}, u32[]{:S(2)}) copy-start(bf16[64,5120]{1,0:T(8,128)(2,1)} %slice.19) | copy-start | bytes 1966084
  740.7 29.4 %collective-permute-start.28 = (bf16[64,5120]{1,0:T(8,128)(2,1)}, bf16[64,5120]{1,0:T(8,128)(2,1)}, u32[]{:S(2)}, u32[]{:S(2)}) collective-permute-start(bf16[64,5120]{1,0:T(8,128)(2,1)} %slice.17), channel_id=1, source_target_pairs={{0,2},{1,3},{2,0},{3,1},{4,6},{5,7},{6,4},{7,5}} | collective-permute-start | bytes 1966088 | tf_op jit(solution)/shard_map/ppermute | solution.py:181
  740.7 30.8 %collective-permute-start.29 = (bf16[64,5120]{1,0:T(8,128)(2,1)S(1)}, bf16[64,5120]{1,0:T(8,128)(2,1)}, u32[]{:S(2)}, u32[]{:S(2)}) collective-permute-start(bf16[64,5120]{1,0:T(8,128)(2,1)S(1)} %copy-done.28), channel_id=1, source_target_pairs={{0,3},{1,2},{2,1},{3,0},{4,7},{5,6},{6,5},{7,4}} | collective-permute-start | bytes 1966088 | tf_op jit(solution)/shard_map/ppermute | solution.py:181
  742.3 18.2 %copy-start.16 = (bf16[512,1280]{1,0:T(8,128)(2,1)S(1)}, bf16[512,1280]{1,0:T(8,128)(2,1)}, u32[]{:S(2)}) copy-start(bf16[512,1280]{1,0:T(8,128)(2,1)} %copy-done.15) | copy-start | bytes 3932164
  758.9 1.7 copy-start.7
